TPU v7x, 256 devices: a whole 4x4x8 slice. The times are simulated.
256 devices in a mesh: lat: 64 (over x_lo, z, y), dp: 4 (over x_hi, core).
Axes of the slice: x: 4 (x_hi: 2, x_lo: 2; x = x_hi * 2 + x_lo), y: 4, z: 8, core: 2. Of those that a mesh axis runs over, the one named last changes fastest.
Arguments:
- state: float32 [4, 128, 256, 128], P('dp', 'lat'), may hold values from -6 to 6
- cotangent: float32 [4, 128, 256, 128], P('dp', 'lat'), may hold values from -0.18 to 0.18
- w_first: bfloat16 [128, 1024], replicated, may hold values from -0.5 to 0.5
- w_middle: bfloat16 [1024, 1024], replicated, may hold values from -0.1875 to 0.1875
- w_last: bfloat16 [1024, 128], replicated, may hold values from -0.1875 to 0.1875
Outputs:
- final_state: float32 [4, 128, 256, 128], P('dp', 'lat')
- grad_first: float32 [128, 1024], replicated
- grad_middle: float32 [1024, 1024], replicated
- grad_last: float32 [1024, 128], replicated
All inputs are finite; a program needn't handle non-finite values.
Results may differ from a plain program's by a relative error of at most 0.0048.
Values sent between devices are 32-bit elements; how exact they have to be, the bound alone decides.
No kernel may reach another device: no remote copies, remote signals or barrier semaphores. Data moves between devices by JAX's collectives and lax.ppermute only.
A program may use at most 64 MiB of HBM per device.

v0:
```python
import math

import jax
import jax.numpy as jnp
from jax import lax
from jax.sharding import PartitionSpec as P

MW = 64
STEPS = 2


highest = lax.Precision.HIGHEST
tend_weight = 0.5


def grid_tables(lon_count, wave_count):
    lon_index = jnp.arange(lon_count, dtype=jnp.int32)
    wave_index = jnp.arange(wave_count, dtype=jnp.int32)
    phase_angle = (lon_index[:, None] * wave_index[None, :] % lon_count).astype(jnp.float32) * (
        2.0 * math.pi / lon_count
    )
    cosine = jnp.cos(phase_angle)
    sine_part = jnp.sin(phase_angle)
    analysis = jnp.stack([cosine, -sine_part], axis=2) / lon_count
    factor = jnp.where(wave_index == 0, 1.0, 2.0).astype(jnp.float32)
    synthesis = jnp.stack([cosine, -sine_part], axis=2) * factor[None, :, None]
    return (analysis, synthesis)


def legendre(wave_ids, lat_count, wave_count):
    lat_index = jnp.arange(lat_count).astype(jnp.float32)
    latitude = (lat_index + 0.5) * (math.pi / lat_count) - 0.5 * math.pi
    sine_lat = jnp.sin(latitude)
    cosine_lat = jnp.cos(latitude)
    quad_weight = cosine_lat * (math.pi / lat_count)
    order_m = wave_ids.astype(jnp.float32)
    counter = jnp.arange(1, wave_count).astype(jnp.float32)
    increments = 0.5 * jnp.log((2.0 * counter + 1.0) / (2.0 * counter))
    summed = jnp.sum(
        jnp.where(counter[None, :] <= order_m[:, None], increments[None, :], 0.0), axis=1
    )
    diagonal = jnp.exp(
        0.5 * math.log(0.5) + summed[:, None] + order_m[:, None] * jnp.log(cosine_lat)[None, :]
    )

    def advance(carry, offset):
        previous, current, ratio_prev = carry
        degree = order_m + offset
        ratio_new = jnp.sqrt((4.0 * degree * degree - 1.0) / (degree * degree - order_m * order_m))
        following = ratio_new[:, None] * (
            sine_lat[None, :] * current - previous / ratio_prev[:, None]
        )
        return ((current, following, ratio_new), following)

    initial = (jnp.zeros_like(diagonal), diagonal, jnp.ones_like(order_m))
    _, remaining = lax.scan(advance, initial, jnp.arange(1, wave_count).astype(jnp.float32))
    poly_table = jnp.concatenate([diagonal[None], remaining], axis=0).transpose(1, 0, 2)
    degree = order_m[:, None] + jnp.arange(wave_count).astype(jnp.float32)[None, :]
    kept_mask = degree <= wave_count - 1
    poly_table = jnp.where(kept_mask[:, :, None], poly_table, 0.0)
    damping = jnp.where(
        kept_mask, 1.0 / (1.0 + degree * (degree + 1.0) / (wave_count * (wave_count - 1.0))), 0.0
    )
    return (poly_table, quad_weight, damping)


def silu_slope(value):
    gate_sig = jax.nn.sigmoid(value)
    return gate_sig * (1.0 + value * (1.0 - gate_sig))


def hidden_rows(rows, w_first, w_middle):
    pre_first = jnp.dot(rows, w_first, preferred_element_type=jnp.float32)
    hidden_first = jax.nn.silu(pre_first).astype(jnp.bfloat16)
    pre_middle = jnp.dot(hidden_first, w_middle, preferred_element_type=jnp.float32)
    hidden_middle = jax.nn.silu(pre_middle).astype(jnp.bfloat16)
    return (pre_first, hidden_first, pre_middle, hidden_middle)


def body(state, cotangent, w_first, w_middle, w_last):
    sample, lat_rows, lon_count, features = state.shape
    hidden_count = w_first.shape[1]
    band_count = lax.axis_size("lat")
    lat_count = lat_rows * band_count
    local_waves = MW // band_count
    wave_ids = lax.axis_index("lat") * local_waves + jnp.arange(local_waves, dtype=jnp.int32)
    analysis, synthesis = grid_tables(lon_count, MW)
    poly_table, quad_weight, damping = legendre(wave_ids, lat_count, MW)
    weighted = poly_table * quad_weight[None, None, :]
    row_count = sample * lat_rows * lon_count

    def spectral(field, first, last, in_table, out_table):
        wave_grid = jnp.einsum("bjxf,xmp->bjmpf", field, first, precision=highest)
        coeffs = (
            jnp.einsum(
                "mkj,bjmpf->bmkpf",
                in_table,
                lax.all_to_all(wave_grid, "lat", split_axis=2, concat_axis=1, tiled=True),
                precision=highest,
            )
            * damping[None, :, :, None, None]
        )
        back_grid = jnp.einsum("mkj,bmkpf->bjmpf", out_table, coeffs, precision=highest)
        back_bands = lax.all_to_all(back_grid, "lat", split_axis=1, concat_axis=2, tiled=True)
        return jnp.einsum("bjmpf,xmp->bjxf", back_bands, last, precision=highest)

    saved = []
    field = state
    for step_index in range(STEPS):
        rows = field.reshape(row_count, features).astype(jnp.bfloat16)
        pre_first, hidden_first, pre_middle, hidden_middle = hidden_rows(rows, w_first, w_middle)
        tendency = jnp.dot(hidden_middle, w_last, preferred_element_type=jnp.float32)
        saved.append((rows, pre_first, hidden_first, pre_middle, hidden_middle))
        moved = field + tend_weight * tendency.reshape(field.shape)
        field = spectral(moved, analysis, synthesis, weighted, poly_table)
    grad = cotangent
    total_first = jnp.zeros((features, hidden_count), jnp.float32)
    total_middle = jnp.zeros((hidden_count, hidden_count), jnp.float32)
    total_last = jnp.zeros((hidden_count, features), jnp.float32)
    for step_index in reversed(range(STEPS)):
        pulled = spectral(grad, synthesis, analysis, poly_table, weighted)
        scaled = (tend_weight * pulled).astype(jnp.bfloat16).reshape(row_count, features)
        rows, pre_first, hidden_first, pre_middle, hidden_middle = saved[step_index]
        total_last = total_last + jnp.dot(
            hidden_middle.T, scaled, preferred_element_type=jnp.float32
        )
        middle_back = jnp.dot(scaled, w_last.T, preferred_element_type=jnp.float32)
        middle_grad = (middle_back * silu_slope(pre_middle)).astype(jnp.bfloat16)
        total_middle = total_middle + jnp.dot(
            hidden_first.T, middle_grad, preferred_element_type=jnp.float32
        )
        first_back = jnp.dot(middle_grad, w_middle.T, preferred_element_type=jnp.float32)
        first_grad = (first_back * silu_slope(pre_first)).astype(jnp.bfloat16)
        total_first = total_first + jnp.dot(rows.T, first_grad, preferred_element_type=jnp.float32)
        if step_index > 0:
            back_rows = jnp.dot(first_grad, w_first.T, preferred_element_type=jnp.float32)
            grad = pulled + back_rows.reshape(field.shape)
    total_first, total_middle, total_last = lax.psum(
        (total_first, total_middle, total_last), ("lat", "dp")
    )
    return (field, total_first, total_middle, total_last)


def solution(mesh):
    in_specs = (P("dp", "lat", None, None), P("dp", "lat", None, None), P(), P(), P())
    out_specs = (P("dp", "lat", None, None), P(), P(), P())
    return jax.shard_map(body, mesh=mesh, in_specs=in_specs, out_specs=out_specs, check_vma=False)
```

profile of v0, /device:TPU:1, one launch (start us, length us, event | category | flops | bytes accessed | tf_op | source)
XLA Modules:
  0.0 566.1 jit_solution(16079854312345815015)
XLA Ops:
  7.5 1.3 convolution_bitcast_fusion.5
  8.8 0.8 copy.40
  9.5 13.8 %all-to-all-start.4 = ((f32[1,2,64,2,128]{4,1,3,0,2:T(2,128)}), f32[1,2,64,2,128]{4,1,3,0,2:T(2,128)}, u32[]{:S(2)}, u32[]{:S(2)}) async-start(f32[1,2,64,2,128]{4,1,3,0,2:T(2,128)} %copy.40), calls=%async_computation.4 | async-start | bytes 262144 | tf_op jit(solution)/shard_map/all_to_all | solution.py:98
  24.9 125.0 %while.19 = (s32[]{:T(128)}, f32[1,128]{1,0:T(1,128)S(1)}, f32[1,128]{1,0:T(1,128)S(1)}, f32[1]{0:T(128)}, f32[63,1,128]{2,1,0:T(1,128)}, /*index=5*/f32[63]{0:T...) while((s32[]{:T(128)}, f32[1,128]{1,0:T(1,128)S(1)}, ...), condition=%wide.region_2.3_spmd.clone, body=%wide.region_1.2_spmd.clone.sunk | while | flops 1033 | bytes 5353 | solution.py:56
  24.9 0.6 dynamic_slice.9
  54.6 0.6 dynamic_slice.9
  58.6 0.6 dynamic_slice.9
  62.6 0.6 dynamic_slice.9
  92.3 0.6 dynamic_slice.9
  96.3 0.6 dynamic_slice.9
  100.3 0.6 dynamic_slice.9
  130.0 0.6 dynamic_slice.9
  134.0 0.6 dynamic_slice.9
  149.9 1.0 convert_element_type.123
  152.0 2.8 multiply_convert_fusion.6
  156.3 0.8 copy.29
  157.0 0.7 fusion.56
  157.8 10.9 %all-to-all-start = ((f32[1,2,64,2,128]{4,1,3,0,2:T(2,128)}), f32[1,2,64,2,128]{4,1,3,0,2:T(2,128)}, u32[]{:S(2)}, u32[]{:S(2)}) async-start(f32[1,2,64,2,128]{4,1,3,0,2:T(2,128)} %copy.29), calls=%async_computation | async-start | bytes 262144 | tf_op jit(solution)/shard_map/all_to_all | solution.py:98
  168.7 1.0 copy.41
  169.7 1.0 fusion.12
  170.7 1.8 convolution_bitcast_fusion.9
  172.5 1.7 copy.42
  174.1 4.3 all-to-all-done
  178.5 6.6 %all-to-all-start.5 = ((f32[1,128,1,2,128]{4,3,0,2,1:T(2,128)}), f32[1,128,1,2,128]{4,3,0,2,1:T(2,128)}, u32[]{:S(2)}, u32[]{:S(2)}) async-start(f32[1,128,1,2,128]{4,3,0,2,1:T(2,128)} %copy.42), calls=%async_computation.5 | async-start | bytes 262144 | tf_op jit(solution)/shard_map/all_to_all | solution.py:104
  185.1 1.0 copy.30
  186.0 1.0 fusion.8
  187.0 1.8 convolution_bitcast_fusion.11
  188.8 1.7 copy.32
  190.5 4.4 all-to-all-done.5
  194.9 6.7 %all-to-all-start.1 = ((f32[1,128,1,2,128]{4,3,0,2,1:T(2,128)}), f32[1,128,1,2,128]{4,3,0,2,1:T(2,128)}, u32[]{:S(2)}, u32[]{:S(2)}) async-start(f32[1,128,1,2,128]{4,3,0,2,1:T(2,128)} %copy.32), calls=%async_computation.1 | async-start | bytes 262144 | tf_op jit(solution)/shard_map/all_to_all | solution.py:104
  201.6 2.1 multiply_convert_fusion.8
  203.7 7.7 %all-to-all-done.1 = f32[1,128,1,2,128]{4,3,0,2,1:T(2,128)} async-done(((f32[1,128,1,2,128]{4,3,0,2,1:T(2,128)}), f32[1,128,1,2,128]{4,3,0,2,1:T(2,128)}, u32[]{:S(2)}, u32[]{:S(2)}) %all-to-all-start.1) | async-done | bytes 131104 | tf_op jit(solution)/shard_map/all_to_all | solution.py:104
  211.3 2.1 fusion.96
  213.4 0.7 copy-done.9
  214.5 2.6 multiply_convert_fusion.4
  217.1 0.9 multiply_convert_fusion.3
  218.0 1.7 multiply_convert_fusion.2
  219.7 1.1 copy-done.2
  221.6 0.8 copy.45
  222.3 5.4 all-to-all-start.6
  227.7 5.2 fusion.93
  232.9 4.6 all-to-all-done.6
  237.6 0.9 copy.46
  238.5 1.0 fusion.14
  239.5 1.8 convolution_bitcast_fusion.8
  241.3 1.7 copy.47
  243.0 6.4 %all-to-all-start.7 = ((f32[1,128,1,2,128]{4,3,0,2,1:T(2,128)}), f32[1,128,1,2,128]{4,3,0,2,1:T(2,128)}, u32[]{:S(2)}, u32[]{:S(2)}) async-start(f32[1,128,1,2,128]{4,3,0,2,1:T(2,128)} %copy.47), calls=%async_computation.7 | async-start | bytes 262144 | tf_op jit(solution)/shard_map/all_to_all | solution.py:104
  249.6 2.5 fusion.100
  252.1 7.0 %all-to-all-done.7 = f32[1,128,1,2,128]{4,3,0,2,1:T(2,128)} async-done(((f32[1,128,1,2,128]{4,3,0,2,1:T(2,128)}), f32[1,128,1,2,128]{4,3,0,2,1:T(2,128)}, u32[]{:S(2)}, u32[]{:S(2)}) %all-to-all-start.7) | async-done | bytes 131104 | tf_op jit(solution)/shard_map/all_to_all | solution.py:104
  259.2 1.3 fusion.6
  260.5 3.5 multiply_convert_fusion.1
  264.0 1.3 convolution_add_fusion.1
  265.3 4.6 fusion.4
  269.9 2.3 convolution_add_fusion.2
  272.2 5.9 %convolution_add_fusion = f32[1024,1024]{1,0:T(8,128)} fusion(f32[1024,1024]{1,0:T(8,128)} %fusion.93, bf16[512,1024]{1,0:T(8,128)(2,1)} %multiply_convert_fusion.1, f32[512,1024]{1,0:T(8,128)S(1)} %copy-done.7), kind=kOutput, calls=%fused_computation.5 | convolution fusion | flops 1077411840 | bytes 11534336 | tf_op jit(solution)/shard_map/dot_general | solution.py:129
  278.1 1.2 copy-done.1
  279.3 1.4 convolution_multiply_fusion
  281.1 13.8 %all_to_all.120 = f32[1,2,64,2,128]{4,1,3,0,2:T(2,128)S(1)} all-to-all(f32[1,2,64,2,128]{4,1,3,0,2:T(2,128)S(1)} %copy.35), channel_id=1, replica_groups=mesh['lat'=64,'dp'=4] {'lat'}, dimensions={2} | all-to-all | bytes 262144 | tf_op jit(solution)/shard_map/all_to_all | solution.py:98
  295.7 14.1 %all_to_all.121 = f32[1,128,1,2,128]{4,3,0,2,1:T(2,128)S(1)} all-to-all(f32[1,128,1,2,128]{4,3,0,2,1:T(2,128)S(1)} %copy.37), channel_id=1, replica_groups=mesh['lat'=64,'dp'=4] {'lat'}, dimensions={1} | all-to-all | bytes 262144 | tf_op jit(solution)/shard_map/all_to_all | solution.py:104
  309.8 1.2 convolution_bitcast_fusion.2
  311.0 240.6 %all-reduce.3.cloned.1.call-done = (f32[128,1024]{1,0:T(8,128)}, f32[1024,1024]{1,0:T(8,128)}, f32[1024,128]{1,0:T(8,128)}) async-done(((f32[128,1024]{1,0:T(8,128)}, f32[1024,1024]{1,0:T(8,128)}, f32[1024,128]{1,0:T(8,128)}), (f32[128,1024]{1,0:T(8,128)}, f32[1024,1024]{1,0:T(8,128)}, f32[1024,128]{1,0:T(8,128)})) %all-reduce.3.cloned.1.call-update) | async-done | bytes 5242896 | tf_op jit(solution)/shard_map/psum | solution.py:138
  551.7 1.9 copy.109
  553.6 4.8 copy.110
  558.4 0.8 copy.111
  (318 shorter events, 77.1 us)
Async XLA Ops:
  7.2 144.8 %copy-start = (bf16[1024,1024]{1,0:T(8,128)(2,1)S(1)}, bf16[1024,1024]{1,0:T(8,128)(2,1)}, u32[]{:S(2)}) copy-start(bf16[1024,1024]{1,0:T(8,128)(2,1)} %param.10) | copy-start | bytes 6291460
  7.2 144.3 %copy-start.4 = (bf16[128,1024]{1,0:T(8,128)(2,1)S(1)}, bf16[128,1024]{1,0:T(8,128)(2,1)}, u32[]{:S(2)}) copy-start(bf16[128,1024]{1,0:T(8,128)(2,1)} %param.9) | copy-start | bytes 786436
  9.5 148.3 %all-to-all-start.4 = ((f32[1,2,64,2,128]{4,1,3,0,2:T(2,128)}), f32[1,2,64,2,128]{4,1,3,0,2:T(2,128)}, u32[]{:S(2)}, u32[]{:S(2)}) async-start(f32[1,2,64,2,128]{4,1,3,0,2:T(2,128)} %copy.40), calls=%async_computation.4 | async-start | bytes 262144 | tf_op jit(solution)/shard_map/all_to_all | solution.py:98
  150.8 0.7 copy-start.19
  151.9 2.9 copy-start.6
  151.9 2.9 copy-start.14
  152.0 3.3 copy-start.11
  154.8 0.8 copy-start.23
  157.8 20.7 %all-to-all-start = ((f32[1,2,64,2,128]{4,1,3,0,2:T(2,128)}), f32[1,2,64,2,128]{4,1,3,0,2:T(2,128)}, u32[]{:S(2)}, u32[]{:S(2)}) async-start(f32[1,2,64,2,128]{4,1,3,0,2:T(2,128)} %copy.29), calls=%async_computation | async-start | bytes 262144 | tf_op jit(solution)/shard_map/all_to_all | solution.py:98
  178.5 16.4 %all-to-all-start.5 = ((f32[1,128,1,2,128]{4,3,0,2,1:T(2,128)}), f32[1,128,1,2,128]{4,3,0,2,1:T(2,128)}, u32[]{:S(2)}, u32[]{:S(2)}) async-start(f32[1,128,1,2,128]{4,3,0,2,1:T(2,128)} %copy.42), calls=%async_computation.5 | async-start | bytes 262144 | tf_op jit(solution)/shard_map/all_to_all | solution.py:104
  194.9 16.5 %all-to-all-start.1 = ((f32[1,128,1,2,128]{4,3,0,2,1:T(2,128)}), f32[1,128,1,2,128]{4,3,0,2,1:T(2,128)}, u32[]{:S(2)}, u32[]{:S(2)}) async-start(f32[1,128,1,2,128]{4,3,0,2,1:T(2,128)} %copy.32), calls=%async_computation.1 | async-start | bytes 262144 | tf_op jit(solution)/shard_map/all_to_all | solution.py:104
  213.4 0.7 copy-start.9
  214.5 3.5 copy-start.8
  214.5 2.6 copy-start.15
  214.5 2.6 copy-start.22
  218.0 1.7 copy-start.24
  218.0 3.2 copy-start.13
  219.7 1.1 copy-start.2
  222.3 15.2 %all-to-all-start.6 = ((f32[1,2,64,2,128]{4,1,3,0,2:T(2,128)}), f32[1,2,64,2,128]{4,1,3,0,2:T(2,128)}, u32[]{:S(2)}, u32[]{:S(2)}) async-start(f32[1,2,64,2,128]{4,1,3,0,2:T(2,128)} %copy.45), calls=%async_computation.6 | async-start | bytes 262144 | tf_op jit(solution)/shard_map/all_to_all | solution.py:98
  232.9 27.5 %copy-start.16 = (bf16[1024,128]{1,0:T(8,128)(2,1)S(1)}, bf16[1024,128]{1,0:T(8,128)(2,1)}, u32[]{:S(2)}) copy-start(bf16[1024,128]{1,0:T(8,128)(2,1)} %param.11) | copy-start | bytes 786436
  243.0 16.2 %all-to-all-start.7 = ((f32[1,128,1,2,128]{4,3,0,2,1:T(2,128)}), f32[1,128,1,2,128]{4,3,0,2,1:T(2,128)}, u32[]{:S(2)}, u32[]{:S(2)}) async-start(f32[1,128,1,2,128]{4,3,0,2,1:T(2,128)} %copy.47), calls=%async_computation.7 | async-start | bytes 262144 | tf_op jit(solution)/shard_map/all_to_all | solution.py:104
  249.4 302.3 %all-reduce.3.cloned.1.call-start = ((), (), s32[]{:S(2)}) async-start(), calls=%async_computation.8 | async-start | bytes 10485760 | tf_op jit(solution)/shard_map/psum | solution.py:138
  260.5 3.5 copy-start.5
  264.0 1.3 copy-start.20
  265.3 4.6 copy-start.3
  265.3 4.6 copy-start.10
  269.9 2.3 copy-start.7
  278.1 1.2 copy-start.1
  278.1 2.6 copy-start.12
  279.3 15.6 %copy-start.18 = (f32[64,1,1,1,128]{4,1,3,2,0:T(1,128)S(1)}, f32[64,1,1,1,128]{4,1,3,2,0:T(1,128)}, u32[]{:S(2)}) copy-start(f32[64,1,1,1,128]{4,1,3,2,0:T(1,128)} %fusion.56) | copy-start | bytes 98308
  279.3 15.9 %copy-start.17 = (f32[64,1,128]{2,1,0:T(1,128)S(1)}, f32[64,1,128]{2,1,0:T(1,128)}, u32[]{:S(2)}) copy-start(f32[64,1,128]{2,1,0:T(1,128)} %pad_maximum_fusion.1) | copy-start | bytes 98308
  553.6 4.8 copy-start.21
Sparse Core Ops, SparseCore 0:
  278.2 273.3 all-reduce.2
where the time goes:
time: 569 us; the launch traced here: 566 us
  waiting for transfers between devices  269 us (47%)
  local copies, waits for them, and re-layouts  62.4 us (11%)
  matrix products  54.2 us (10%)
  starting transfers between devices  50.1 us (9%)
  loops' own time  48.4 us (9%)
  other arithmetic  39.2 us (7%)
  blocking collectives  27.9 us (5%)
  between operations  15.1 us (3%)
    psum x1, waiting for transfers between devices, body(): lax.psum((total_first, total_middle, total_last), ('lat', 'dp'))  241 us
    another operation x1, loops' own time, legendre(): lax.scan(advance, initial, jnp.arange(1, wave_count).astype(jnp.float32))  48.4 us
    dynamic_slice x63, local copies, waits for them, and re-layouts, legendre(): lax.scan(advance, initial, jnp.arange(1, wave_count).astype(jnp.float32))  40.7 us
    dynamic_update_slice x63, other arithmetic, legendre(): lax.scan(advance, initial, jnp.arange(1, wave_count).astype(jnp.float32))  35.8 us
    all_to_all x3, starting transfers between devices, spectral(): lax.all_to_all(wave_grid, 'lat', split_axis=2, concat_axis=1, tiled=True)  30.2 us
    all_to_all x3, starting transfers between devices, spectral(): lax.all_to_all(back_grid, 'lat', split_axis=1, concat_axis=2, tiled=True)  19.7 us
    all_to_all x3, waiting for transfers between devices, spectral(): lax.all_to_all(back_grid, 'lat', split_axis=1, concat_axis=2, tiled=True)  19.1 us
    all_to_all x1, blocking collectives, spectral(): lax.all_to_all(back_grid, 'lat', split_axis=1, concat_axis=2, tiled=True)  14.1 us
  transfers between devices with their start and end apart: 7, of which 6 were waited for; matrix products, arithmetic and copies ran while one was open for 19% of the time, Pallas kernels for 0%

commit v1 on v0

v1 whole, which is shorter than its diff:
```python
import functools
import math

import jax
import jax.numpy as jnp
from jax import lax
from jax.experimental import pallas as pl
from jax.experimental.pallas import tpu as pltpu
from jax.sharding import Mesh, PartitionSpec as P

MW = 64
STEPS = 2
highest = lax.Precision.HIGHEST
tend_weight = 0.5

FINE = (("xl", 2), ("z", 8), ("y", 4), ("xh", 2), ("c", 2))
ALL = tuple(name for name, _ in FINE)
LAT = ("xl", "z", "y")
SWAP = [(0, 1), (1, 0)]


def device_id(x, y, z, core):
    return ((((x % 2) * 8 + z) * 4 + y) * 2 + x // 2) * 2 + core


def reduce_groups():
    wide, deep = [], []
    for y in range(4):
        for pair in range(4):
            wide.append([device_id(x, y, 2 * pair + q, 0) for x in range(4) for q in range(2)])
    for x in range(4):
        for pair in range(4):
            wide.append(
                [device_id(x, y, (2 * pair + 1 + q) % 8, 1) for y in range(4) for q in range(2)]
            )
    for x in range(4):
        for parity in range(2):
            deep.append(
                [device_id(x, y, 2 * pair + parity, 0) for y in range(4) for pair in range(4)]
            )
    for y in range(4):
        for parity in range(2):
            deep.append(
                [device_id(x, y, 2 * pair + parity, 1) for x in range(4) for pair in range(4)]
            )
    return wide, deep


WIDE, DEEP = reduce_groups()


def exchange(value, groups):
    return lax.all_to_all(value, ALL, 0, 0, axis_index_groups=groups, tiled=True)


def grid_tables(lon_count, wave_count):
    lon_index = jnp.arange(lon_count, dtype=jnp.int32)
    wave_index = jnp.arange(wave_count, dtype=jnp.int32)
    phase_angle = (wave_index[:, None] * lon_index[None, :] % lon_count).astype(jnp.float32) * (
        2.0 * math.pi / lon_count
    )
    both = jnp.stack([jnp.cos(phase_angle), -jnp.sin(phase_angle)], axis=0)
    factor = jnp.where(wave_index == 0, 1.0, 2.0).astype(jnp.float32)
    return both / lon_count, both * factor[None, :, None]


def legendre_kernel(lat_count, wave_count, order_ref, forward_ref, backward_ref, table):
    bands = lat_count // 2
    place = lax.broadcasted_iota(jnp.int32, (1, lat_count), 1)
    lat_index = jnp.where(place >= bands, 2 * (place - bands) + 1, 2 * place).astype(jnp.float32)
    latitude = (lat_index + 0.5) * (math.pi / lat_count) - 0.5 * math.pi
    sine_lat = jnp.sin(latitude)
    cosine_lat = jnp.cos(latitude)
    quad_weight = cosine_lat * (math.pi / lat_count)
    order_m = jnp.full((1, lat_count), order_ref[0], jnp.int32).astype(jnp.float32)
    counter = lax.broadcasted_iota(jnp.int32, (1, lat_count), 1).astype(jnp.float32) + 1.0
    increments = 0.5 * jnp.log((2.0 * counter + 1.0) / (2.0 * counter))
    summed = jnp.sum(jnp.where(counter <= order_m, increments, 0.0), axis=1, keepdims=True)
    current = jnp.exp(0.5 * math.log(0.5) + summed + order_m * jnp.log(cosine_lat))
    previous = jnp.zeros_like(current)
    ratio_prev = jnp.ones_like(current)
    table[0:1, :] = current
    for offset in range(1, wave_count):
        degree = order_m + float(offset)
        ratio = jnp.sqrt((4.0 * degree * degree - 1.0) / (degree * degree - order_m * order_m))
        following = ratio * (sine_lat * current - previous / ratio_prev)
        previous, current, ratio_prev = current, following, ratio
        table[offset : offset + 1, :] = current
    degree = (
        lax.broadcasted_iota(jnp.int32, (wave_count, lat_count), 0) + order_ref[0]
    ).astype(jnp.float32)
    kept = degree <= wave_count - 1
    poly = jnp.where(kept, table[...], 0.0)
    damping = jnp.where(
        kept, 1.0 / (1.0 + degree * (degree + 1.0) / (wave_count * (wave_count - 1.0))), 0.0
    )
    weighted = poly * quad_weight
    forward_ref[...] = jnp.dot(
        poly.T, damping * weighted, precision=highest, preferred_element_type=jnp.float32
    )
    backward_ref[...] = jnp.dot(
        weighted.T, damping * poly, precision=highest, preferred_element_type=jnp.float32
    )


def legendre(order, lat_count, wave_count):
    square = jax.ShapeDtypeStruct((lat_count, lat_count), jnp.float32)
    return pl.pallas_call(
        functools.partial(legendre_kernel, lat_count, wave_count),
        out_shape=(square, square),
        in_specs=[pl.BlockSpec(memory_space=pltpu.SMEM)],
        out_specs=(pl.BlockSpec(memory_space=pltpu.VMEM),) * 2,
        scratch_shapes=[pltpu.VMEM((wave_count, lat_count), jnp.float32)],
        name="legendre",
    )(order)


def silu_slope(value):
    gate_sig = jax.nn.sigmoid(value)
    return gate_sig * (1.0 + value * (1.0 - gate_sig))


def hidden_rows(rows, w_first, w_middle):
    pre_first = jnp.dot(rows, w_first, preferred_element_type=jnp.float32)
    hidden_first = jax.nn.silu(pre_first).astype(jnp.bfloat16)
    pre_middle = jnp.dot(hidden_first, w_middle, preferred_element_type=jnp.float32)
    hidden_middle = jax.nn.silu(pre_middle).astype(jnp.bfloat16)
    return (pre_first, hidden_first, pre_middle, hidden_middle)


def sum_gradients(first, middle, last):
    hidden, features = last.shape
    core = lax.axis_index("c")
    half, part = hidden // 2, features // 2
    blocks = half // part
    packed = jnp.concatenate(
        [
            middle.reshape(2, half, hidden),
            first.reshape(2, part, hidden),
            last.reshape(2, blocks, part, features).transpose(0, 2, 1, 3).reshape(2, part, hidden),
        ],
        axis=1,
    )
    rows = packed.shape[1]
    keep = lax.dynamic_index_in_dim(packed, core, 0, keepdims=False)
    send = lax.dynamic_index_in_dim(packed, 1 - core, 0, keepdims=False)
    held = keep + lax.ppermute(send, "c", SWAP)
    wide, deep = len(WIDE[0]), len(DEEP[0])
    piece = rows // wide
    held = exchange(held.reshape(wide, piece, hidden), WIDE).sum(0)
    held = held.reshape(2, piece // 2, 8, hidden // 8).transpose(0, 2, 1, 3)
    held = exchange(held.reshape(deep, piece // 2, hidden // 8), DEEP).sum(0)
    held = exchange(jnp.broadcast_to(held[None], (deep,) + held.shape), DEEP)
    held = held.reshape(2, 8, piece // 2, hidden // 8).transpose(0, 2, 1, 3)
    held = held.reshape(piece, hidden)
    held = exchange(jnp.broadcast_to(held[None], (wide,) + held.shape), WIDE)
    held = held.reshape(rows, hidden)
    other = lax.ppermute(held, "c", SWAP)
    low = jnp.where(core == 0, held, other)
    high = jnp.where(core == 0, other, held)
    both = jnp.stack([low, high])
    middle = both[:, :half].reshape(hidden, hidden)
    first = both[:, half : half + part].reshape(features, hidden)
    last = both[:, half + part :].reshape(2, part, blocks, features)
    last = last.transpose(0, 2, 1, 3).reshape(hidden, features)
    return first, middle, last


def body(state, cotangent, w_first, w_middle, w_last):
    _, lat_rows, lon_count, features = state.shape
    hidden_count = w_first.shape[1]
    bands = lax.axis_size("xl") * lax.axis_size("z") * lax.axis_size("y")
    lat_count = lat_rows * bands
    row_count = lat_rows * lon_count
    analysis, synthesis = grid_tables(lon_count, MW)
    analysis = analysis.reshape(2 * MW, lon_count)
    synthesis = synthesis.reshape(2 * MW, lon_count)
    order = lax.axis_index(LAT).astype(jnp.int32).reshape(1)
    forward_op, backward_op = legendre(order, lat_count, MW)

    def to_waves(field, table):
        return jnp.einsum("qx,jxf->jqf", table, field, precision=highest)

    def to_grid(waves, table):
        return jnp.einsum("qx,jqf->jxf", table, waves, precision=highest)

    def spectral_pair(field, grad):
        waves = jnp.stack([to_waves(field, analysis), to_waves(grad, synthesis)])
        waves = waves.reshape(2, lat_rows, 2, MW, features).transpose(3, 0, 1, 2, 4)
        waves = waves.reshape(MW, 8, features)
        owned = lax.all_to_all(waves, LAT, 0, 0, tiled=True)
        owned = owned.reshape(bands, 2, lat_rows, 2, features).transpose(1, 2, 0, 3, 4)
        owned = owned.reshape(2, lat_count, 2 * features)
        back = jnp.stack(
            [
                jnp.dot(forward_op, owned[0], precision=highest),
                jnp.dot(backward_op, owned[1], precision=highest),
            ]
        )
        back = back.reshape(2, lat_rows, bands, 2, features).transpose(2, 0, 1, 3, 4)
        back = back.reshape(bands, 8, features)
        bands_back = lax.all_to_all(back, LAT, 0, 0, tiled=True)
        bands_back = bands_back.reshape(MW, 2, lat_rows, 2, features).transpose(1, 2, 3, 0, 4)
        bands_back = bands_back.reshape(2, lat_rows, 2 * MW, features)
        return to_grid(bands_back[0], synthesis), to_grid(bands_back[1], analysis)

    def advance(field):
        rows = field.reshape(row_count, features).astype(jnp.bfloat16)
        saved = hidden_rows(rows, w_first, w_middle)
        tendency = jnp.dot(saved[3], w_last, preferred_element_type=jnp.float32)
        return field + tend_weight * tendency.reshape(field.shape), (rows,) + saved

    def pull(pulled, saved, totals):
        scaled = (tend_weight * pulled).astype(jnp.bfloat16).reshape(row_count, features)
        rows, pre_first, hidden_first, pre_middle, hidden_middle = saved
        last = jnp.dot(hidden_middle.T, scaled, preferred_element_type=jnp.float32)
        middle_back = jnp.dot(scaled, w_last.T, preferred_element_type=jnp.float32)
        middle_grad = (middle_back * silu_slope(pre_middle)).astype(jnp.bfloat16)
        middle = jnp.dot(hidden_first.T, middle_grad, preferred_element_type=jnp.float32)
        first_back = jnp.dot(middle_grad, w_middle.T, preferred_element_type=jnp.float32)
        first_grad = (first_back * silu_slope(pre_first)).astype(jnp.bfloat16)
        first = jnp.dot(rows.T, first_grad, preferred_element_type=jnp.float32)
        found = (first, middle, last)
        if totals is not None:
            found = tuple(a + b for a, b in zip(totals, found))
        return first_grad, found

    moved, saved_0 = advance(state[0])
    field, pulled = spectral_pair(moved, cotangent[0])
    moved, saved_1 = advance(field)
    first_grad, totals = pull(pulled, saved_1, None)
    back_rows = jnp.dot(first_grad, w_first.T, preferred_element_type=jnp.float32)
    grad = pulled + back_rows.reshape(pulled.shape)
    final, pulled = spectral_pair(moved, grad)
    _, totals = pull(pulled, saved_0, totals)
    return (final[None],) + sum_gradients(*totals)


def solution(mesh):
    fine = Mesh(mesh.devices.reshape(tuple(size for _, size in FINE)), ALL)
    grid = P(("xh", "c"), LAT, None, None)
    return jax.shard_map(
        body,
        mesh=fine,
        in_specs=(grid, grid, P(), P(), P()),
        out_specs=(grid, P(), P(), P()),
        check_vma=False,
    )
```

time: 569 us -> 262 us (0.46)
  waiting for transfers between devices: 269 us -> 40.2 us
  blocking collectives: 27.9 us -> 82.9 us
  loops' own time: 48.4 us -> 0 us
  local copies, waits for them, and re-layouts: 62.4 us -> 26.7 us
  other arithmetic: 39.2 us -> 17.3 us
  between operations: 15.1 us -> 1.23 us
  starting transfers between devices: 50.1 us -> 37.7 us
    psum x1 -> x0, waiting for transfers between devices: 241 us -> none  [body(): lax.psum((total_first, total_middle, total_last), ('lat', 'dp'))]
    all_to_all x2 -> x4, blocking collectives: 27.9 us -> 82.9 us  [exchange(): lax.all_to_all(value, ALL, 0, 0, axis_index_groups=groups, tiled=True)]
    another operation x1 -> x0, loops' own time: 48.4 us -> none  [legendre(): lax.scan(advance, initial, jnp.arange(1, wave_count).astype(jnp.float32))]
    dynamic_slice x63 -> x0, local copies, waits for them, and re-layouts: 40.7 us -> none  [legendre(): lax.scan(advance, initial, jnp.arange(1, wave_count).astype(jnp.float32))]
    dynamic_update_slice x63 -> x0, other arithmetic: 35.8 us -> none  [legendre(): lax.scan(advance, initial, jnp.arange(1, wave_count).astype(jnp.float32))]
    all_to_all x6 -> x4, starting transfers between devices: 49.8 us -> 30.6 us  [the longest x2 18.7 us: spectral_pair(): owned = lax.all_to_all(waves, LAT, 0, 0, tiled=True)]
    ppermute x0 -> x2, waiting for transfers between devices: none -> 8.5 us  [the longest x1 4.88 us: sum_gradients(): held = keep + lax.ppermute(send, 'c', SWAP)]
    another operation x0 -> x6, other arithmetic: none -> 8.25 us  [the longest x3 6.62 us: sum_gradients(): both = jnp.stack([low, high])]
  transfers between devices with their start and end apart: 7 -> 6, of which waited for: 6 -> 6; matrix products, arithmetic and copies ran while one was open for 19% -> 4% of each run, Pallas kernels for 0% -> 0%
where the time goes in v1:
time: 262 us; the launch traced here: 261 us
  blocking collectives  82.9 us (32%)
  matrix products  53.6 us (20%)
  waiting for transfers between devices  40.2 us (15%)
  starting transfers between devices  37.7 us (14%)
  local copies, waits for them, and re-layouts  26.7 us (10%)
  other arithmetic  17.3 us (7%)
    all_to_all x4, blocking collectives, exchange(): lax.all_to_all(value, ALL, 0, 0, axis_index_groups=groups, tiled=True)  82.9 us
    all_to_all x2, starting transfers between devices, spectral_pair(): owned = lax.all_to_all(waves, LAT, 0, 0, tiled=True)  18.7 us
    all_to_all x2, waiting for transfers between devices, spectral_pair(): owned = lax.all_to_all(waves, LAT, 0, 0, tiled=True)  17.8 us
    all_to_all x2, waiting for transfers between devices, spectral_pair(): bands_back = lax.all_to_all(back, LAT, 0, 0, tiled=True)  13.9 us
    all_to_all x2, starting transfers between devices, spectral_pair(): bands_back = lax.all_to_all(back, LAT, 0, 0, tiled=True)  11.9 us
    dot_general x2, matrix products, pull(): jnp.dot(hidden_first.T, middle_grad, preferred_element_type=jnp.float32)  9.17 us
    another operation x3, other arithmetic, sum_gradients(): both = jnp.stack([low, high])  6.62 us
    dot_general x2, matrix products, pull(): first = jnp.dot(rows.T, first_grad, preferred_element_type=jnp.float32)  6.12 us
  transfers between devices with their start and end apart: 6, of which 6 were waited for; matrix products, arithmetic and copies ran while one was open for 4% of the time, Pallas kernels for 0%

profile of v1, /device:TPU:1, one launch (start us, length us, event | category | flops | bytes accessed | tf_op | source)
XLA Modules:
  0.0 260.9 jit_solution(14229574366031810230)
XLA Ops:
  0.9 1.1 convert_element_type.61
  2.8 1.3 fusion.6
  4.1 1.4 fusion.33
  5.5 2.8 %multiply_convert_fusion.6 = (bf16[512,1024]{1,0:T(8,128)(2,1)S(1)}, f32[512,1024]{1,0:T(8,128)}) fusion(bf16[1024,1024]{1,0:T(8,128)(2,1)S(1)} %copy-done, f32[512,1024]{1,0:T(8,128)S(1)} %fusion.33), kind=kOutput, calls=%fused_computation.17 | convolution fusion | flops 1078984704 | bytes 7340032 | tf_op jit(solution)/shard_map/dot_general | solution.py:126
  9.1 0.9 copy.59
  10.0 13.6 %all-to-all-start = ((f32[64,8,128]{2,1,0:T(8,128)}), f32[64,8,128]{2,1,0:T(8,128)S(1)}, u32[]{:S(2)}, u32[]{:S(2)}) async-start(f32[64,8,128]{2,1,0:T(8,128)} %bitcast.260), calls=%async_computation | async-start | bytes 524288 | tf_op jit(solution)/shard_map/all_to_all | solution.py:191
  23.6 1.3 legendre.1
  24.9 9.6 %all-to-all-done = f32[64,8,128]{2,1,0:T(8,128)S(1)} async-done(((f32[64,8,128]{2,1,0:T(8,128)}), f32[64,8,128]{2,1,0:T(8,128)S(1)}, u32[]{:S(2)}, u32[]{:S(2)}) %all-to-all-start) | async-done | bytes 262176 | tf_op jit(solution)/shard_map/all_to_all | solution.py:191
  35.4 1.0 copy.61
  37.1 1.0 copy.62
  38.1 1.1 convolution_bitcast_fusion.5
  39.2 1.1 convolution_bitcast_fusion.6
  41.3 6.9 %all-to-all-start.1 = ((f32[64,8,128]{2,1,0:T(8,128)}), f32[64,8,128]{2,1,0:T(8,128)}, u32[]{:S(2)}, u32[]{:S(2)}) async-start(f32[64,8,128]{2,1,0:T(8,128)} %copy.65), calls=%async_computation.1 | async-start | bytes 524288 | tf_op jit(solution)/shard_map/all_to_all | solution.py:202
  48.3 1.6 bitcast_multiply_fusion.1
  49.9 8.6 %all-to-all-done.1 = f32[64,8,128]{2,1,0:T(8,128)} async-done(((f32[64,8,128]{2,1,0:T(8,128)}), f32[64,8,128]{2,1,0:T(8,128)}, u32[]{:S(2)}, u32[]{:S(2)}) %all-to-all-start.1) | async-done | bytes 262176 | tf_op jit(solution)/shard_map/all_to_all | solution.py:202
  58.6 1.0 copy.66
  59.6 1.2 multiply_convert_fusion.8
  60.8 2.1 fusion.32
  62.8 1.7 copy.68
  64.5 1.3 fusion.34
  65.8 3.2 %multiply_convert_fusion.4 = (bf16[512,1024]{1,0:T(8,128)(2,1)}, f32[512,1024]{1,0:T(8,128)}) fusion(bf16[1024,1024]{1,0:T(8,128)(2,1)S(1)} %copy-done, f32[512,1024]{1,0:T(8,128)S(1)} %fusion.34), kind=kOutput, calls=%fused_computation.13 | convolution fusion | flops 1078984704 | bytes 7340032 | tf_op jit(solution)/shard_map/dot_general | solution.py:126
  69.0 1.7 copy.72
  70.7 2.7 %multiply_convert_fusion.3 = bf16[512,1024]{1,0:T(8,128)(2,1)S(1)} fusion(f32[512,1024]{1,0:T(8,128)} %get-tuple-element.48, bf16[512,128]{1,0:T(8,128)(2,1)} %bitcast.297, bf16[1024,128]{1,0:T(8,128)(2,1)} %param.9), kind=kOutput, calls=%fused_computation.12 | convolution fusion | flops 138936320 | bytes 3538944 | tf_op jit(solution)/shard_map/dot_general | solution.py:217
  73.5 1.7 multiply_convert_fusion.2
  75.1 1.0 copy-done.2
  76.1 1.2 fusion.35
  77.3 1.8 copy.73
  79.1 2.4 convolution_multiply_fusion.1
  81.5 1.8 copy.69
  83.3 1.5 fusion.10
  84.8 1.4 fusion.12
  86.2 0.9 copy.75
  87.1 5.1 %all-to-all-start.2 = ((f32[64,8,128]{2,1,0:T(8,128)}), f32[64,8,128]{2,1,0:T(8,128)S(1)}, u32[]{:S(2)}, u32[]{:S(2)}) async-start(f32[64,8,128]{2,1,0:T(8,128)} %bitcast.261), calls=%async_computation.2 | async-start | bytes 524288 | tf_op jit(solution)/shard_map/all_to_all | solution.py:191
  92.2 2.5 fusion.36
  94.7 8.2 %all-to-all-done.2 = f32[64,8,128]{2,1,0:T(8,128)S(1)} async-done(((f32[64,8,128]{2,1,0:T(8,128)}), f32[64,8,128]{2,1,0:T(8,128)S(1)}, u32[]{:S(2)}, u32[]{:S(2)}) %all-to-all-start.2) | async-done | bytes 262176 | tf_op jit(solution)/shard_map/all_to_all | solution.py:191
  103.9 1.8 convolution_bitcast_fusion.3
  105.6 1.0 copy.77
  106.8 1.1 convolution_bitcast_fusion.4
  107.9 0.9 pad_maximum_fusion.4
  109.7 5.0 %all-to-all-start.3 = ((f32[64,8,128]{2,1,0:T(8,128)}), f32[64,8,128]{2,1,0:T(8,128)S(1)}, u32[]{:S(2)}, u32[]{:S(2)}) async-start(f32[64,8,128]{2,1,0:T(8,128)} %copy.81), calls=%async_computation.3 | async-start | bytes 524288 | tf_op jit(solution)/shard_map/all_to_all | solution.py:202
  114.7 5.2 %fusion.26 = f32[1024,1024]{1,0:T(8,128)} fusion(bf16[512,1024]{1,0:T(8,128)(2,1)} %copy-done.22, f32[512,1024]{1,0:T(8,128)} %copy-done.8), kind=kOutput, calls=%fused_computation.83 | convolution fusion | flops 1076363264 | bytes 7340032 | tf_op jit(solution)/shard_map/dot_general | solution.py:219
  119.9 5.3 %all-to-all-done.3 = f32[64,8,128]{2,1,0:T(8,128)S(1)} async-done(((f32[64,8,128]{2,1,0:T(8,128)}), f32[64,8,128]{2,1,0:T(8,128)S(1)}, u32[]{:S(2)}, u32[]{:S(2)}) %all-to-all-start.3) | async-done | bytes 262176 | tf_op jit(solution)/shard_map/all_to_all | solution.py:202
  125.9 1.1 fusion.4
  127.0 1.0 copy.85
  128.0 1.7 convolution_add_fusion.1
  130.6 2.8 %multiply_convert_fusion.1 = bf16[512,1024]{1,0:T(8,128)(2,1)} fusion(f32[512,1024]{1,0:T(8,128)S(1)} %copy-done.21, bf16[512,128]{1,0:T(8,128)(2,1)} %bitcast.275, bf16[1024,128]{1,0:T(8,128)(2,1)S(1)} %copy-done.16), kind=kOutput, calls=%fused_computation.10 | convolution fusion | flops 138936320 | bytes 3538944 | tf_op jit(solution)/shard_map/dot_general | solution.py:217
  133.3 4.6 %fusion.2 = f32[128,1024]{1,0:T(8,128)} fusion(bf16[512,128]{1,0:T(8,128)(2,1)S(1)} %bitcast.273, f32[512,1024]{1,0:T(8,128)} %copy-done.6, bf16[512,1024]{1,0:T(8,128)(2,1)} %multiply_convert_fusion.1, bf16[1024,1024]{1,0:T(8,128)(2,1)S(1)} %copy-done), kind=kOutput, calls=%fused_computation.24 | convolution fusion | flops 1212678144 | bytes 5898240 | tf_op jit(solution)/shard_map/dot_general | solution.py:222
  138.0 1.5 convolution_add_fusion.2
  139.7 4.0 %convolution_add_fusion = f32[1024,1024]{1,0:T(8,128)S(1)} fusion(f32[1024,1024]{1,0:T(8,128)} %fusion.26, bf16[512,1024]{1,0:T(8,128)(2,1)} %multiply_convert_fusion.1, f32[512,1024]{1,0:T(8,128)S(1)} %copy-done.7), kind=kOutput, calls=%fused_computation.8 | convolution fusion | flops 1077411840 | bytes 11534336 | tf_op jit(solution)/shard_map/dot_general | solution.py:219
  144.6 1.8 dynamic-slice_bitcast_fusion
  146.4 1.3 copy-done.1
  147.6 5.3 %collective-permute-start = (f32[640,1024]{1,0:T(8,128)}, f32[640,1024]{1,0:T(8,128)}, u32[]{:S(2)}, u32[]{:S(2)}) collective-permute-start(f32[640,1024]{1,0:T(8,128)} %dynamic-slice_bitcast_fusion), channel_id=1, source_target_pairs={{0,1},{1,0},{2,3},{3,2},{4,5},{5,4},{6,7},{7,6},{8,9},{9,8},{10,11... | collective-permute-start | bytes 7864328 | tf_op jit(solution)/shard_map/ppermute | solution.py:147
  153.0 4.9 %collective-permute-done = f32[640,1024]{1,0:T(8,128)} collective-permute-done((f32[640,1024]{1,0:T(8,128)}, f32[640,1024]{1,0:T(8,128)}, u32[]{:S(2)}, u32[]{:S(2)}) %collective-permute-start) | collective-permute-done | bytes 2621472 | tf_op jit(solution)/shard_map/ppermute | solution.py:147
  157.9 3.1 %bitcast_add_fusion = f32[640,1024]{1,0:T(8,128)S(1)} fusion(f32[640,1024]{1,0:T(8,128)} %collective-permute-done, f32[2,640,1024]{2,1,0:T(8,128)} %copy-done.1, s32[]{:T(128)S(6)} %select_n.52), kind=kLoop, calls=%fused_computation.4 | loop fusion | flops 655360 | bytes 7864324 | tf_op jit(solution)/shard_map/add | solution.py:147
  161.0 23.4 %all_to_all.40 = f32[8,80,1024]{2,1,0:T(8,128)} all-to-all(f32[8,80,1024]{2,1,0:T(8,128)S(1)} %bitcast.238), channel_id=1, replica_groups={{0,16,128,144,2,18,130,146},{32,48,160,176,34,50,162,178},{64,80,192,20..., dimensions={0} | all-to-all | bytes 5242880 | tf_op jit(solution)/shard_map/all_to_all | solution.py:53
  184.4 2.0 reduce_sum.18
  186.6 19.5 %all_to_all.41 = f32[16,40,128]{2,1,0:T(8,128)S(1)} all-to-all(f32[16,40,128]{2,1,0:T(8,128)S(1)} %bitcast.254), channel_id=1, replica_groups={{0,32,64,96,4,36,68,100,8,40,72,104,12,44,76,108},{16,48,80,112,20,52,8..., dimensions={0} | all-to-all | bytes 655360 | tf_op jit(solution)/shard_map/all_to_all | solution.py:53
  206.1 18.0 %all_to_all.42 = f32[16,40,128]{2,1,0:T(8,128)S(1)} all-to-all(f32[16,40,128]{2,1,0:T(8,128)S(1)} %broadcast_in_dim.30), channel_id=1, replica_groups={{0,32,64,96,4,36,68,100,8,40,72,104,12,44,76,108},{16,48,80,112,20,52,8..., dimensions={0} | all-to-all | bytes 655360 | tf_op jit(solution)/shard_map/all_to_all | solution.py:53
  224.5 22.0 %all_to_all.43 = f32[8,80,1024]{2,1,0:T(8,128)} all-to-all(f32[8,80,1024]{2,1,0:T(8,128)S(1)} %broadcast_in_dim.32), channel_id=1, replica_groups={{0,16,128,144,2,18,130,146},{32,48,160,176,34,50,162,178},{64,80,192,20..., dimensions={0} | all-to-all | bytes 5242880 | tf_op jit(solution)/shard_map/all_to_all | solution.py:53
  246.5 1.8 collective-permute-start.1
  249.6 3.6 %collective-permute-done.1 = f32[640,1024]{1,0:T(8,128)} collective-permute-done((f32[640,1024]{1,0:T(8,128)}, f32[640,1024]{1,0:T(8,128)}, u32[]{:S(2)}, u32[]{:S(2)}) %collective-permute-start.1) | collective-permute-done | bytes 2621472 | tf_op jit(solution)/shard_map/ppermute | solution.py:158
  253.2 3.2 %select_bitcast_fusion.1 = (f32[1,640,1024]{2,1,0:T(8,128)S(1)}, f32[1,640,1024]{2,1,0:T(8,128)S(1)}) fusion(f32[640,1024]{1,0:T(8,128)} %collective-permute-done.1, pred[]{:T(512)S(6)} %eq.20, f32[8,80,1024]{2,1,0:T(8,128)} %all_to_all.43), kind=kLoop, calls=%fused_computation.6 | loop fusion | flops 1310720 | bytes 10485761 | tf_op jit(solution)/shard_map/stack | solution.py:161
  256.4 0.9 pad_maximum_fusion.1
  257.3 2.5 fusion
  (87 shorter events, 11.9 us)
Async XLA Ops:
  0.6 4.8 %copy-start = (bf16[1024,1024]{1,0:T(8,128)(2,1)S(1)}, bf16[1024,1024]{1,0:T(8,128)(2,1)}, u32[]{:S(2)}) copy-start(bf16[1024,1024]{1,0:T(8,128)(2,1)} %param.8) | copy-start | bytes 6291460
  2.1 2.0 copy-start.17
  2.8 1.3 copy-start.10
  5.4 2.9 %copy-start.6 = (f32[512,1024]{1,0:T(8,128)}, f32[512,1024]{1,0:T(8,128)S(1)}, u32[]{:S(2)}) copy-start(f32[512,1024]{1,0:T(8,128)S(1)} %fusion.33) | copy-start | bytes 6291460
  5.5 2.9 %copy-start.15 = (bf16[1024,128]{1,0:T(8,128)(2,1)S(1)}, bf16[1024,128]{1,0:T(8,128)(2,1)}, u32[]{:S(2)}) copy-start(bf16[1024,128]{1,0:T(8,128)(2,1)} %param.9) | copy-start | bytes 786436
  5.5 3.3 %copy-start.13 = (f32[1,2,256,128]{3,2,1,0:T(8,128)S(1)}, f32[1,2,256,128]{3,2,1,0:T(8,128)}, u32[]{:S(2)}) copy-start(f32[1,2,256,128]{3,2,1,0:T(8,128)} %param.5) | copy-start | bytes 786436
  10.0 24.5 %all-to-all-start = ((f32[64,8,128]{2,1,0:T(8,128)}), f32[64,8,128]{2,1,0:T(8,128)S(1)}, u32[]{:S(2)}, u32[]{:S(2)}) async-start(f32[64,8,128]{2,1,0:T(8,128)} %bitcast.260), calls=%async_computation | async-start | bytes 524288 | tf_op jit(solution)/shard_map/all_to_all | solution.py:191
  40.4 24.1 %copy-start.4 = (bf16[128,1024]{1,0:T(8,128)(2,1)S(1)}, bf16[128,1024]{1,0:T(8,128)(2,1)}, u32[]{:S(2)}) copy-start(bf16[128,1024]{1,0:T(8,128)(2,1)} %param.7) | copy-start | bytes 786436
  41.3 17.3 %all-to-all-start.1 = ((f32[64,8,128]{2,1,0:T(8,128)}), f32[64,8,128]{2,1,0:T(8,128)}, u32[]{:S(2)}, u32[]{:S(2)}) async-start(f32[64,8,128]{2,1,0:T(8,128)} %copy.65), calls=%async_computation.1 | async-start | bytes 524288 | tf_op jit(solution)/shard_map/all_to_all | solution.py:202
  65.8 3.2 %copy-start.8 = (f32[512,1024]{1,0:T(8,128)}, f32[512,1024]{1,0:T(8,128)S(1)}, u32[]{:S(2)}) copy-start(f32[512,1024]{1,0:T(8,128)S(1)} %fusion.34) | copy-start | bytes 6291460
  70.7 2.7 %copy-start.9 = (f32[512,1024]{1,0:T(8,128)S(1)}, f32[512,1024]{1,0:T(8,128)}, u32[]{:S(2)}) copy-start(f32[512,1024]{1,0:T(8,128)} %copy-done.8) | copy-start | bytes 6291460
  73.4 1.7 copy-start.22
  75.1 1.0 copy-start.2
  77.3 7.5 %copy-start.14 = (f32[2,256,128]{1,2,0:T(8,128)S(1)}, f32[2,256,128]{1,2,0:T(8,128)}, u32[]{:S(2)}) copy-start(f32[2,256,128]{1,2,0:T(8,128)} %get-tuple-element.44) | copy-start | bytes 786436
  87.1 15.8 %all-to-all-start.2 = ((f32[64,8,128]{2,1,0:T(8,128)}), f32[64,8,128]{2,1,0:T(8,128)S(1)}, u32[]{:S(2)}, u32[]{:S(2)}) async-start(f32[64,8,128]{2,1,0:T(8,128)} %bitcast.261), calls=%async_computation.2 | async-start | bytes 524288 | tf_op jit(solution)/shard_map/all_to_all | solution.py:191
  109.7 15.5 %all-to-all-start.3 = ((f32[64,8,128]{2,1,0:T(8,128)}), f32[64,8,128]{2,1,0:T(8,128)S(1)}, u32[]{:S(2)}, u32[]{:S(2)}) async-start(f32[64,8,128]{2,1,0:T(8,128)} %copy.81), calls=%async_computation.3 | async-start | bytes 524288 | tf_op jit(solution)/shard_map/all_to_all | solution.py:202
  125.9 4.6 %copy-start.16 = (bf16[1024,128]{1,0:T(8,128)(2,1)S(1)}, bf16[1024,128]{1,0:T(8,128)(2,1)}, u32[]{:S(2)}) copy-start(bf16[1024,128]{1,0:T(8,128)(2,1)} %param.9) | copy-start | bytes 786436
  128.0 2.5 copy-start.19
  128.0 2.5 copy-start.21
  130.5 2.8 %copy-start.18 = (bf16[1,2,256,128]{3,2,1,0:T(8,128)(2,1)S(1)}, bf16[1,2,256,128]{3,2,1,0:T(8,128)(2,1)}, u32[]{:S(2)}) copy-start(bf16[1,2,256,128]{3,2,1,0:T(8,128)(2,1)} %copy-done.17) | copy-start | bytes 393220
  133.3 4.6 %copy-start.3 = (bf16[512,1024]{1,0:T(8,128)(2,1)S(1)}, bf16[512,1024]{1,0:T(8,128)(2,1)}, u32[]{:S(2)}) copy-start(bf16[512,1024]{1,0:T(8,128)(2,1)} %copy-done.2) | copy-start | bytes 3145732
  133.3 4.6 %copy-start.12 = (bf16[2,256,128]{2,1,0:T(8,128)(2,1)S(1)}, bf16[2,256,128]{2,1,0:T(8,128)(2,1)}, u32[]{:S(2)}) copy-start(bf16[2,256,128]{2,1,0:T(8,128)(2,1)} %copy.68) | copy-start | bytes 393220
  137.9 1.7 copy-start.7
  139.7 4.0 %copy-start.5 = (f32[2,8,8,8,128]{4,3,1,2,0:T(8,128)S(1)}, f32[2,8,8,8,128]{4,3,1,2,0:T(8,128)}, u32[]{:S(2)}) copy-start(f32[2,8,8,8,128]{4,3,1,2,0:T(8,128)} %copy.113) | copy-start | bytes 1572868
  144.5 3.1 %copy-start.1 = (f32[2,640,1024]{2,1,0:T(8,128)}, f32[2,640,1024]{2,1,0:T(8,128)S(1)}, u32[]{:S(2)}) copy-start(f32[2,640,1024]{2,1,0:T(8,128)S(1)} %pad_maximum_fusion) | copy-start | bytes 15728644
  147.6 10.2 %collective-permute-start = (f32[640,1024]{1,0:T(8,128)}, f32[640,1024]{1,0:T(8,128)}, u32[]{:S(2)}, u32[]{:S(2)}) collective-permute-start(f32[640,1024]{1,0:T(8,128)} %dynamic-slice_bitcast_fusion), channel_id=1, source_target_pairs={{0,1},{1,0},{2,3},{3,2},{4,5},{5,4},{6,7},{7,6},{8,9},{9,8},{10,11... | collective-permute-start | bytes 7864328 | tf_op jit(solution)/shard_map/ppermute | solution.py:147
  224.5 23.8 %copy-start.11 = (f32[2,64,256]{2,1,0:T(8,128)S(1)}, f32[2,64,256]{2,1,0:T(8,128)}, u32[]{:S(2)}) copy-start(f32[2,64,256]{2,1,0:T(8,128)} %copy-done.10) | copy-start | bytes 393220
  224.5 23.8 %copy-start.20 = (f32[1,2,2,64,128]{4,3,2,1,0:T(8,128)S(1)}, f32[1,2,2,64,128]{4,3,2,1,0:T(8,128)}, u32[]{:S(2)}) copy-start(f32[1,2,2,64,128]{4,3,2,1,0:T(8,128)} %get-tuple-element.29) | copy-start | bytes 393220
  246.5 6.7 %collective-permute-start.1 = (f32[640,1024]{1,0:T(8,128)}, f32[640,1024]{1,0:T(8,128)}, u32[]{:S(2)}, u32[]{:S(2)}) collective-permute-start(f32[640,1024]{1,0:T(8,128)} %bitcast.93), channel_id=1, source_target_pairs={{0,1},{1,0},{2,3},{3,2},{4,5},{5,4},{6,7},{7,6},{8,9},{9,8},{10,11... | collective-permute-start | bytes 7864328 | tf_op jit(solution)/shard_map/ppermute | solution.py:158

commit v2 on v1

v2 whole, which is shorter than its diff:
```python
import functools
import math

import jax
import jax.numpy as jnp
from jax import lax
from jax.experimental import pallas as pl
from jax.experimental.pallas import tpu as pltpu
from jax.sharding import Mesh, PartitionSpec as P

MW = 64
NLON = 256
highest = lax.Precision.HIGHEST
tend_weight = 0.5

FINE = (("xl", 2), ("z", 8), ("y", 4), ("xh", 2), ("c", 2))
ALL = tuple(name for name, _ in FINE)
LAT = ("xl", "z", "y")
SWAP = [(0, 1), (1, 0)]


def device_id(x, y, z, core):
    return ((((x % 2) * 8 + z) * 4 + y) * 2 + x // 2) * 2 + core


def reduce_groups():
    wide, deep = [], []
    for y in range(4):
        for pair in range(4):
            wide.append([device_id(x, y, 2 * pair + q, 0) for x in range(4) for q in range(2)])
    for x in range(4):
        for pair in range(4):
            wide.append(
                [device_id(x, y, (2 * pair + 1 + q) % 8, 1) for y in range(4) for q in range(2)]
            )
    for x in range(4):
        for parity in range(2):
            deep.append(
                [device_id(x, y, 2 * pair + parity, 0) for y in range(4) for pair in range(4)]
            )
    for y in range(4):
        for parity in range(2):
            deep.append(
                [device_id(x, y, 2 * pair + parity, 1) for x in range(4) for pair in range(4)]
            )
    return wide, deep


WIDE, DEEP = reduce_groups()


def exchange(value, groups):
    return lax.all_to_all(value, ALL, 0, 0, axis_index_groups=groups, tiled=True)


def legendre_kernel(lat_count, wave_count, order_ref, forward_ref, backward_ref, table):
    bands = lat_count // 2
    place = lax.broadcasted_iota(jnp.int32, (1, lat_count), 1)
    lat_index = jnp.where(place >= bands, 2 * (place - bands) + 1, 2 * place).astype(jnp.float32)
    latitude = (lat_index + 0.5) * (math.pi / lat_count) - 0.5 * math.pi
    sine_lat = jnp.sin(latitude)
    cosine_lat = jnp.cos(latitude)
    quad_weight = cosine_lat * (math.pi / lat_count)
    order_m = jnp.full((1, lat_count), order_ref[0], jnp.int32).astype(jnp.float32)
    counter = lax.broadcasted_iota(jnp.int32, (1, lat_count), 1).astype(jnp.float32) + 1.0
    increments = 0.5 * jnp.log((2.0 * counter + 1.0) / (2.0 * counter))
    summed = jnp.sum(jnp.where(counter <= order_m, increments, 0.0), axis=1, keepdims=True)
    current = jnp.exp(0.5 * math.log(0.5) + summed + order_m * jnp.log(cosine_lat))
    previous = jnp.zeros_like(current)
    ratio_prev = jnp.ones_like(current)
    table[0:1, :] = current
    for offset in range(1, wave_count):
        degree = order_m + float(offset)
        ratio = jnp.sqrt((4.0 * degree * degree - 1.0) / (degree * degree - order_m * order_m))
        following = ratio * (sine_lat * current - previous / ratio_prev)
        previous, current, ratio_prev = current, following, ratio
        table[offset : offset + 1, :] = current
    degree = (
        lax.broadcasted_iota(jnp.int32, (wave_count, lat_count), 0) + order_ref[0]
    ).astype(jnp.float32)
    kept = degree <= wave_count - 1
    poly = jnp.where(kept, table[...], 0.0)
    damping = jnp.where(
        kept, 1.0 / (1.0 + degree * (degree + 1.0) / (wave_count * (wave_count - 1.0))), 0.0
    )
    scale = jnp.where(order_m > 0.0, 2.0 / NLON, 1.0 / NLON)
    weighted = poly * quad_weight
    poly = poly * scale
    forward_ref[...] = jnp.dot(
        poly.T, damping * weighted, precision=highest, preferred_element_type=jnp.float32
    )
    backward_ref[...] = jnp.dot(
        weighted.T, damping * poly, precision=highest, preferred_element_type=jnp.float32
    )


def legendre(order, lat_count, wave_count):
    square = jax.ShapeDtypeStruct((lat_count, lat_count), jnp.float32)
    return pl.pallas_call(
        functools.partial(legendre_kernel, lat_count, wave_count),
        out_shape=(square, square),
        in_specs=[pl.BlockSpec(memory_space=pltpu.SMEM)],
        out_specs=(pl.BlockSpec(memory_space=pltpu.VMEM),) * 2,
        scratch_shapes=[pltpu.VMEM((wave_count, lat_count), jnp.float32)],
        name="legendre",
    )(order)


def vmem(count):
    return [pl.BlockSpec(memory_space=pltpu.VMEM)] * count


def call(kernel, shapes, *operands, name, scalars=0, scratch=()):
    return pl.pallas_call(
        kernel,
        out_shape=tuple(jax.ShapeDtypeStruct(shape, dtype) for shape, dtype in shapes),
        in_specs=[pl.BlockSpec(memory_space=pltpu.SMEM)] * scalars
        + vmem(len(operands) - scalars),
        out_specs=tuple(vmem(len(shapes))),
        scratch_shapes=list(scratch),
        name=name,
        compiler_params=pltpu.CompilerParams(vmem_limit_bytes=60 * 1024 * 1024),
    )(*operands)


def mm(left, right):
    return jnp.dot(left, right, preferred_element_type=jnp.float32)


def mm_nt(left, right):
    return lax.dot_general(
        left, right, (((1,), (1,)), ((), ())), preferred_element_type=jnp.float32
    )


def mm_tn(left, right):
    return lax.dot_general(
        left, right, (((0,), (0,)), ((), ())), preferred_element_type=jnp.float32
    )


def mm_exact(left, right):
    return jnp.dot(left, right, precision=highest, preferred_element_type=jnp.float32)


def silu_pair(value):
    gate = jax.nn.sigmoid(value)
    return value * gate, gate * (1.0 + value * (1.0 - gate))


def wave_table(transposed):
    shape = (NLON, 2 * MW) if transposed else (2 * MW, NLON)
    lon = lax.broadcasted_iota(jnp.int32, shape, 0 if transposed else 1)
    row = lax.broadcasted_iota(jnp.int32, shape, 1 if transposed else 0)
    wave = jnp.where(row >= MW, row - MW, row)
    angle = ((lon * wave) & (NLON - 1)).astype(jnp.float32) * (2.0 * math.pi / NLON)
    return jnp.where(row >= MW, -jnp.sin(angle), jnp.cos(angle))


def store_waves(table, fields, out_ref):
    waves = mm_exact(table, jnp.concatenate(fields, axis=1))
    feat = fields[0].shape[1]
    for i in range(len(fields)):
        for p in range(2):
            out_ref[:, 2 * i + p, :] = waves[p * MW : (p + 1) * MW, i * feat : (i + 1) * feat]


def load_fields(table_t, waves_ref):
    columns = [
        jnp.concatenate([waves_ref[:, 2 * i, :], waves_ref[:, 2 * i + 1, :]], axis=0)
        for i in range(4)
    ]
    feat = columns[0].shape[1]
    grid = mm_exact(table_t, jnp.concatenate(columns, axis=1))
    return [grid[:, i * feat : (i + 1) * feat] for i in range(4)]


def physics(rows, w_first, w_middle, h1_ref, s1_ref, h2_ref, s2_ref, at):
    size = rows.shape[0]
    half = h1_ref.shape[2]
    value, slope = silu_pair(mm(rows, w_first[...]))
    hidden = value.astype(jnp.bfloat16)
    h1_ref[0, at : at + size, :] = hidden[:, :half]
    h1_ref[1, at : at + size, :] = hidden[:, half:]
    s1_ref[at : at + size, :] = slope
    value, slope = silu_pair(mm(hidden, w_middle[...]))
    h2_ref[at : at + size, :] = value.astype(jnp.bfloat16)
    s2_ref[at : at + size, :] = slope


def first_kernel(
    state, cotangent, w_first, w_middle, w_last,
    waves, table, table_t, h1, s1, h2, s2,
):
    table[...] = wave_table(False)
    table_t[...] = wave_table(True)
    moved = []
    for j in range(2):
        field = state[j]
        physics(field.astype(jnp.bfloat16), w_first, w_middle, h1, s1, h2, s2, j * NLON)
        tendency = mm(h2[j * NLON : (j + 1) * NLON, :], w_last[...])
        moved.append(field + tend_weight * tendency)
    store_waves(table[...], moved + [cotangent[0], cotangent[1]], waves)


def middle_kernel(
    waves_in, table, table_t, w_first, w_middle, w_last,
    waves, x, h1, h2, ga1, ga2, gt, s1, s2,
):
    fields = load_fields(table_t[...], waves_in)
    moved, grads = [], []
    for j in range(2):
        rows = slice(j * NLON, (j + 1) * NLON)
        field, pulled = fields[j], fields[2 + j]
        x[rows, :] = field.astype(jnp.bfloat16)
        physics(field.astype(jnp.bfloat16), w_first, w_middle, h1, s1, h2, s2, j * NLON)
        moved.append(field + tend_weight * mm(h2[rows, :], w_last[...]))
        scaled = (tend_weight * pulled).astype(jnp.bfloat16)
        gt[rows, :] = scaled
        back = (mm_nt(scaled, w_last[...]) * s2[rows, :]).astype(jnp.bfloat16)
        ga2[rows, :] = back
        back = (mm_nt(back, w_middle[...]) * s1[rows, :]).astype(jnp.bfloat16)
        ga1[rows, :] = back
        grads.append(pulled + mm_nt(back, w_first[...]))
    store_waves(table[...], moved + grads, waves)


def weights_kernel(x, h1, h2, ga1, ga2, gt, first, middle, last):
    first[...] = mm_tn(x[...], ga1[...])
    for h in range(2):
        middle[h] = mm_tn(h1[h], ga2[...])
    last[...] = mm_tn(h2[...], gt[...])


def last_kernel(
    core_ref, waves_in, table_t, state, h1, h2, s1, s2, w_middle, w_last, first, middle, last,
    final, keep, send, ga2, ga1, gt, last_sum, first_sum,
):
    fields = load_fields(table_t[...], waves_in)
    for j in range(2):
        rows = slice(j * NLON, (j + 1) * NLON)
        final[j] = fields[j]
        scaled = (tend_weight * fields[2 + j]).astype(jnp.bfloat16)
        gt[rows, :] = scaled
        back = (mm_nt(scaled, w_last[...]) * s2[rows, :]).astype(jnp.bfloat16)
        ga2[rows, :] = back
        back = (mm_nt(back, w_middle[...]) * s1[rows, :]).astype(jnp.bfloat16)
        ga1[rows, :] = back
    core = core_ref[0]
    rows = jnp.concatenate([state[0], state[1]], axis=0).astype(jnp.bfloat16)
    first_sum[...] = first[...] + mm_tn(rows, ga1[...])
    last_sum[...] = last[...] + mm_tn(h2[...], gt[...])
    half = h1.shape[2]
    part, blocks = half // 8, 8
    for out, which in ((send, 1 - core), (keep, core)):
        out[0:half, :] = middle[which] + mm_tn(h1[which], ga2[...])
        out[half : half + part, :] = first_sum[pl.ds(pl.multiple_of(which * part, part), part), :]
        for b in range(blocks):
            at = pl.multiple_of(which * half + b * part, part)
            out[half + part : half + 2 * part, b * 128 : (b + 1) * 128] = last_sum[
                pl.ds(at, part), :
            ]


def latitudes_kernel(owned, forward_op, backward_op, back):
    for i, operator in ((0, forward_op), (1, backward_op)):
        parts = [
            jnp.concatenate([owned[:, 4 * i + p, :], owned[:, 4 * i + 2 + p, :]], axis=0)
            for p in range(2)
        ]
        found = mm_exact(operator[...], jnp.concatenate(parts, axis=1))
        bands = owned.shape[0]
        feat = owned.shape[2]
        for j in range(2):
            for p in range(2):
                back[:, 4 * i + 2 * j + p, :] = found[
                    j * bands : (j + 1) * bands, p * feat : (p + 1) * feat
                ]


def sum_wide_kernel(parts, out):
    total = parts[0]
    for i in range(1, parts.shape[0]):
        total = total + parts[i]
    size = out.shape[1]
    for r in range(2):
        for b in range(8):
            out[r * 8 + b] = total[r * size : (r + 1) * size, b * 128 : (b + 1) * 128]


def sum_deep_kernel(parts, out):
    total = parts[0]
    for i in range(1, parts.shape[0]):
        total = total + parts[i]
    for i in range(out.shape[0]):
        out[i] = total


def spread_kernel(parts, out):
    size = parts.shape[1]
    for r in range(2):
        for b in range(8):
            piece = parts[r * 8 + b]
            for i in range(out.shape[0]):
                out[i, r * size : (r + 1) * size, b * 128 : (b + 1) * 128] = piece


def add_kernel(left, right, out):
    out[...] = left[...] + right[...]


def unpack_kernel(core_ref, own, other, first, middle, last):
    core = core_ref[0]
    half = middle.shape[0] // 2
    part, blocks = half // 8, 8
    for source, which in ((own, core), (other, 1 - core)):
        middle[pl.ds(pl.multiple_of(which * half, half), half), :] = source[0:half, :]
        first[pl.ds(pl.multiple_of(which * part, part), part), :] = source[half : half + part, :]
        for b in range(blocks):
            at = pl.multiple_of(which * half + b * part, part)
            last[pl.ds(at, part), :] = source[
                half + part : half + 2 * part, b * 128 : (b + 1) * 128
            ]


def body(state, cotangent, w_first, w_middle, w_last):
    _, lat_rows, lon_count, features = state.shape
    hidden = w_first.shape[1]
    rows = lat_rows * lon_count
    bands = lax.axis_size("xl") * lax.axis_size("z") * lax.axis_size("y")
    f32, bf16 = jnp.float32, jnp.bfloat16
    core = lax.axis_index("c").astype(jnp.int32).reshape(1)
    order = lax.axis_index(LAT).astype(jnp.int32).reshape(1)
    state, cotangent = state[0], cotangent[0]
    weights = (w_first, w_middle, w_last)
    waves_of = ((MW, 8, features), f32)
    halves = ((2, rows, hidden // 2), bf16)
    wide16, wide32 = ((rows, hidden), bf16), ((rows, hidden), f32)
    thin16 = ((rows, features), bf16)

    def cross(waves):
        owned = lax.all_to_all(waves, LAT, 0, 0, tiled=True)
        (back,) = call(
            latitudes_kernel, [waves_of], owned, forward_op, backward_op, name="latitudes"
        )
        return lax.all_to_all(back, LAT, 0, 0, tiled=True)

    forward_op, backward_op = legendre(order, lat_rows * bands, MW)
    waves, table, table_t, h1_0, s1_0, h2_0, s2_0 = call(
        first_kernel,
        [waves_of, ((2 * MW, NLON), f32), ((NLON, 2 * MW), f32), halves, wide32, wide16, wide32],
        state, cotangent, *weights,
        name="first",
    )
    waves = cross(waves)
    waves, x, h1, h2, ga1, ga2, gt = call(
        middle_kernel,
        [waves_of, thin16, halves, wide16, wide16, wide16, thin16],
        waves, table, table_t, *weights,
        name="middle",
        scratch=[pltpu.VMEM((rows, hidden), f32)] * 2,
    )
    waves = cross(waves)
    first, middle, last = call(
        weights_kernel,
        [((features, hidden), f32), ((2, hidden // 2, hidden), f32), ((hidden, features), f32)],
        x, h1, h2, ga1, ga2, gt,
        name="weights",
    )
    packed = ((hidden // 2 + features, hidden), f32)
    final, keep, send = call(
        last_kernel,
        [((lat_rows, lon_count, features), f32), packed, packed],
        core, waves, table_t, state, h1_0, h2_0, s1_0, s2_0, w_middle, w_last, first, middle, last,
        name="last",
        scalars=1,
        scratch=[
            pltpu.VMEM((rows, hidden), bf16),
            pltpu.VMEM((rows, hidden), bf16),
            pltpu.VMEM((rows, features), bf16),
            pltpu.VMEM((hidden, features), f32),
            pltpu.VMEM((features, hidden), f32),
        ],
    )
    (held,) = call(add_kernel, [packed], keep, lax.ppermute(send, "c", SWAP), name="add")
    wide, deep = len(WIDE[0]), len(DEEP[0])
    piece = packed[0][0] // wide
    held = exchange(held.reshape(wide, piece, hidden), WIDE)
    parts = ((deep, piece // 2, hidden // 8), f32)
    (held,) = call(sum_wide_kernel, [parts], held, name="sum_wide")
    held = exchange(held, DEEP)
    (held,) = call(sum_deep_kernel, [parts], held, name="sum_deep")
    held = exchange(held, DEEP)
    (held,) = call(spread_kernel, [((wide, piece, hidden), f32)], held, name="spread")
    held = exchange(held, WIDE).reshape(packed[0])
    first, middle, last = call(
        unpack_kernel,
        [((features, hidden), f32), ((hidden, hidden), f32), ((hidden, features), f32)],
        core, held, lax.ppermute(held, "c", SWAP),
        name="unpack",
        scalars=1,
    )
    return final[None], first, middle, last


def solution(mesh):
    fine = Mesh(mesh.devices.reshape(tuple(size for _, size in FINE)), ALL)
    grid = P(("xh", "c"), LAT, None, None)
    return jax.shard_map(
        body,
        mesh=fine,
        in_specs=(grid, grid, P(), P(), P()),
        out_specs=(grid, P(), P(), P()),
        check_vma=False,
    )
```

time: 262 us -> 227 us (0.87)
  matrix products: 53.6 us -> 0 us
  Pallas kernels: 1.27 us -> 54.4 us
  blocking collectives: 82.9 us -> 119 us
  local copies, waits for them, and re-layouts: 26.7 us -> 2.89 us
  other arithmetic: 17.3 us -> 0 us
  waiting for transfers between devices: 40.2 us -> 23.9 us
  starting transfers between devices: 37.7 us -> 25.1 us
    dot_general x28 -> x0, matrix products: 53.6 us -> none  [the longest x2 9.17 us: pull(): jnp.dot(hidden_first.T, middle_grad, preferred_element_type=jnp.float32)]
    pallas_call x0 -> x11, Pallas kernels: none -> 53.2 us  [call(): pl.pallas_call(kernel, out_shape=tuple((jax.ShapeDtypeStruct(shape, dtype...]
    all_to_all x0 -> x2, blocking collectives: none -> 33.4 us  [the longest x1 17.3 us: cross(): return lax.all_to_all(back, LAT, 0, 0, tiled=True)]
    all_to_all x4 -> x2, waiting for transfers between devices: 31.8 us -> 14.5 us  [the longest x1 9.59 us: cross(): owned = lax.all_to_all(waves, LAT, 0, 0, tiled=True)]
    all_to_all x4 -> x2, starting transfers between devices: 30.6 us -> 18.3 us  [the longest x1 13.6 us: cross(): owned = lax.all_to_all(waves, LAT, 0, 0, tiled=True)]
    another operation x6 -> x0, other arithmetic: 8.25 us -> none  [the longest x3 6.62 us: sum_gradients(): both = jnp.stack([low, high])]
    reshape x4 -> x0, local copies, waits for them, and re-layouts: 4.39 us -> none  [the longest x1 1.83 us: body(): grad = pulled + back_rows.reshape(pulled.shape)]
    convert_element_type x3 -> x0, local copies, waits for them, and re-layouts: 4.36 us -> none  [the longest x2 2.7 us: pull(): (tend_weight * pulled).astype(jnp.bfloat16).reshape(row_count, features)]
  transfers between devices with their start and end apart: 6 -> 4, of which waited for: 6 -> 4; matrix products, arithmetic and copies ran while one was open for 4% -> 0% of each run, Pallas kernels for 0% -> 3%
where the time goes in v2:
time: 227 us; the launch traced here: 226 us
  blocking collectives  119 us (52%)
  Pallas kernels  54.4 us (24%)
  starting transfers between devices  25.1 us (11%)
  waiting for transfers between devices  23.9 us (11%)
  local copies, waits for them, and re-layouts  2.89 us (1%)
    all_to_all x4, blocking collectives, exchange(): lax.all_to_all(value, ALL, 0, 0, axis_index_groups=groups, tiled=True)  85.3 us
    pallas_call x11, Pallas kernels, call(): pl.pallas_call(kernel, out_shape=tuple((jax.ShapeDtypeStruct(shape, dtype...  53.2 us
    all_to_all x1, blocking collectives, cross(): return lax.all_to_all(back, LAT, 0, 0, tiled=True)  17.3 us
    all_to_all x1, blocking collectives, cross(): owned = lax.all_to_all(waves, LAT, 0, 0, tiled=True)  16.1 us
    all_to_all x1, starting transfers between devices, cross(): owned = lax.all_to_all(waves, LAT, 0, 0, tiled=True)  13.6 us
    all_to_all x1, waiting for transfers between devices, cross(): owned = lax.all_to_all(waves, LAT, 0, 0, tiled=True)  9.59 us
    ppermute x1, starting transfers between devices, body(): lax.ppermute(send, 'c', SWAP)  5.88 us
    all_to_all x1, waiting for transfers between devices, cross(): return lax.all_to_all(back, LAT, 0, 0, tiled=True)  4.88 us
  transfers between devices with their start and end apart: 4, of which 4 were waited for; matrix products, arithmetic and copies ran while one was open for 0% of the time, Pallas kernels for 3%

profile of v2, /device:TPU:1, one launch (start us, length us, event | category | flops | bytes accessed | tf_op | source)
XLA Modules:
  0.0 225.7 jit_solution(13210620715506628856)
XLA Ops:
  0.6 7.4 %first.1 = (f32[64,8,128]{2,1,0:T(8,128)}, f32[128,256]{1,0:T(8,128)}, f32[256,128]{1,0:T(8,128)}, bf16[2,512,512]{2,1,0:T(8,128)(2,1)}, f32[512,1024]{1,0:T(8,1...) custom-call(f32[2,256,128]{2,1,0:T(8,128)} %bitcast.10, f32[2,256,128]{2,1,0:T(8,128)} %bitcast.12, ...), custom_call_target="tpu_custom_call" | custom-call | tf_op jit(solution)/shard_map/first/pallas_call | solution.py:114
  8.0 13.6 %all-to-all-start = ((f32[64,8,128]{2,1,0:T(8,128)}), f32[64,8,128]{2,1,0:T(8,128)S(1)}, u32[]{:S(2)}, u32[]{:S(2)}) async-start(f32[64,8,128]{2,1,0:T(8,128)} %get-tuple-element.29), calls=%async_computation | async-start | bytes 524288 | tf_op jit(solution)/shard_map/all_to_all | solution.py:342
  21.6 1.3 legendre.1
  22.9 9.6 %all-to-all-done.owned = f32[64,8,128]{2,1,0:T(8,128)S(1)} async-done(((f32[64,8,128]{2,1,0:T(8,128)}), f32[64,8,128]{2,1,0:T(8,128)S(1)}, u32[]{:S(2)}, u32[]{:S(2)}) %all-to-all-start) | async-done | bytes 262176 | tf_op jit(solution)/shard_map/all_to_all | solution.py:342
  32.5 0.0 copy-start.3
  32.5 0.7 copy-done.3
  33.2 2.3 %latitudes.2 = f32[64,8,128]{2,1,0:T(8,128)} custom-call(f32[64,8,128]{2,1,0:T(8,128)} %copy-done.3, f32[128,128]{1,0:T(8,128)} %get-tuple-element.30.forward_op, f32[128,128]{1,0:T(8,128)} %get-tuple-element.31.backward_op), custom_call_target="tpu_custom_call" | custom-call | tf_op jit(solution)/shard_map/latitudes/pallas_call | solution.py:114
  35.5 17.3 %all_to_all.40.waves_in = f32[64,8,128]{2,1,0:T(8,128)} all-to-all(f32[64,8,128]{2,1,0:T(8,128)} %latitudes.2), channel_id=1, replica_groups=mesh['xl'=2,'z'=8,'y'=4,'xh'=2,'c'=2] {'xl','z','y'}, dimensions={0} | all-to-all | bytes 524288 | tf_op jit(solution)/shard_map/all_to_all | solution.py:346
  52.8 7.6 %middle.1 = (f32[64,8,128]{2,1,0:T(8,128)}, bf16[512,128]{1,0:T(8,128)(2,1)}, bf16[2,512,512]{2,1,0:T(8,128)(2,1)}, bf16[512,1024]{1,0:T(8,128)(2,1)}, bf16[512,...) custom-call(f32[64,8,128]{2,1,0:T(8,128)} %all_to_all.40.waves_in, ...), custom_call_target="tpu_custom_call" | custom-call | tf_op jit(solution)/shard_map/middle/pallas_call | solution.py:114
  60.4 16.1 %all_to_all.41.owned = f32[64,8,128]{2,1,0:T(8,128)} all-to-all(f32[64,8,128]{2,1,0:T(8,128)} %get-tuple-element.34), channel_id=1, replica_groups=mesh['xl'=2,'z'=8,'y'=4,'xh'=2,'c'=2] {'xl','z','y'}, dimensions={0} | all-to-all | bytes 524288 | tf_op jit(solution)/shard_map/all_to_all | solution.py:342
  76.5 2.3 %latitudes.3 = f32[64,8,128]{2,1,0:T(8,128)} custom-call(f32[64,8,128]{2,1,0:T(8,128)} %all_to_all.41.owned, f32[128,128]{1,0:T(8,128)} %get-tuple-element.30.forward_op, f32[128,128]{1,0:T(8,128)} %get-tuple-element.31.backward_op), custom_call_target="tpu_custom_call" | custom-call | tf_op jit(solution)/shard_map/latitudes/pallas_call | solution.py:114
  78.8 4.8 %all-to-all-start.3 = ((f32[64,8,128]{2,1,0:T(8,128)}), f32[64,8,128]{2,1,0:T(8,128)S(1)}, u32[]{:S(2)}, u32[]{:S(2)}) async-start(f32[64,8,128]{2,1,0:T(8,128)} %latitudes.3), calls=%async_computation.3 | async-start | bytes 524288 | tf_op jit(solution)/shard_map/all_to_all | solution.py:346
  83.6 5.8 %weights.1 = (f32[128,1024]{1,0:T(8,128)}, f32[2,512,1024]{2,1,0:T(8,128)}, f32[1024,128]{1,0:T(8,128)}) custom-call(bf16[512,128]{1,0:T(8,128)(2,1)} %get-tuple-element.39.x, bf16[2,512,512]{2,1,0:T(8,128)(2,1)} %get-tuple-element.40.h1, bf16[512,1024]{1,0:T(8,128)(2,1)} %get-tuple-element.41.h2, bf16[512,1024]{1,0:T(8,128)(2,1)} %get-tuple-element.42.ga1, ...), custom_call_target="tpu_custom_call" | custom-call | tf_op jit(solution)/shard_map/weights/pallas_call | solution.py:114
  89.4 4.9 %all-to-all-done.3.waves_in = f32[64,8,128]{2,1,0:T(8,128)S(1)} async-done(((f32[64,8,128]{2,1,0:T(8,128)}), f32[64,8,128]{2,1,0:T(8,128)S(1)}, u32[]{:S(2)}, u32[]{:S(2)}) %all-to-all-start.3) | async-done | bytes 262176 | tf_op jit(solution)/shard_map/all_to_all | solution.py:346
  94.3 0.0 copy-start.2
  94.3 0.7 copy-done.2
  95.0 11.2 %last.1 = (f32[2,256,128]{2,1,0:T(8,128)}, f32[640,1024]{1,0:T(8,128)}, f32[640,1024]{1,0:T(8,128)}) custom-call(s32[1]{0:T(128)} %bitcast.core_ref, f32[64,8,128]{2,1,0:T(8,128)} %copy-done.2, f32[256,128]{1,0:T(8,128)} %get-tuple-element.33.table_t, f32[2,256,128]{2,1,0:T(8,128)} %bitcast.11, bf16[2,512,512]{2,1,0:T(8,128)(2,1)} %get-tuple-element.35.h1, ...), custom_call_target="tpu_custom_call" | custom-call | tf_op jit(solution)/shard_map/last/pallas_call | solution.py:114
  106.1 5.9 %collective-permute-start = (f32[640,1024]{1,0:T(8,128)}, f32[640,1024]{1,0:T(8,128)S(1)}, u32[]{:S(2)}, u32[]{:S(2)}) collective-permute-start(f32[640,1024]{1,0:T(8,128)} %get-tuple-element.50), channel_id=1, source_target_pairs={{0,1},{1,0},{2,3},{3,2},{4,5},{5,4},{6,7},{7,6},{8,9},{9,8},{10,11... | collective-permute-start | bytes 7864328 | tf_op jit(solution)/shard_map/ppermute | solution.py:385
  112.0 4.7 %collective-permute-done.right = f32[640,1024]{1,0:T(8,128)S(1)} collective-permute-done((f32[640,1024]{1,0:T(8,128)}, f32[640,1024]{1,0:T(8,128)S(1)}, u32[]{:S(2)}, u32[]{:S(2)}) %collective-permute-start) | collective-permute-done | bytes 2621472 | tf_op jit(solution)/shard_map/ppermute | solution.py:385
  116.7 0.0 copy-start.1
  116.8 1.5 copy-done.1
  118.2 4.3 %add.9 = f32[640,1024]{1,0:T(8,128)} custom-call(f32[640,1024]{1,0:T(8,128)} %get-tuple-element.49.left, f32[640,1024]{1,0:T(8,128)} %copy-done.1), custom_call_target="tpu_custom_call" | custom-call | tf_op jit(solution)/shard_map/add/pallas_call | solution.py:114
  122.6 23.5 %all_to_all.42.parts = f32[8,80,1024]{2,1,0:T(8,128)} all-to-all(f32[8,80,1024]{2,1,0:T(8,128)} %bitcast.9), channel_id=1, replica_groups={{0,16,128,144,2,18,130,146},{32,48,160,176,34,50,162,178},{64,80,192,20..., dimensions={0} | all-to-all | bytes 5242880 | tf_op jit(solution)/shard_map/all_to_all | solution.py:53
  146.1 2.6 %sum_wide.1 = f32[16,40,128]{2,1,0:T(8,128)} custom-call(f32[8,80,1024]{2,1,0:T(8,128)} %all_to_all.42.parts), custom_call_target="tpu_custom_call" | custom-call | tf_op jit(solution)/shard_map/sum_wide/pallas_call | solution.py:114
  148.7 20.0 %all_to_all.43.parts = f32[16,40,128]{2,1,0:T(8,128)} all-to-all(f32[16,40,128]{2,1,0:T(8,128)} %sum_wide.1), channel_id=1, replica_groups={{0,32,64,96,4,36,68,100,8,40,72,104,12,44,76,108},{16,48,80,112,20,52,8..., dimensions={0} | all-to-all | bytes 655360 | tf_op jit(solution)/shard_map/all_to_all | solution.py:53
  168.7 1.7 sum_deep.1
  170.5 19.6 %all_to_all.44.parts = f32[16,40,128]{2,1,0:T(8,128)} all-to-all(f32[16,40,128]{2,1,0:T(8,128)} %sum_deep.1), channel_id=1, replica_groups={{0,32,64,96,4,36,68,100,8,40,72,104,12,44,76,108},{16,48,80,112,20,52,8..., dimensions={0} | all-to-all | bytes 655360 | tf_op jit(solution)/shard_map/all_to_all | solution.py:53
  190.1 2.8 %spread.1 = f32[8,80,1024]{2,1,0:T(8,128)} custom-call(f32[16,40,128]{2,1,0:T(8,128)} %all_to_all.44.parts), custom_call_target="tpu_custom_call" | custom-call | tf_op jit(solution)/shard_map/spread/pallas_call | solution.py:114
  192.8 22.1 %all_to_all.45 = f32[8,80,1024]{2,1,0:T(8,128)S(1)} all-to-all(f32[8,80,1024]{2,1,0:T(8,128)} %spread.1), channel_id=1, replica_groups={{0,16,128,144,2,18,130,146},{32,48,160,176,34,50,162,178},{64,80,192,20..., dimensions={0} | all-to-all | bytes 5242880 | tf_op jit(solution)/shard_map/all_to_all | solution.py:53
  215.0 0.0 copy-start
  215.0 0.9 collective-permute-start.1
  215.8 4.7 %collective-permute-done.1.other = f32[640,1024]{1,0:T(8,128)} collective-permute-done((f32[640,1024]{1,0:T(8,128)S(1)}, f32[640,1024]{1,0:T(8,128)}, u32[]{:S(2)}, u32[]{:S(2)}) %collective-permute-start.1) | collective-permute-done | bytes 2621472 | tf_op jit(solution)/shard_map/ppermute | solution.py:399
  220.5 0.0 copy-done
  220.5 5.2 %unpack.1 = (f32[128,1024]{1,0:T(8,128)}, f32[1024,1024]{1,0:T(8,128)}, f32[1024,128]{1,0:T(8,128)}) custom-call(s32[1]{0:T(128)} %bitcast.core_ref, f32[640,1024]{1,0:T(8,128)} %bitcast.8, f32[640,1024]{1,0:T(8,128)} %collective-permute-done.1.other), custom_call_target="tpu_custom_call" | custom-call | tf_op jit(solution)/shard_map/unpack/pallas_call | solution.py:114
Async XLA Ops:
  8.0 24.4 %all-to-all-start = ((f32[64,8,128]{2,1,0:T(8,128)}), f32[64,8,128]{2,1,0:T(8,128)S(1)}, u32[]{:S(2)}, u32[]{:S(2)}) async-start(f32[64,8,128]{2,1,0:T(8,128)} %get-tuple-element.29), calls=%async_computation | async-start | bytes 524288 | tf_op jit(solution)/shard_map/all_to_all | solution.py:342
  32.5 0.7 copy-start.3
  78.8 15.5 %all-to-all-start.3 = ((f32[64,8,128]{2,1,0:T(8,128)}), f32[64,8,128]{2,1,0:T(8,128)S(1)}, u32[]{:S(2)}, u32[]{:S(2)}) async-start(f32[64,8,128]{2,1,0:T(8,128)} %latitudes.3), calls=%async_computation.3 | async-start | bytes 524288 | tf_op jit(solution)/shard_map/all_to_all | solution.py:346
  94.3 0.7 copy-start.2
  106.1 10.6 %collective-permute-start = (f32[640,1024]{1,0:T(8,128)}, f32[640,1024]{1,0:T(8,128)S(1)}, u32[]{:S(2)}, u32[]{:S(2)}) collective-permute-start(f32[640,1024]{1,0:T(8,128)} %get-tuple-element.50), channel_id=1, source_target_pairs={{0,1},{1,0},{2,3},{3,2},{4,5},{5,4},{6,7},{7,6},{8,9},{9,8},{10,11... | collective-permute-start | bytes 7864328 | tf_op jit(solution)/shard_map/ppermute | solution.py:385
  116.7 1.5 copy-start.1
  215.0 5.5 %copy-start = (f32[8,80,1024]{2,1,0:T(8,128)}, f32[8,80,1024]{2,1,0:T(8,128)S(1)}, u32[]{:S(2)}) copy-start(f32[8,80,1024]{2,1,0:T(8,128)S(1)} %all_to_all.45) | copy-start | bytes 7864324
  215.0 5.5 %collective-permute-start.1 = (f32[640,1024]{1,0:T(8,128)S(1)}, f32[640,1024]{1,0:T(8,128)}, u32[]{:S(2)}, u32[]{:S(2)}) collective-permute-start(f32[640,1024]{1,0:T(8,128)S(1)} %bitcast.7), channel_id=1, source_target_pairs={{0,1},{1,0},{2,3},{3,2},{4,5},{5,4},{6,7},{7,6},{8,9},{9,8},{10,11... | collective-permute-start | bytes 7864328 | tf_op jit(solution)/shard_map/ppermute | solution.py:399

commit v3 on v2

--- a/solution.py
+++ b/solution.py
@@ -103,6 +103,7 @@
         out_specs=(pl.BlockSpec(memory_space=pltpu.VMEM),) * 2,
         scratch_shapes=[pltpu.VMEM((wave_count, lat_count), jnp.float32)],
         name="legendre",
+        compiler_params=pltpu.CompilerParams(vmem_limit_bytes=2 * 1024 * 1024),
     )(order)
 
 
@@ -110,16 +111,24 @@
     return [pl.BlockSpec(memory_space=pltpu.VMEM)] * count
 
 
-def call(kernel, shapes, *operands, name, scalars=0, scratch=()):
+def nbytes(shape, dtype):
+    return math.prod(shape) * jnp.dtype(dtype).itemsize
+
+
+def call(kernel, shapes, *operands, name, scalars=0, scratch=(), spare=4):
+    held = [(operand.shape, operand.dtype) for operand in operands[scalars:]]
+    held += list(shapes) + list(scratch)
     return pl.pallas_call(
         kernel,
         out_shape=tuple(jax.ShapeDtypeStruct(shape, dtype) for shape, dtype in shapes),
         in_specs=[pl.BlockSpec(memory_space=pltpu.SMEM)] * scalars
         + vmem(len(operands) - scalars),
         out_specs=tuple(vmem(len(shapes))),
-        scratch_shapes=list(scratch),
+        scratch_shapes=[pltpu.VMEM(shape, dtype) for shape, dtype in scratch],
         name=name,
-        compiler_params=pltpu.CompilerParams(vmem_limit_bytes=60 * 1024 * 1024),
+        compiler_params=pltpu.CompilerParams(
+            vmem_limit_bytes=sum(nbytes(*each) for each in held) + spare * 1024 * 1024
+        ),
     )(*operands)
 
 
@@ -233,8 +242,8 @@
 
 
 def last_kernel(
-    core_ref, waves_in, table_t, state, h1, h2, s1, s2, w_middle, w_last, first, middle, last,
-    final, keep, send, ga2, ga1, gt, last_sum, first_sum,
+    core_ref, waves_in, table_t, h1, h2, s2, w_last, middle,
+    final, send, ga2, gt,
 ):
     fields = load_fields(table_t[...], waves_in)
     for j in range(2):
@@ -242,24 +251,31 @@
         final[j] = fields[j]
         scaled = (tend_weight * fields[2 + j]).astype(jnp.bfloat16)
         gt[rows, :] = scaled
-        back = (mm_nt(scaled, w_last[...]) * s2[rows, :]).astype(jnp.bfloat16)
-        ga2[rows, :] = back
-        back = (mm_nt(back, w_middle[...]) * s1[rows, :]).astype(jnp.bfloat16)
-        ga1[rows, :] = back
-    core = core_ref[0]
+        ga2[rows, :] = (mm_nt(scaled, w_last[...]) * s2[rows, :]).astype(jnp.bfloat16)
+    which = 1 - core_ref[0]
+    send[...] = middle[which] + mm_tn(h1[which], ga2[...])
+
+
+def rest_kernel(
+    core_ref, state, h1, h2, s1, ga2, gt, w_middle, first, middle, last,
+    keep, keep_thin, send_thin, ga1, first_sum, last_sum,
+):
+    for j in range(2):
+        rows = slice(j * NLON, (j + 1) * NLON)
+        back = mm_nt(ga2[rows, :], w_middle[...])
+        ga1[rows, :] = (back * s1[rows, :]).astype(jnp.bfloat16)
     rows = jnp.concatenate([state[0], state[1]], axis=0).astype(jnp.bfloat16)
     first_sum[...] = first[...] + mm_tn(rows, ga1[...])
     last_sum[...] = last[...] + mm_tn(h2[...], gt[...])
+    core = core_ref[0]
     half = h1.shape[2]
     part, blocks = half // 8, 8
-    for out, which in ((send, 1 - core), (keep, core)):
-        out[0:half, :] = middle[which] + mm_tn(h1[which], ga2[...])
-        out[half : half + part, :] = first_sum[pl.ds(pl.multiple_of(which * part, part), part), :]
+    for out, which in ((send_thin, 1 - core), (keep_thin, core)):
+        out[0:part, :] = first_sum[pl.ds(pl.multiple_of(which * part, part), part), :]
         for b in range(blocks):
             at = pl.multiple_of(which * half + b * part, part)
-            out[half + part : half + 2 * part, b * 128 : (b + 1) * 128] = last_sum[
-                pl.ds(at, part), :
-            ]
+            out[part : 2 * part, b * 128 : (b + 1) * 128] = last_sum[pl.ds(at, part), :]
+    keep[...] = middle[core] + mm_tn(h1[core], ga2[...])
 
 
 def latitudes_kernel(owned, forward_op, backward_op, back):
@@ -305,22 +321,70 @@
                 out[i, r * size : (r + 1) * size, b * 128 : (b + 1) * 128] = piece
 
 
-def add_kernel(left, right, out):
-    out[...] = left[...] + right[...]
-
-
-def unpack_kernel(core_ref, own, other, first, middle, last):
-    core = core_ref[0]
+def add_kernel(left, left_thin, right, right_thin, out):
+    half = left.shape[0]
+    out[0:half, :] = left[...] + right[...]
+    out[half:, :] = left_thin[...] + right_thin[...]
+
+
+def place(core_ref, other, source, outs, sem):
+    first, middle, last = outs
+    which = 1 - core_ref[0] if other else core_ref[0]
     half = middle.shape[0] // 2
     part, blocks = half // 8, 8
-    for source, which in ((own, core), (other, 1 - core)):
-        middle[pl.ds(pl.multiple_of(which * half, half), half), :] = source[0:half, :]
-        first[pl.ds(pl.multiple_of(which * part, part), part), :] = source[half : half + part, :]
-        for b in range(blocks):
-            at = pl.multiple_of(which * half + b * part, part)
-            last[pl.ds(at, part), :] = source[
-                half + part : half + 2 * part, b * 128 : (b + 1) * 128
-            ]
+    copies = [
+        (source.at[pl.ds(0, half)], middle.at[pl.ds(pl.multiple_of(which * half, half), half)]),
+        (
+            source.at[pl.ds(half, part)],
+            first.at[pl.ds(pl.multiple_of(which * part, part), part)],
+        ),
+    ]
+    for b in range(blocks):
+        at = pl.multiple_of(which * half + b * part, part)
+        copies.append(
+            (
+                source.at[pl.ds(half + part, part), pl.ds(b * 128, 128)],
+                last.at[pl.ds(at, part)],
+            )
+        )
+    started = [
+        pltpu.make_async_copy(start, end, sem.at[i]) for i, (start, end) in enumerate(copies)
+    ]
+    for copy in started:
+        copy.start()
+    for copy in started:
+        copy.wait()
+
+
+def own_kernel(core_ref, source, first, middle, last, sem):
+    place(core_ref, False, source, (first, middle, last), sem)
+
+
+def other_kernel(core_ref, source, _first, _middle, _last, first, middle, last, sem):
+    place(core_ref, True, source, (first, middle, last), sem)
+
+
+def unpack(core, own, other, hidden, features):
+    outs = [
+        jax.ShapeDtypeStruct(shape, jnp.float32)
+        for shape in ((features, hidden), (hidden, hidden), (hidden, features))
+    ]
+    smem = pl.BlockSpec(memory_space=pltpu.SMEM)
+    hbm = pl.BlockSpec(memory_space=pltpu.HBM)
+    settings = dict(
+        out_shape=tuple(outs),
+        out_specs=(hbm,) * 3,
+        scratch_shapes=[pltpu.SemaphoreType.DMA((10,))],
+        compiler_params=pltpu.CompilerParams(vmem_limit_bytes=4 * 1024 * 1024),
+    )
+    grads = pl.pallas_call(own_kernel, in_specs=[smem] + vmem(1), name="own", **settings)(core, own)
+    return pl.pallas_call(
+        other_kernel,
+        in_specs=[smem] + vmem(1) + [hbm] * 3,
+        input_output_aliases={2: 0, 3: 1, 4: 2},
+        name="other",
+        **settings,
+    )(core, other, *grads)
 
 
 def body(state, cotangent, w_first, w_middle, w_last):
@@ -358,7 +422,7 @@
         [waves_of, thin16, halves, wide16, wide16, wide16, thin16],
         waves, table, table_t, *weights,
         name="middle",
-        scratch=[pltpu.VMEM((rows, hidden), f32)] * 2,
+        scratch=[wide32] * 2,
     )
     waves = cross(waves)
     first, middle, last = call(
@@ -368,21 +432,27 @@
         name="weights",
     )
     packed = ((hidden // 2 + features, hidden), f32)
-    final, keep, send = call(
+    half32, thin32 = ((hidden // 2, hidden), f32), ((features, hidden), f32)
+    final, send, ga2, gt = call(
         last_kernel,
-        [((lat_rows, lon_count, features), f32), packed, packed],
-        core, waves, table_t, state, h1_0, h2_0, s1_0, s2_0, w_middle, w_last, first, middle, last,
+        [((lat_rows, lon_count, features), f32), half32, wide16, thin16],
+        core, waves, table_t, h1_0, h2_0, s2_0, w_last, middle,
         name="last",
         scalars=1,
-        scratch=[
-            pltpu.VMEM((rows, hidden), bf16),
-            pltpu.VMEM((rows, hidden), bf16),
-            pltpu.VMEM((rows, features), bf16),
-            pltpu.VMEM((hidden, features), f32),
-            pltpu.VMEM((features, hidden), f32),
-        ],
-    )
-    (held,) = call(add_kernel, [packed], keep, lax.ppermute(send, "c", SWAP), name="add")
+    )
+    received = lax.ppermute(send, "c", SWAP)
+    keep, keep_thin, send_thin = call(
+        rest_kernel,
+        [half32, thin32, thin32],
+        core, state, h1_0, h2_0, s1_0, ga2, gt, w_middle, first, middle, last,
+        name="rest",
+        scalars=1,
+        scratch=[wide16, thin32, ((hidden, features), f32)],
+    )
+    (held,) = call(
+        add_kernel, [packed], keep, keep_thin, received, lax.ppermute(send_thin, "c", SWAP),
+        name="add",
+    )
     wide, deep = len(WIDE[0]), len(DEEP[0])
     piece = packed[0][0] // wide
     held = exchange(held.reshape(wide, piece, hidden), WIDE)
@@ -393,13 +463,8 @@
     held = exchange(held, DEEP)
     (held,) = call(spread_kernel, [((wide, piece, hidden), f32)], held, name="spread")
     held = exchange(held, WIDE).reshape(packed[0])
-    first, middle, last = call(
-        unpack_kernel,
-        [((features, hidden), f32), ((hidden, hidden), f32), ((hidden, features), f32)],
-        core, held, lax.ppermute(held, "c", SWAP),
-        name="unpack",
-        scalars=1,
-    )
+    other = lax.ppermute(held, "c", SWAP)
+    first, middle, last = unpack(core, held, other, hidden, features)
     return final[None], first, middle, last
 
 

time: 227 us -> 218 us (0.960)
  local copies, waits for them, and re-layouts: 2.89 us -> 35.2 us
  Pallas kernels: 54.4 us -> 22.1 us
  waiting for transfers between devices: 23.9 us -> 13.3 us
    pallas_call x11, Pallas kernels: 53.2 us -> 18.4 us  [call(): pl.pallas_call(kernel, out_shape=tuple((jax.ShapeDtypeStruct(shape, dtype...]
    unnamed x8 -> x90, local copies, waits for them, and re-layouts: 2.89 us -> 35.2 us
    ppermute x2 -> x3, waiting for transfers between devices: 9.41 us -> 4.52 us  [the longest x1 2.98 us: body(): other = lax.ppermute(held, 'c', SWAP)]
    all_to_all x1, waiting for transfers between devices: 4.88 us -> 0.01 us  [cross(): return lax.all_to_all(back, LAT, 0, 0, tiled=True)]
    pallas_call x0 -> x2, Pallas kernels: none -> 3.1 us  [the longest x1 1.55 us: unpack(): pl.pallas_call(own_kernel, in_specs=[smem] + vmem(1), name='own', **setti...]
    ppermute x2 -> x3, starting transfers between devices: 6.73 us -> 4.52 us  [the longest x1 3.31 us: body(): received = lax.ppermute(send, 'c', SWAP)]
  transfers between devices with their start and end apart: 4 -> 5, of which waited for: 4 -> 3; matrix products, arithmetic and copies ran while one was open for 0% -> 0% of each run, Pallas kernels for 3% -> 3%
where the time goes in v3:
time: 218 us; the launch traced here: 217 us
  blocking collectives  121 us (56%)
  local copies, waits for them, and re-layouts  35.2 us (16%)
  starting transfers between devices  24.3 us (11%)
  Pallas kernels  22.1 us (10%)
  waiting for transfers between devices  13.3 us (6%)
    all_to_all x4, blocking collectives, exchange(): lax.all_to_all(value, ALL, 0, 0, axis_index_groups=groups, tiled=True)  87.1 us
    unnamed x90, local copies, waits for them, and re-layouts  35.2 us
    pallas_call x11, Pallas kernels, call(): pl.pallas_call(kernel, out_shape=tuple((jax.ShapeDtypeStruct(shape, dtype...  18.4 us
    all_to_all x1, blocking collectives, cross(): return lax.all_to_all(back, LAT, 0, 0, tiled=True)  17 us
    all_to_all x1, blocking collectives, cross(): owned = lax.all_to_all(waves, LAT, 0, 0, tiled=True)  16.9 us
    all_to_all x1, starting transfers between devices, cross(): owned = lax.all_to_all(waves, LAT, 0, 0, tiled=True)  13.8 us
    all_to_all x1, waiting for transfers between devices, cross(): owned = lax.all_to_all(waves, LAT, 0, 0, tiled=True)  8.83 us
    all_to_all x1, starting transfers between devices, cross(): return lax.all_to_all(back, LAT, 0, 0, tiled=True)  5.91 us
  transfers between devices with their start and end apart: 5, of which 3 were waited for; matrix products, arithmetic and copies ran while one was open for 0% of the time, Pallas kernels for 3%

profile of v3, /device:TPU:1, one launch (start us, length us, event | category | flops | bytes accessed | tf_op | source)
XLA Modules:
  0.0 217.0 jit_solution(8087151318520447996)
XLA Ops:
  0.6 1.6 copy-done
  2.2 0.9 copy-done.8
  3.2 0.9 copy-done.22
  4.1 0.9 copy-done.24
  5.1 0.9 copy-done.31
  6.0 3.7 %first.1 = (f32[64,8,128]{2,1,0:T(8,128)S(1)}, f32[128,256]{1,0:T(8,128)S(1)}, f32[256,128]{1,0:T(8,128)S(1)}, bf16[2,512,512]{2,1,0:T(8,128)(2,1)S(1)}, f32[512...) custom-call(f32[2,256,128]{2,1,0:T(8,128)S(1)} %bitcast.10, f32[2,256,128]{2,1,0:T(8,128)S(1)} %bitcast.12, ...), custom_call_target="tpu_custom_call" | custom-call | tf_op jit(solution)/shard_map/first/pallas_call | solution.py:121
  9.8 1.0 copy-done.5
  10.8 1.4 copy-done.10
  12.1 1.4 copy-done.12
  13.5 0.7 copy-done.38
  14.2 0.7 copy-done.39
  14.8 13.8 %all-to-all-start = ((f32[64,8,128]{2,1,0:T(8,128)}), f32[64,8,128]{2,1,0:T(8,128)}, u32[]{:S(2)}, u32[]{:S(2)}) async-start(f32[64,8,128]{2,1,0:T(8,128)} %copy-done.38), calls=%async_computation | async-start | bytes 524288 | tf_op jit(solution)/shard_map/all_to_all | solution.py:406
  28.7 0.6 legendre.1
  29.3 0.6 copy-done.32
  29.9 0.6 copy-done.35
  30.5 8.8 %all-to-all-done.owned = f32[64,8,128]{2,1,0:T(8,128)} async-done(((f32[64,8,128]{2,1,0:T(8,128)}), f32[64,8,128]{2,1,0:T(8,128)}, u32[]{:S(2)}, u32[]{:S(2)}) %all-to-all-start) | async-done | bytes 262176 | tf_op jit(solution)/shard_map/all_to_all | solution.py:406
  39.4 0.8 copy-done.33
  40.2 0.8 copy-done.36
  41.1 1.6 latitudes.2
  42.7 17.0 %all_to_all.40.waves_in = f32[64,8,128]{2,1,0:T(8,128)S(1)} all-to-all(f32[64,8,128]{2,1,0:T(8,128)S(1)} %latitudes.2), channel_id=1, replica_groups=mesh['xl'=2,'z'=8,'y'=4,'xh'=2,'c'=2] {'xl','z','y'}, dimensions={0} | all-to-all | bytes 524288 | tf_op jit(solution)/shard_map/all_to_all | solution.py:410
  59.7 0.9 copy-done.23
  60.6 0.9 copy-done.40
  61.5 5.0 %middle.1 = (f32[64,8,128]{2,1,0:T(8,128)S(1)}, bf16[512,128]{1,0:T(8,128)(2,1)S(1)}, bf16[2,512,512]{2,1,0:T(8,128)(2,1)S(1)}, bf16[512,1024]{1,0:T(8,128)(2,1)...) custom-call(f32[64,8,128]{2,1,0:T(8,128)S(1)} %all_to_all.40.waves_in, ...), custom_call_target="tpu_custom_call" | custom-call | tf_op jit(solution)/shard_map/middle/pallas_call | solution.py:121
  66.6 0.0 copy-start.14
  66.6 1.0 copy-done.14
  67.5 1.0 copy-done.16
  68.5 1.0 copy-done.18
  69.5 1.1 copy-done.20
  70.5 16.9 %all_to_all.41.owned = f32[64,8,128]{2,1,0:T(8,128)S(1)} all-to-all(f32[64,8,128]{2,1,0:T(8,128)S(1)} %get-tuple-element.41), channel_id=1, replica_groups=mesh['xl'=2,'z'=8,'y'=4,'xh'=2,'c'=2] {'xl','z','y'}, dimensions={0} | all-to-all | bytes 524288 | tf_op jit(solution)/shard_map/all_to_all | solution.py:406
  87.5 0.6 latitudes.3
  88.1 0.0 copy-start.26
  88.1 0.7 copy-done.26
  88.8 5.9 %all-to-all-start.3 = ((f32[64,8,128]{2,1,0:T(8,128)}), f32[64,8,128]{2,1,0:T(8,128)}, u32[]{:S(2)}, u32[]{:S(2)}) async-start(f32[64,8,128]{2,1,0:T(8,128)} %copy-done.26), calls=%async_computation.3 | async-start | bytes 524288 | tf_op jit(solution)/shard_map/all_to_all | solution.py:410
  94.7 0.0 copy-start.15
  94.7 1.2 copy-done.15
  95.9 1.2 copy-done.17
  97.2 1.2 copy-done.19
  98.4 1.2 copy-done.21
  99.6 0.9 copy-done.42
  100.5 0.9 copy-done.44
  101.4 1.7 weights.1
  103.1 0.0 copy-start.2
  103.1 2.0 copy-done.2
  105.1 0.8 copy-done.27
  105.9 0.8 copy-done.29
  106.7 2.2 %copy-done.3 = f32[2,512,1024]{2,1,0:T(8,128)S(1)} copy-done((f32[2,512,1024]{2,1,0:T(8,128)S(1)}, f32[2,512,1024]{2,1,0:T(8,128)}, u32[]{:S(2)}) %copy-start.3) | copy-done | bytes 4194328
  108.9 1.2 copy-done.6
  110.2 1.6 copy-done.13
  111.8 2.7 %last.1 = (f32[2,256,128]{2,1,0:T(8,128)}, f32[512,1024]{1,0:T(8,128)S(1)}, bf16[512,1024]{1,0:T(8,128)(2,1)S(1)}, bf16[512,128]{1,0:T(8,128)(2,1)S(1)}) custom-call(s32[1]{0:T(128)} %bitcast.core_ref, f32[64,8,128]{2,1,0:T(8,128)} %all-to-all-done.3.waves_in, f32[256,128]{1,0:T(8,128)S(1)} %get-tuple-element.40.table_t, ...), custom_call_target="tpu_custom_call" | custom-call | tf_op jit(solution)/shard_map/last/pallas_call | solution.py:121
  114.5 3.3 %collective-permute-start = (f32[512,1024]{1,0:T(8,128)S(1)}, f32[512,1024]{1,0:T(8,128)S(1)}, u32[]{:S(2)}, u32[]{:S(2)}) collective-permute-start(f32[512,1024]{1,0:T(8,128)S(1)} %get-tuple-element.60), channel_id=1, source_target_pairs={{0,1},{1,0},{2,3},{3,2},{4,5},{5,4},{6,7},{7,6},{8,9},{9,8},{10,11... | collective-permute-start | bytes 6291464 | tf_op jit(solution)/shard_map/ppermute | solution.py:443
  117.8 2.3 %rest.1 = (f32[512,1024]{1,0:T(8,128)S(1)}, f32[128,1024]{1,0:T(8,128)S(1)}, f32[128,1024]{1,0:T(8,128)S(1)}) custom-call(s32[1]{0:T(128)} %bitcast.core_ref, f32[2,256,128]{2,1,0:T(8,128)S(1)} %bitcast.11, bf16[2,512,512]{2,1,0:T(8,128)(2,1)S(1)} %get-tuple-element.42.h1, bf16[512,1024]{1,0:T(8,128)(2,1)S(1)} %copy-done.7, f32[512,1024]{1,0:T(8,128)S(1)} %copy-done.11, ...), custom_call_target="tpu_custom_call" | custom-call | tf_op jit(solution)/shard_map/rest/pallas_call | solution.py:121
  120.2 0.8 collective-permute-start.1
  121.0 1.5 collective-permute-done.1.right_thin
  122.5 0.3 add.9
  122.8 24.5 %all_to_all.42.parts = f32[8,80,1024]{2,1,0:T(8,128)S(1)} all-to-all(f32[8,80,1024]{2,1,0:T(8,128)S(1)} %bitcast.9), channel_id=1, replica_groups={{0,16,128,144,2,18,130,146},{32,48,160,176,34,50,162,178},{64,80,192,20..., dimensions={0} | all-to-all | bytes 5242880 | tf_op jit(solution)/shard_map/all_to_all | solution.py:53
  147.2 0.1 sum_wide.1
  147.4 23.0 %all_to_all.43.parts = f32[16,40,128]{2,1,0:T(8,128)S(1)} all-to-all(f32[16,40,128]{2,1,0:T(8,128)S(1)} %sum_wide.1), channel_id=1, replica_groups={{0,32,64,96,4,36,68,100,8,40,72,104,12,44,76,108},{16,48,80,112,20,52,8..., dimensions={0} | all-to-all | bytes 655360 | tf_op jit(solution)/shard_map/all_to_all | solution.py:53
  170.4 17.9 %all_to_all.44.parts = f32[16,40,128]{2,1,0:T(8,128)S(1)} all-to-all(f32[16,40,128]{2,1,0:T(8,128)S(1)} %sum_deep.1), channel_id=1, replica_groups={{0,32,64,96,4,36,68,100,8,40,72,104,12,44,76,108},{16,48,80,112,20,52,8..., dimensions={0} | all-to-all | bytes 655360 | tf_op jit(solution)/shard_map/all_to_all | solution.py:53
  188.4 0.3 spread.1
  188.7 21.6 %all_to_all.45 = f32[8,80,1024]{2,1,0:T(8,128)S(1)} all-to-all(f32[8,80,1024]{2,1,0:T(8,128)S(1)} %spread.1), channel_id=1, replica_groups={{0,16,128,144,2,18,130,146},{32,48,160,176,34,50,162,178},{64,80,192,20..., dimensions={0} | all-to-all | bytes 5242880 | tf_op jit(solution)/shard_map/all_to_all | solution.py:53
  210.3 0.4 collective-permute-start.2
  210.7 1.6 own.1
  212.3 3.0 %collective-permute-done.2.source = f32[640,1024]{1,0:T(8,128)S(1)} collective-permute-done((f32[640,1024]{1,0:T(8,128)S(1)}, f32[640,1024]{1,0:T(8,128)S(1)}, u32[]{:S(2)}, u32[]{:S(2)}) %collective-permute-start.2) | collective-permute-done | bytes 2621472 | tf_op jit(solution)/shard_map/ppermute | solution.py:466
  215.2 1.6 other.1
  (56 shorter events, 0.1 us)
Async XLA Ops:
  0.6 1.6 copy-start
  2.2 0.9 copy-start.8
  3.2 0.9 copy-start.22
  4.1 0.9 copy-start.24
  5.1 0.9 copy-start.31
  6.0 53.6 %copy-start.1 = (bf16[1024,1024]{1,0:T(8,128)(2,1)S(1)}, bf16[1024,1024]{1,0:T(8,128)(2,1)}, u32[]{:S(2)}) copy-start(bf16[1024,1024]{1,0:T(8,128)(2,1)} %w_middle.5) | copy-start | bytes 6291460
  6.0 53.6 %copy-start.9 = (bf16[1024,128]{1,0:T(8,128)(2,1)S(1)}, bf16[1024,128]{1,0:T(8,128)(2,1)}, u32[]{:S(2)}) copy-start(bf16[1024,128]{1,0:T(8,128)(2,1)} %w_last.5) | copy-start | bytes 786436
  9.8 1.0 copy-start.5
  10.8 1.4 copy-start.10
  12.1 1.4 copy-start.12
  13.5 0.7 copy-start.38
  14.2 0.7 copy-start.39
  14.8 24.5 %all-to-all-start = ((f32[64,8,128]{2,1,0:T(8,128)}), f32[64,8,128]{2,1,0:T(8,128)}, u32[]{:S(2)}, u32[]{:S(2)}) async-start(f32[64,8,128]{2,1,0:T(8,128)} %copy-done.38), calls=%async_computation | async-start | bytes 524288 | tf_op jit(solution)/shard_map/all_to_all | solution.py:406
  29.3 0.6 copy-start.32
  29.9 0.6 copy-start.35
  39.4 0.8 copy-start.33
  40.2 0.8 copy-start.36
  41.1 46.4 %copy-start.34 = (f32[128,128]{1,0:T(8,128)S(1)}, f32[128,128]{1,0:T(8,128)}, u32[]{:S(2)}) copy-start(f32[128,128]{1,0:T(8,128)} %copy-done.32) | copy-start | bytes 196612
  41.1 46.4 %copy-start.37 = (f32[128,128]{1,0:T(8,128)S(1)}, f32[128,128]{1,0:T(8,128)}, u32[]{:S(2)}) copy-start(f32[128,128]{1,0:T(8,128)} %copy-done.35) | copy-start | bytes 196612
  59.7 1.0 copy-start.23
  60.6 0.9 copy-start.40
  66.6 1.0 copy-start.14
  67.5 1.0 copy-start.16
  68.5 1.0 copy-start.18
  69.5 1.1 copy-start.20
  70.5 16.9 %copy-start.41 = (bf16[512,128]{1,0:T(8,128)(2,1)}, bf16[512,128]{1,0:T(8,128)(2,1)S(1)}, u32[]{:S(2)}) copy-start(bf16[512,128]{1,0:T(8,128)(2,1)S(1)} %get-tuple-element.45.x) | copy-start | bytes 393220
  70.5 16.9 %copy-start.43 = (bf16[512,128]{1,0:T(8,128)(2,1)}, bf16[512,128]{1,0:T(8,128)(2,1)S(1)}, u32[]{:S(2)}) copy-start(bf16[512,128]{1,0:T(8,128)(2,1)S(1)} %get-tuple-element.50.gt) | copy-start | bytes 393220
  88.1 0.7 copy-start.26
  88.8 17.9 %all-to-all-start.3 = ((f32[64,8,128]{2,1,0:T(8,128)}), f32[64,8,128]{2,1,0:T(8,128)}, u32[]{:S(2)}, u32[]{:S(2)}) async-start(f32[64,8,128]{2,1,0:T(8,128)} %copy-done.26), calls=%async_computation.3 | async-start | bytes 524288 | tf_op jit(solution)/shard_map/all_to_all | solution.py:410
  94.7 1.2 copy-start.15
  95.9 1.2 copy-start.17
  97.2 1.2 copy-start.19
  98.4 1.2 copy-start.21
  99.6 0.9 copy-start.42
  100.5 0.9 copy-start.44
  103.1 2.0 copy-start.2
  105.1 0.8 copy-start.27
  105.9 0.8 copy-start.29
  106.7 2.2 %copy-start.3 = (f32[2,512,1024]{2,1,0:T(8,128)S(1)}, f32[2,512,1024]{2,1,0:T(8,128)}, u32[]{:S(2)}) copy-start(f32[2,512,1024]{2,1,0:T(8,128)} %copy-done.2) | copy-start | bytes 12582916
  108.9 1.2 copy-start.6
  110.1 1.6 copy-start.13
  111.7 6.0 %copy-start.4 = (f32[2,512,1024]{2,1,0:T(8,128)S(1)}, f32[2,512,1024]{2,1,0:T(8,128)}, u32[]{:S(2)}) copy-start(f32[2,512,1024]{2,1,0:T(8,128)} %copy-done.2) | copy-start | bytes 12582916
  111.7 6.0 %copy-start.7 = (bf16[512,1024]{1,0:T(8,128)(2,1)S(1)}, bf16[512,1024]{1,0:T(8,128)(2,1)}, u32[]{:S(2)}) copy-start(bf16[512,1024]{1,0:T(8,128)(2,1)} %copy-done.5) | copy-start | bytes 3145732
  111.7 6.1 %copy-start.11 = (f32[512,1024]{1,0:T(8,128)S(1)}, f32[512,1024]{1,0:T(8,128)}, u32[]{:S(2)}) copy-start(f32[512,1024]{1,0:T(8,128)} %copy-done.10) | copy-start | bytes 6291460
  111.7 6.1 %copy-start.25 = (f32[1,2,256,128]{3,2,1,0:T(8,128)S(1)}, f32[1,2,256,128]{3,2,1,0:T(8,128)}, u32[]{:S(2)}) copy-start(f32[1,2,256,128]{3,2,1,0:T(8,128)} %param.5) | copy-start | bytes 786436
  111.8 6.1 %copy-start.28 = (f32[128,1024]{1,0:T(8,128)S(1)}, f32[128,1024]{1,0:T(8,128)}, u32[]{:S(2)}) copy-start(f32[128,1024]{1,0:T(8,128)} %copy-done.27) | copy-start | bytes 1572868
  111.8 6.1 %copy-start.30 = (f32[1024,128]{1,0:T(8,128)S(1)}, f32[1024,128]{1,0:T(8,128)}, u32[]{:S(2)}) copy-start(f32[1024,128]{1,0:T(8,128)} %copy-done.29) | copy-start | bytes 1572868
  114.5 8.0 %collective-permute-start = (f32[512,1024]{1,0:T(8,128)S(1)}, f32[512,1024]{1,0:T(8,128)S(1)}, u32[]{:S(2)}, u32[]{:S(2)}) collective-permute-start(f32[512,1024]{1,0:T(8,128)S(1)} %get-tuple-element.60), channel_id=1, source_target_pairs={{0,1},{1,0},{2,3},{3,2},{4,5},{5,4},{6,7},{7,6},{8,9},{9,8},{10,11... | collective-permute-start | bytes 6291464 | tf_op jit(solution)/shard_map/ppermute | solution.py:443
  120.2 2.4 %collective-permute-start.1 = (f32[128,1024]{1,0:T(8,128)S(1)}, f32[128,1024]{1,0:T(8,128)S(1)}, u32[]{:S(2)}, u32[]{:S(2)}) collective-permute-start(f32[128,1024]{1,0:T(8,128)S(1)} %get-tuple-element.61), channel_id=1, source_target_pairs={{0,1},{1,0},{2,3},{3,2},{4,5},{5,4},{6,7},{7,6},{8,9},{9,8},{10,11... | collective-permute-start | bytes 1572872 | tf_op jit(solution)/shard_map/ppermute | solution.py:453
  210.3 4.9 %collective-permute-start.2 = (f32[640,1024]{1,0:T(8,128)S(1)}, f32[640,1024]{1,0:T(8,128)S(1)}, u32[]{:S(2)}, u32[]{:S(2)}) collective-permute-start(f32[640,1024]{1,0:T(8,128)S(1)} %bitcast.7), channel_id=1, source_target_pairs={{0,1},{1,0},{2,3},{3,2},{4,5},{5,4},{6,7},{7,6},{8,9},{9,8},{10,11... | collective-permute-start | bytes 7864328 | tf_op jit(solution)/shard_map/ppermute | solution.py:466

commit v4 on v3

--- a/solution.py
+++ b/solution.py
@@ -53,7 +53,7 @@
     return lax.all_to_all(value, ALL, 0, 0, axis_index_groups=groups, tiled=True)
 
 
-def legendre_kernel(lat_count, wave_count, order_ref, forward_ref, backward_ref, table):
+def legendre(lat_count, wave_count, ids, forward_ref, backward_ref, table):
     bands = lat_count // 2
     place = lax.broadcasted_iota(jnp.int32, (1, lat_count), 1)
     lat_index = jnp.where(place >= bands, 2 * (place - bands) + 1, 2 * place).astype(jnp.float32)
@@ -61,7 +61,7 @@
     sine_lat = jnp.sin(latitude)
     cosine_lat = jnp.cos(latitude)
     quad_weight = cosine_lat * (math.pi / lat_count)
-    order_m = jnp.full((1, lat_count), order_ref[0], jnp.int32).astype(jnp.float32)
+    order_m = jnp.full((1, lat_count), ids[0], jnp.int32).astype(jnp.float32)
     counter = lax.broadcasted_iota(jnp.int32, (1, lat_count), 1).astype(jnp.float32) + 1.0
     increments = 0.5 * jnp.log((2.0 * counter + 1.0) / (2.0 * counter))
     summed = jnp.sum(jnp.where(counter <= order_m, increments, 0.0), axis=1, keepdims=True)
@@ -76,7 +76,7 @@
         previous, current, ratio_prev = current, following, ratio
         table[offset : offset + 1, :] = current
     degree = (
-        lax.broadcasted_iota(jnp.int32, (wave_count, lat_count), 0) + order_ref[0]
+        lax.broadcasted_iota(jnp.int32, (wave_count, lat_count), 0) + ids[0]
     ).astype(jnp.float32)
     kept = degree <= wave_count - 1
     poly = jnp.where(kept, table[...], 0.0)
@@ -92,19 +92,6 @@
     backward_ref[...] = jnp.dot(
         weighted.T, damping * poly, precision=highest, preferred_element_type=jnp.float32
     )
-
-
-def legendre(order, lat_count, wave_count):
-    square = jax.ShapeDtypeStruct((lat_count, lat_count), jnp.float32)
-    return pl.pallas_call(
-        functools.partial(legendre_kernel, lat_count, wave_count),
-        out_shape=(square, square),
-        in_specs=[pl.BlockSpec(memory_space=pltpu.SMEM)],
-        out_specs=(pl.BlockSpec(memory_space=pltpu.VMEM),) * 2,
-        scratch_shapes=[pltpu.VMEM((wave_count, lat_count), jnp.float32)],
-        name="legendre",
-        compiler_params=pltpu.CompilerParams(vmem_limit_bytes=2 * 1024 * 1024),
-    )(order)
 
 
 def vmem(count):
@@ -197,18 +184,23 @@
     s2_ref[at : at + size, :] = slope
 
 
-def first_kernel(
-    state, cotangent, w_first, w_middle, w_last,
-    waves, table, table_t, h1, s1, h2, s2,
-):
+def tables_kernel(ids, table, table_t, forward_op, backward_op, poly):
     table[...] = wave_table(False)
     table_t[...] = wave_table(True)
+    legendre(forward_op.shape[0], MW, ids, forward_op, backward_op, poly)
+
+
+def first_kernel(
+    state, cotangent, table, w_first, w_middle, w_last,
+    waves, x, h1, s1, h2, s2,
+):
     moved = []
     for j in range(2):
+        rows = slice(j * NLON, (j + 1) * NLON)
         field = state[j]
+        x[rows, :] = field.astype(jnp.bfloat16)
         physics(field.astype(jnp.bfloat16), w_first, w_middle, h1, s1, h2, s2, j * NLON)
-        tendency = mm(h2[j * NLON : (j + 1) * NLON, :], w_last[...])
-        moved.append(field + tend_weight * tendency)
+        moved.append(field + tend_weight * mm(h2[rows, :], w_last[...]))
     store_waves(table[...], moved + [cotangent[0], cotangent[1]], waves)
 
 
@@ -234,15 +226,8 @@
     store_waves(table[...], moved + grads, waves)
 
 
-def weights_kernel(x, h1, h2, ga1, ga2, gt, first, middle, last):
-    first[...] = mm_tn(x[...], ga1[...])
-    for h in range(2):
-        middle[h] = mm_tn(h1[h], ga2[...])
-    last[...] = mm_tn(h2[...], gt[...])
-
-
 def last_kernel(
-    core_ref, waves_in, table_t, h1, h2, s2, w_last, middle,
+    ids, waves_in, table_t, h1_0, s2, h1_1, ga2_1, w_last,
     final, send, ga2, gt,
 ):
     fields = load_fields(table_t[...], waves_in)
@@ -252,30 +237,33 @@
         scaled = (tend_weight * fields[2 + j]).astype(jnp.bfloat16)
         gt[rows, :] = scaled
         ga2[rows, :] = (mm_nt(scaled, w_last[...]) * s2[rows, :]).astype(jnp.bfloat16)
-    which = 1 - core_ref[0]
-    send[...] = middle[which] + mm_tn(h1[which], ga2[...])
-
-
-def rest_kernel(
-    core_ref, state, h1, h2, s1, ga2, gt, w_middle, first, middle, last,
-    keep, keep_thin, send_thin, ga1, first_sum, last_sum,
+    which = 1 - ids[1]
+    send[...] = mm_tn(h1_0[which], ga2[...]) + mm_tn(h1_1[which], ga2_1[...])
+
+
+def thin_kernel(
+    ids, x_0, h2_0, s1, ga2, gt_0, w_middle, x_1, h2_1, ga1_1, gt_1,
+    keep, send, ga1, first, last,
 ):
     for j in range(2):
         rows = slice(j * NLON, (j + 1) * NLON)
         back = mm_nt(ga2[rows, :], w_middle[...])
         ga1[rows, :] = (back * s1[rows, :]).astype(jnp.bfloat16)
-    rows = jnp.concatenate([state[0], state[1]], axis=0).astype(jnp.bfloat16)
-    first_sum[...] = first[...] + mm_tn(rows, ga1[...])
-    last_sum[...] = last[...] + mm_tn(h2[...], gt[...])
-    core = core_ref[0]
-    half = h1.shape[2]
-    part, blocks = half // 8, 8
-    for out, which in ((send_thin, 1 - core), (keep_thin, core)):
-        out[0:part, :] = first_sum[pl.ds(pl.multiple_of(which * part, part), part), :]
+    first[...] = mm_tn(x_0[...], ga1[...]) + mm_tn(x_1[...], ga1_1[...])
+    last[...] = mm_tn(h2_0[...], gt_0[...]) + mm_tn(h2_1[...], gt_1[...])
+    core = ids[1]
+    part, blocks = keep.shape[0] // 2, 8
+    half = part * blocks
+    for out, which in ((send, 1 - core), (keep, core)):
+        out[0:part, :] = first[pl.ds(pl.multiple_of(which * part, part), part), :]
         for b in range(blocks):
             at = pl.multiple_of(which * half + b * part, part)
-            out[part : 2 * part, b * 128 : (b + 1) * 128] = last_sum[pl.ds(at, part), :]
-    keep[...] = middle[core] + mm_tn(h1[core], ga2[...])
+            out[part : 2 * part, b * 128 : (b + 1) * 128] = last[pl.ds(at, part), :]
+
+
+def keep_kernel(ids, h1_0, ga2_0, h1_1, ga2_1, keep):
+    core = ids[1]
+    keep[...] = mm_tn(h1_0[core], ga2_0[...]) + mm_tn(h1_1[core], ga2_1[...])
 
 
 def latitudes_kernel(owned, forward_op, backward_op, back):
@@ -327,9 +315,9 @@
     out[half:, :] = left_thin[...] + right_thin[...]
 
 
-def place(core_ref, other, source, outs, sem):
+def place(ids, other, source, outs, sem):
     first, middle, last = outs
-    which = 1 - core_ref[0] if other else core_ref[0]
+    which = 1 - ids[1] if other else ids[1]
     half = middle.shape[0] // 2
     part, blocks = half // 8, 8
     copies = [
@@ -356,12 +344,12 @@
         copy.wait()
 
 
-def own_kernel(core_ref, source, first, middle, last, sem):
-    place(core_ref, False, source, (first, middle, last), sem)
-
-
-def other_kernel(core_ref, source, _first, _middle, _last, first, middle, last, sem):
-    place(core_ref, True, source, (first, middle, last), sem)
+def own_kernel(ids, source, first, middle, last, sem):
+    place(ids, False, source, (first, middle, last), sem)
+
+
+def other_kernel(ids, source, _first, _middle, _last, first, middle, last, sem):
+    place(ids, True, source, (first, middle, last), sem)
 
 
 def unpack(core, own, other, hidden, features):
@@ -393,14 +381,13 @@
     rows = lat_rows * lon_count
     bands = lax.axis_size("xl") * lax.axis_size("z") * lax.axis_size("y")
     f32, bf16 = jnp.float32, jnp.bfloat16
-    core = lax.axis_index("c").astype(jnp.int32).reshape(1)
-    order = lax.axis_index(LAT).astype(jnp.int32).reshape(1)
-    state, cotangent = state[0], cotangent[0]
-    weights = (w_first, w_middle, w_last)
+    ids = jnp.stack([lax.axis_index(LAT), lax.axis_index("c")]).astype(jnp.int32)
     waves_of = ((MW, 8, features), f32)
     halves = ((2, rows, hidden // 2), bf16)
     wide16, wide32 = ((rows, hidden), bf16), ((rows, hidden), f32)
     thin16 = ((rows, features), bf16)
+    part = ((lat_rows, lon_count, features), f32)
+    square = ((lat_rows * bands,) * 2, f32)
 
     def cross(waves):
         owned = lax.all_to_all(waves, LAT, 0, 0, tiled=True)
@@ -409,49 +396,53 @@
         )
         return lax.all_to_all(back, LAT, 0, 0, tiled=True)
 
-    forward_op, backward_op = legendre(order, lat_rows * bands, MW)
-    waves, table, table_t, h1_0, s1_0, h2_0, s2_0 = call(
+    table, table_t, forward_op, backward_op = call(
+        tables_kernel,
+        [((2 * MW, NLON), f32), ((NLON, 2 * MW), f32), square, square],
+        ids,
+        name="tables",
+        scalars=1,
+        scratch=[((MW, lat_rows * bands), f32)],
+    )
+    waves, x_0, h1_0, s1_0, h2_0, s2_0 = call(
         first_kernel,
-        [waves_of, ((2 * MW, NLON), f32), ((NLON, 2 * MW), f32), halves, wide32, wide16, wide32],
-        state, cotangent, *weights,
+        [waves_of, thin16, halves, wide32, wide16, wide32],
+        state[0], cotangent[0], table, w_first, w_middle, w_last,
         name="first",
     )
     waves = cross(waves)
-    waves, x, h1, h2, ga1, ga2, gt = call(
+    waves, x_1, h1_1, h2_1, ga1_1, ga2_1, gt_1 = call(
         middle_kernel,
         [waves_of, thin16, halves, wide16, wide16, wide16, thin16],
-        waves, table, table_t, *weights,
+        waves, table, table_t, w_first, w_middle, w_last,
         name="middle",
         scratch=[wide32] * 2,
     )
     waves = cross(waves)
-    first, middle, last = call(
-        weights_kernel,
-        [((features, hidden), f32), ((2, hidden // 2, hidden), f32), ((hidden, features), f32)],
-        x, h1, h2, ga1, ga2, gt,
-        name="weights",
-    )
     packed = ((hidden // 2 + features, hidden), f32)
     half32, thin32 = ((hidden // 2, hidden), f32), ((features, hidden), f32)
-    final, send, ga2, gt = call(
+    final, send, ga2_0, gt_0 = call(
         last_kernel,
-        [((lat_rows, lon_count, features), f32), half32, wide16, thin16],
-        core, waves, table_t, h1_0, h2_0, s2_0, w_last, middle,
+        [part, half32, wide16, thin16],
+        ids, waves, table_t, h1_0, s2_0, h1_1, ga2_1, w_last,
         name="last",
         scalars=1,
     )
     received = lax.ppermute(send, "c", SWAP)
-    keep, keep_thin, send_thin = call(
-        rest_kernel,
-        [half32, thin32, thin32],
-        core, state, h1_0, h2_0, s1_0, ga2, gt, w_middle, first, middle, last,
-        name="rest",
+    keep_thin, send_thin = call(
+        thin_kernel,
+        [thin32, thin32],
+        ids, x_0, h2_0, s1_0, ga2_0, gt_0, w_middle, x_1, h2_1, ga1_1, gt_1,
+        name="thin",
         scalars=1,
         scratch=[wide16, thin32, ((hidden, features), f32)],
     )
+    received_thin = lax.ppermute(send_thin, "c", SWAP)
+    (keep,) = call(
+        keep_kernel, [half32], ids, h1_0, ga2_0, h1_1, ga2_1, name="keep", scalars=1
+    )
     (held,) = call(
-        add_kernel, [packed], keep, keep_thin, received, lax.ppermute(send_thin, "c", SWAP),
-        name="add",
+        add_kernel, [packed], keep, keep_thin, received, received_thin, name="add"
     )
     wide, deep = len(WIDE[0]), len(DEEP[0])
     piece = packed[0][0] // wide
@@ -464,7 +455,7 @@
     (held,) = call(spread_kernel, [((wide, piece, hidden), f32)], held, name="spread")
     held = exchange(held, WIDE).reshape(packed[0])
     other = lax.ppermute(held, "c", SWAP)
-    first, middle, last = unpack(core, held, other, hidden, features)
+    first, middle, last = unpack(ids, held, other, hidden, features)
     return final[None], first, middle, last
 
 

time: 218 us -> 195 us (0.89)
  blocking collectives: 121 us -> 157 us
  local copies, waits for them, and re-layouts: 35.2 us -> 5.4 us
  starting transfers between devices: 24.3 us -> 5.3 us
  waiting for transfers between devices: 13.3 us -> 2.5 us
    unnamed x90 -> x16, local copies, waits for them, and re-layouts: 35.2 us -> 5.4 us
    all_to_all x1 -> x2, blocking collectives: 16.9 us -> 41.2 us  [cross(): owned = lax.all_to_all(waves, LAT, 0, 0, tiled=True)]
    all_to_all x2 -> x0, starting transfers between devices: 19.7 us -> none  [the longest x1 13.8 us: cross(): owned = lax.all_to_all(waves, LAT, 0, 0, tiled=True)]
    all_to_all x1 -> x2, blocking collectives: 17 us -> 33.2 us  [cross(): return lax.all_to_all(back, LAT, 0, 0, tiled=True)]
    all_to_all x2 -> x0, waiting for transfers between devices: 8.83 us -> none  [the longest x1 8.83 us: cross(): owned = lax.all_to_all(waves, LAT, 0, 0, tiled=True)]
    all_to_all x4, blocking collectives: 87.1 us -> 82.5 us  [exchange(): lax.all_to_all(value, ALL, 0, 0, axis_index_groups=groups, tiled=True)]
    pallas_call x11 -> x12, Pallas kernels: 18.4 us -> 19.2 us  [call(): pl.pallas_call(kernel, out_shape=tuple((jax.ShapeDtypeStruct(shape, dtype...]
  transfers between devices with their start and end apart: 5 -> 3, of which waited for: 3 -> 2; matrix products, arithmetic and copies ran while one was open for 0% -> 0% of each run, Pallas kernels for 3% -> 3%
where the time goes in v4:
time: 195 us; the launch traced here: 194 us
  blocking collectives  157 us (81%)
  Pallas kernels  23.4 us (12%)
  local copies, waits for them, and re-layouts  5.4 us (3%)
  starting transfers between devices  5.3 us (3%)
  waiting for transfers between devices  2.5 us (1%)
    all_to_all x4, blocking collectives, exchange(): lax.all_to_all(value, ALL, 0, 0, axis_index_groups=groups, tiled=True)  82.5 us
    all_to_all x2, blocking collectives, cross(): owned = lax.all_to_all(waves, LAT, 0, 0, tiled=True)  41.2 us
    all_to_all x2, blocking collectives, cross(): return lax.all_to_all(back, LAT, 0, 0, tiled=True)  33.2 us
    pallas_call x12, Pallas kernels, call(): pl.pallas_call(kernel, out_shape=tuple((jax.ShapeDtypeStruct(shape, dtype...  19.2 us
    unnamed x16, local copies, waits for them, and re-layouts  5.4 us
    ppermute x1, starting transfers between devices, body(): received = lax.ppermute(send, 'c', SWAP)  4.08 us
  transfers between devices with their start and end apart: 3, of which 2 were waited for; matrix products, arithmetic and copies ran while one was open for 0% of the time, Pallas kernels for 3%

profile of v4, /device:TPU:1, one launch (start us, length us, event | category | flops | bytes accessed | tf_op | source)
XLA Modules:
  0.0 194.4 jit_solution(5674188781877990803)
XLA Ops:
  0.6 0.1 pad_add_fusion.ids
  0.7 2.0 %tables.1 = (f32[128,256]{1,0:T(8,128)S(1)}, f32[256,128]{1,0:T(8,128)S(1)}, f32[128,128]{1,0:T(8,128)S(1)}, f32[128,128]{1,0:T(8,128)S(1)}) custom-call(s32[2]{0:T(128)S(1)} %pad_add_fusion.ids), custom_call_target="tpu_custom_call" | custom-call | tf_op jit(solution)/shard_map/tables/pallas_call | solution.py:108
  2.7 0.0 copy-start
  2.7 1.6 copy-done
  4.3 0.0 copy-start.2
  4.3 0.9 copy-done.2
  5.2 0.0 copy-start.4
  5.2 0.9 copy-done.4
  6.2 0.0 copy-start.6
  6.2 0.9 copy-done.6
  7.1 0.0 copy-start.7
  7.2 0.9 copy-done.7
  8.1 0.0 copy-start.1
  8.1 0.0 copy-start.3
  8.1 0.0 copy-start.5
  8.1 2.8 %first.1 = (f32[64,8,128]{2,1,0:T(8,128)S(1)}, bf16[512,128]{1,0:T(8,128)(2,1)S(1)}, bf16[2,512,512]{2,1,0:T(8,128)(2,1)S(1)}, f32[512,1024]{1,0:T(8,128)S(1)}, ...) custom-call(f32[2,256,128]{2,1,0:T(8,128)S(1)} %bitcast.10, f32[2,256,128]{2,1,0:T(8,128)S(1)} %bitcast.11, ...), custom_call_target="tpu_custom_call" | custom-call | tf_op jit(solution)/shard_map/first/pallas_call | solution.py:108
  10.9 24.2 %all_to_all.40.owned = f32[64,8,128]{2,1,0:T(8,128)S(1)} all-to-all(f32[64,8,128]{2,1,0:T(8,128)S(1)} %get-tuple-element.34), channel_id=1, replica_groups=mesh['xl'=2,'z'=8,'y'=4,'xh'=2,'c'=2] {'xl','z','y'}, dimensions={0} | all-to-all | bytes 524288 | tf_op jit(solution)/shard_map/all_to_all | solution.py:393
  35.1 0.6 latitudes.2
  35.8 17.0 %all_to_all.41.waves_in = f32[64,8,128]{2,1,0:T(8,128)S(1)} all-to-all(f32[64,8,128]{2,1,0:T(8,128)S(1)} %latitudes.2), channel_id=1, replica_groups=mesh['xl'=2,'z'=8,'y'=4,'xh'=2,'c'=2] {'xl','z','y'}, dimensions={0} | all-to-all | bytes 524288 | tf_op jit(solution)/shard_map/all_to_all | solution.py:397
  52.8 0.0 copy-done.1
  52.8 0.0 copy-done.3
  52.8 0.0 copy-done.5
  52.8 5.2 %middle.1 = (f32[64,8,128]{2,1,0:T(8,128)S(1)}, bf16[512,128]{1,0:T(8,128)(2,1)S(1)}, bf16[2,512,512]{2,1,0:T(8,128)(2,1)S(1)}, bf16[512,1024]{1,0:T(8,128)(2,1)...) custom-call(f32[64,8,128]{2,1,0:T(8,128)S(1)} %all_to_all.41.waves_in, ...), custom_call_target="tpu_custom_call" | custom-call | tf_op jit(solution)/shard_map/middle/pallas_call | solution.py:108
  57.9 16.9 %all_to_all.42.owned = f32[64,8,128]{2,1,0:T(8,128)S(1)} all-to-all(f32[64,8,128]{2,1,0:T(8,128)S(1)} %get-tuple-element.38), channel_id=1, replica_groups=mesh['xl'=2,'z'=8,'y'=4,'xh'=2,'c'=2] {'xl','z','y'}, dimensions={0} | all-to-all | bytes 524288 | tf_op jit(solution)/shard_map/all_to_all | solution.py:393
  74.9 0.6 latitudes.3
  75.5 16.2 %all_to_all.43.waves_in = f32[64,8,128]{2,1,0:T(8,128)S(1)} all-to-all(f32[64,8,128]{2,1,0:T(8,128)S(1)} %latitudes.3), channel_id=1, replica_groups=mesh['xl'=2,'z'=8,'y'=4,'xh'=2,'c'=2] {'xl','z','y'}, dimensions={0} | all-to-all | bytes 524288 | tf_op jit(solution)/shard_map/all_to_all | solution.py:397
  91.6 2.7 %last.1 = (f32[2,256,128]{2,1,0:T(8,128)}, f32[512,1024]{1,0:T(8,128)S(1)}, bf16[512,1024]{1,0:T(8,128)(2,1)S(1)}, bf16[512,128]{1,0:T(8,128)(2,1)S(1)}) custom-call(s32[2]{0:T(128)S(1)} %pad_add_fusion.ids, f32[64,8,128]{2,1,0:T(8,128)S(1)} %all_to_all.43.waves_in, f32[256,128]{1,0:T(8,128)S(1)} %get-tuple-element.37.table_t, ...), custom_call_target="tpu_custom_call" | custom-call | tf_op jit(solution)/shard_map/last/pallas_call | solution.py:108
  94.3 4.1 %collective-permute-start = (f32[512,1024]{1,0:T(8,128)S(1)}, f32[512,1024]{1,0:T(8,128)S(1)}, u32[]{:S(2)}, u32[]{:S(2)}) collective-permute-start(f32[512,1024]{1,0:T(8,128)S(1)} %get-tuple-element.54), channel_id=1, source_target_pairs={{0,1},{1,0},{2,3},{3,2},{4,5},{5,4},{6,7},{7,6},{8,9},{9,8},{10,11... | collective-permute-start | bytes 6291464 | tf_op jit(solution)/shard_map/ppermute | solution.py:431
  98.4 2.8 %thin.1 = (f32[128,1024]{1,0:T(8,128)S(1)}, f32[128,1024]{1,0:T(8,128)S(1)}) custom-call(s32[2]{0:T(128)S(1)} %pad_add_fusion.ids, bf16[512,128]{1,0:T(8,128)(2,1)S(1)} %get-tuple-element.45.x_0, bf16[512,1024]{1,0:T(8,128)(2,1)S(1)} %get-tuple-element.46.h2_0, f32[512,1024]{1,0:T(8,128)S(1)} %get-tuple-element.47.s1, ...), custom_call_target="tpu_custom_call" | custom-call | tf_op jit(solution)/shard_map/thin/pallas_call | solution.py:108
  101.2 0.1 collective-permute-start.1
  101.3 1.8 keep.1.left
  103.1 0.1 collective-permute-done.1.right_thin
  103.2 0.0 collective-permute-done.right
  103.2 0.4 add.11
  103.5 23.0 %all_to_all.44.parts = f32[8,80,1024]{2,1,0:T(8,128)S(1)} all-to-all(f32[8,80,1024]{2,1,0:T(8,128)S(1)} %bitcast.9), channel_id=1, replica_groups={{0,16,128,144,2,18,130,146},{32,48,160,176,34,50,162,178},{64,80,192,20..., dimensions={0} | all-to-all | bytes 5242880 | tf_op jit(solution)/shard_map/all_to_all | solution.py:53
  126.6 0.1 sum_wide.1
  126.7 19.5 %all_to_all.45.parts = f32[16,40,128]{2,1,0:T(8,128)S(1)} all-to-all(f32[16,40,128]{2,1,0:T(8,128)S(1)} %sum_wide.1), channel_id=1, replica_groups={{0,32,64,96,4,36,68,100,8,40,72,104,12,44,76,108},{16,48,80,112,20,52,8..., dimensions={0} | all-to-all | bytes 655360 | tf_op jit(solution)/shard_map/all_to_all | solution.py:53
  146.2 18.1 %all_to_all.46.parts = f32[16,40,128]{2,1,0:T(8,128)S(1)} all-to-all(f32[16,40,128]{2,1,0:T(8,128)S(1)} %sum_deep.1), channel_id=1, replica_groups={{0,32,64,96,4,36,68,100,8,40,72,104,12,44,76,108},{16,48,80,112,20,52,8..., dimensions={0} | all-to-all | bytes 655360 | tf_op jit(solution)/shard_map/all_to_all | solution.py:53
  164.3 0.3 spread.1
  164.6 21.9 %all_to_all.47 = f32[8,80,1024]{2,1,0:T(8,128)S(1)} all-to-all(f32[8,80,1024]{2,1,0:T(8,128)S(1)} %spread.1), channel_id=1, replica_groups={{0,16,128,144,2,18,130,146},{32,48,160,176,34,50,162,178},{64,80,192,20..., dimensions={0} | all-to-all | bytes 5242880 | tf_op jit(solution)/shard_map/all_to_all | solution.py:53
  186.5 1.1 collective-permute-start.2
  187.6 2.1 %own.1 = (f32[128,1024]{1,0:T(8,128)}, f32[1024,1024]{1,0:T(8,128)}, f32[1024,128]{1,0:T(8,128)}) custom-call(s32[2]{0:T(128)S(1)} %pad_add_fusion.ids, f32[640,1024]{1,0:T(8,128)S(1)} %bitcast.8), custom_call_target="tpu_custom_call" | custom-call | tf_op jit(solution)/shard_map/own/pallas_call | solution.py:368
  189.7 2.4 %collective-permute-done.2.source = f32[640,1024]{1,0:T(8,128)S(1)} collective-permute-done((f32[640,1024]{1,0:T(8,128)S(1)}, f32[640,1024]{1,0:T(8,128)S(1)}, u32[]{:S(2)}, u32[]{:S(2)}) %collective-permute-start.2) | collective-permute-done | bytes 2621472 | tf_op jit(solution)/shard_map/ppermute | solution.py:457
  192.2 2.1 %other.1 = (f32[128,1024]{1,0:T(8,128)}, f32[1024,1024]{1,0:T(8,128)}, f32[1024,128]{1,0:T(8,128)}) custom-call(s32[2]{0:T(128)S(1)} %pad_add_fusion.ids, f32[640,1024]{1,0:T(8,128)S(1)} %collective-permute-done.2.source, f32[128,1024]{1,0:T(8,128)} %get-tuple-element.56._first, ...), custom_call_target="tpu_custom_call", output_to_operand_aliasing={{0}: (2, {}), {1}: (3, {}), {2}: (4, {})} | custom-call | tf_op jit(solution)/shard_map/other/pallas_call | solution.py:369
  (1 shorter events, 0.0 us)
Async XLA Ops:
  2.7 1.6 copy-start
  4.3 0.9 copy-start.2
  5.2 0.9 copy-start.4
  6.2 0.9 copy-start.6
  7.1 0.9 copy-start.7
  8.1 44.7 %copy-start.1 = (bf16[1024,1024]{1,0:T(8,128)(2,1)S(1)}, bf16[1024,1024]{1,0:T(8,128)(2,1)}, u32[]{:S(2)}) copy-start(bf16[1024,1024]{1,0:T(8,128)(2,1)} %w_middle.5) | copy-start | bytes 6291460
  8.1 44.7 %copy-start.3 = (bf16[1024,128]{1,0:T(8,128)(2,1)S(1)}, bf16[1024,128]{1,0:T(8,128)(2,1)}, u32[]{:S(2)}) copy-start(bf16[1024,128]{1,0:T(8,128)(2,1)} %w_last.5) | copy-start | bytes 786436
  8.1 44.7 %copy-start.5 = (bf16[128,1024]{1,0:T(8,128)(2,1)S(1)}, bf16[128,1024]{1,0:T(8,128)(2,1)}, u32[]{:S(2)}) copy-start(bf16[128,1024]{1,0:T(8,128)(2,1)} %w_first.3) | copy-start | bytes 786436
  94.3 8.8 %collective-permute-start = (f32[512,1024]{1,0:T(8,128)S(1)}, f32[512,1024]{1,0:T(8,128)S(1)}, u32[]{:S(2)}, u32[]{:S(2)}) collective-permute-start(f32[512,1024]{1,0:T(8,128)S(1)} %get-tuple-element.54), channel_id=1, source_target_pairs={{0,1},{1,0},{2,3},{3,2},{4,5},{5,4},{6,7},{7,6},{8,9},{9,8},{10,11... | collective-permute-start | bytes 6291464 | tf_op jit(solution)/shard_map/ppermute | solution.py:431
  101.2 2.0 %collective-permute-start.1 = (f32[128,1024]{1,0:T(8,128)S(1)}, f32[128,1024]{1,0:T(8,128)S(1)}, u32[]{:S(2)}, u32[]{:S(2)}) collective-permute-start(f32[128,1024]{1,0:T(8,128)S(1)} %get-tuple-element.55), channel_id=1, source_target_pairs={{0,1},{1,0},{2,3},{3,2},{4,5},{5,4},{6,7},{7,6},{8,9},{9,8},{10,11... | collective-permute-start | bytes 1572872 | tf_op jit(solution)/shard_map/ppermute | solution.py:440
  186.5 5.7 %collective-permute-start.2 = (f32[640,1024]{1,0:T(8,128)S(1)}, f32[640,1024]{1,0:T(8,128)S(1)}, u32[]{:S(2)}, u32[]{:S(2)}) collective-permute-start(f32[640,1024]{1,0:T(8,128)S(1)} %bitcast.7), channel_id=1, source_target_pairs={{0,1},{1,0},{2,3},{3,2},{4,5},{5,4},{6,7},{7,6},{8,9},{9,8},{10,11... | collective-permute-start | bytes 7864328 | tf_op jit(solution)/shard_map/ppermute | solution.py:457

commit v5 on v4

--- a/solution.py
+++ b/solution.py
@@ -53,7 +53,7 @@
     return lax.all_to_all(value, ALL, 0, 0, axis_index_groups=groups, tiled=True)
 
 
-def legendre(lat_count, wave_count, ids, forward_ref, backward_ref, table):
+def legendre(lat_count, wave_count, order, forward_ref, backward_ref, table):
     bands = lat_count // 2
     place = lax.broadcasted_iota(jnp.int32, (1, lat_count), 1)
     lat_index = jnp.where(place >= bands, 2 * (place - bands) + 1, 2 * place).astype(jnp.float32)
@@ -61,7 +61,7 @@
     sine_lat = jnp.sin(latitude)
     cosine_lat = jnp.cos(latitude)
     quad_weight = cosine_lat * (math.pi / lat_count)
-    order_m = jnp.full((1, lat_count), ids[0], jnp.int32).astype(jnp.float32)
+    order_m = jnp.full((1, lat_count), order, jnp.int32).astype(jnp.float32)
     counter = lax.broadcasted_iota(jnp.int32, (1, lat_count), 1).astype(jnp.float32) + 1.0
     increments = 0.5 * jnp.log((2.0 * counter + 1.0) / (2.0 * counter))
     summed = jnp.sum(jnp.where(counter <= order_m, increments, 0.0), axis=1, keepdims=True)
@@ -76,7 +76,7 @@
         previous, current, ratio_prev = current, following, ratio
         table[offset : offset + 1, :] = current
     degree = (
-        lax.broadcasted_iota(jnp.int32, (wave_count, lat_count), 0) + ids[0]
+        lax.broadcasted_iota(jnp.int32, (wave_count, lat_count), 0) + order
     ).astype(jnp.float32)
     kept = degree <= wave_count - 1
     poly = jnp.where(kept, table[...], 0.0)
@@ -102,16 +102,20 @@
     return math.prod(shape) * jnp.dtype(dtype).itemsize
 
 
-def call(kernel, shapes, *operands, name, scalars=0, scratch=(), spare=4):
-    held = [(operand.shape, operand.dtype) for operand in operands[scalars:]]
+def call(kernel, shapes, *operands, name, scratch=(), fetched=0, spare=4):
+    here = len(operands) - fetched
+    held = [(operand.shape, operand.dtype) for operand in operands[:here]]
     held += list(shapes) + list(scratch)
+    operands = operands[:here] + tuple(
+        pltpu.with_memory_space_constraint(operand, pltpu.HBM) for operand in operands[here:]
+    )
     return pl.pallas_call(
         kernel,
         out_shape=tuple(jax.ShapeDtypeStruct(shape, dtype) for shape, dtype in shapes),
-        in_specs=[pl.BlockSpec(memory_space=pltpu.SMEM)] * scalars
-        + vmem(len(operands) - scalars),
+        in_specs=vmem(here) + [pl.BlockSpec(memory_space=pltpu.HBM)] * fetched,
         out_specs=tuple(vmem(len(shapes))),
-        scratch_shapes=[pltpu.VMEM(shape, dtype) for shape, dtype in scratch],
+        scratch_shapes=[pltpu.VMEM(shape, dtype) for shape, dtype in scratch]
+        + [pltpu.SemaphoreType.DMA((fetched,))] * bool(fetched),
         name=name,
         compiler_params=pltpu.CompilerParams(
             vmem_limit_bytes=sum(nbytes(*each) for each in held) + spare * 1024 * 1024
@@ -184,24 +188,38 @@
     s2_ref[at : at + size, :] = slope
 
 
-def tables_kernel(ids, table, table_t, forward_op, backward_op, poly):
+def first_kernel(
+    state_hbm, cotangent_hbm, w_first_hbm, w_middle_hbm, w_last_hbm,
+    waves, x, w_first, w_middle, w_last, table, table_t, forward_op, backward_op, h1, s1, h2, s2,
+    state, cotangent, poly, sem,
+):
+    copies = [
+        pltpu.make_async_copy(start, end, sem.at[i])
+        for i, (start, end) in enumerate(
+            (
+                (state_hbm, state),
+                (cotangent_hbm, cotangent),
+                (w_first_hbm, w_first),
+                (w_middle_hbm, w_middle),
+                (w_last_hbm, w_last),
+            )
+        )
+    ]
+    for copy in copies:
+        copy.start()
     table[...] = wave_table(False)
     table_t[...] = wave_table(True)
-    legendre(forward_op.shape[0], MW, ids, forward_op, backward_op, poly)
-
-
-def first_kernel(
-    state, cotangent, table, w_first, w_middle, w_last,
-    waves, x, h1, s1, h2, s2,
-):
+    legendre(forward_op.shape[0], MW, lax.axis_index(LAT), forward_op, backward_op, poly)
+    for copy in copies:
+        copy.wait()
     moved = []
     for j in range(2):
         rows = slice(j * NLON, (j + 1) * NLON)
-        field = state[j]
+        field = state[0, j]
         x[rows, :] = field.astype(jnp.bfloat16)
         physics(field.astype(jnp.bfloat16), w_first, w_middle, h1, s1, h2, s2, j * NLON)
         moved.append(field + tend_weight * mm(h2[rows, :], w_last[...]))
-    store_waves(table[...], moved + [cotangent[0], cotangent[1]], waves)
+    store_waves(table[...], moved + [cotangent[0, 0], cotangent[0, 1]], waves)
 
 
 def middle_kernel(
@@ -227,7 +245,7 @@
 
 
 def last_kernel(
-    ids, waves_in, table_t, h1_0, s2, h1_1, ga2_1, w_last,
+    waves_in, table_t, h1_0, s2, h1_1, ga2_1, w_last,
     final, send, ga2, gt,
 ):
     fields = load_fields(table_t[...], waves_in)
@@ -237,12 +255,12 @@
         scaled = (tend_weight * fields[2 + j]).astype(jnp.bfloat16)
         gt[rows, :] = scaled
         ga2[rows, :] = (mm_nt(scaled, w_last[...]) * s2[rows, :]).astype(jnp.bfloat16)
-    which = 1 - ids[1]
+    which = 1 - lax.axis_index("c")
     send[...] = mm_tn(h1_0[which], ga2[...]) + mm_tn(h1_1[which], ga2_1[...])
 
 
 def thin_kernel(
-    ids, x_0, h2_0, s1, ga2, gt_0, w_middle, x_1, h2_1, ga1_1, gt_1,
+    x_0, h2_0, s1, ga2, gt_0, w_middle, x_1, h2_1, ga1_1, gt_1,
     keep, send, ga1, first, last,
 ):
     for j in range(2):
@@ -251,7 +269,7 @@
         ga1[rows, :] = (back * s1[rows, :]).astype(jnp.bfloat16)
     first[...] = mm_tn(x_0[...], ga1[...]) + mm_tn(x_1[...], ga1_1[...])
     last[...] = mm_tn(h2_0[...], gt_0[...]) + mm_tn(h2_1[...], gt_1[...])
-    core = ids[1]
+    core = lax.axis_index("c")
     part, blocks = keep.shape[0] // 2, 8
     half = part * blocks
     for out, which in ((send, 1 - core), (keep, core)):
@@ -261,8 +279,8 @@
             out[part : 2 * part, b * 128 : (b + 1) * 128] = last[pl.ds(at, part), :]
 
 
-def keep_kernel(ids, h1_0, ga2_0, h1_1, ga2_1, keep):
-    core = ids[1]
+def keep_kernel(h1_0, ga2_0, h1_1, ga2_1, keep):
+    core = lax.axis_index("c")
     keep[...] = mm_tn(h1_0[core], ga2_0[...]) + mm_tn(h1_1[core], ga2_1[...])
 
 
@@ -315,9 +333,10 @@
     out[half:, :] = left_thin[...] + right_thin[...]
 
 
-def place(ids, other, source, outs, sem):
+def place(other, source, outs, sem):
     first, middle, last = outs
-    which = 1 - ids[1] if other else ids[1]
+    core = lax.axis_index("c")
+    which = 1 - core if other else core
     half = middle.shape[0] // 2
     part, blocks = half // 8, 8
     copies = [
@@ -344,20 +363,19 @@
         copy.wait()
 
 
-def own_kernel(ids, source, first, middle, last, sem):
-    place(ids, False, source, (first, middle, last), sem)
-
-
-def other_kernel(ids, source, _first, _middle, _last, first, middle, last, sem):
-    place(ids, True, source, (first, middle, last), sem)
-
-
-def unpack(core, own, other, hidden, features):
+def own_kernel(source, first, middle, last, sem):
+    place(False, source, (first, middle, last), sem)
+
+
+def other_kernel(source, _first, _middle, _last, first, middle, last, sem):
+    place(True, source, (first, middle, last), sem)
+
+
+def unpack(own, other, hidden, features):
     outs = [
         jax.ShapeDtypeStruct(shape, jnp.float32)
         for shape in ((features, hidden), (hidden, hidden), (hidden, features))
     ]
-    smem = pl.BlockSpec(memory_space=pltpu.SMEM)
     hbm = pl.BlockSpec(memory_space=pltpu.HBM)
     settings = dict(
         out_shape=tuple(outs),
@@ -365,14 +383,14 @@
         scratch_shapes=[pltpu.SemaphoreType.DMA((10,))],
         compiler_params=pltpu.CompilerParams(vmem_limit_bytes=4 * 1024 * 1024),
     )
-    grads = pl.pallas_call(own_kernel, in_specs=[smem] + vmem(1), name="own", **settings)(core, own)
+    grads = pl.pallas_call(own_kernel, in_specs=vmem(1), name="own", **settings)(own)
     return pl.pallas_call(
         other_kernel,
-        in_specs=[smem] + vmem(1) + [hbm] * 3,
-        input_output_aliases={2: 0, 3: 1, 4: 2},
+        in_specs=vmem(1) + [hbm] * 3,
+        input_output_aliases={1: 0, 2: 1, 3: 2},
         name="other",
         **settings,
-    )(core, other, *grads)
+    )(other, *grads)
 
 
 def body(state, cotangent, w_first, w_middle, w_last):
@@ -381,7 +399,6 @@
     rows = lat_rows * lon_count
     bands = lax.axis_size("xl") * lax.axis_size("z") * lax.axis_size("y")
     f32, bf16 = jnp.float32, jnp.bfloat16
-    ids = jnp.stack([lax.axis_index(LAT), lax.axis_index("c")]).astype(jnp.int32)
     waves_of = ((MW, 8, features), f32)
     halves = ((2, rows, hidden // 2), bf16)
     wide16, wide32 = ((rows, hidden), bf16), ((rows, hidden), f32)
@@ -396,19 +413,21 @@
         )
         return lax.all_to_all(back, LAT, 0, 0, tiled=True)
 
-    table, table_t, forward_op, backward_op = call(
-        tables_kernel,
-        [((2 * MW, NLON), f32), ((NLON, 2 * MW), f32), square, square],
-        ids,
-        name="tables",
-        scalars=1,
-        scratch=[((MW, lat_rows * bands), f32)],
-    )
-    waves, x_0, h1_0, s1_0, h2_0, s2_0 = call(
+    (
+        waves, x_0, w_first, w_middle, w_last, table, table_t, forward_op, backward_op,
+        h1_0, s1_0, h2_0, s2_0,
+    ) = call(
         first_kernel,
-        [waves_of, thin16, halves, wide32, wide16, wide32],
-        state[0], cotangent[0], table, w_first, w_middle, w_last,
+        [
+            waves_of, thin16,
+            (w_first.shape, bf16), (w_middle.shape, bf16), (w_last.shape, bf16),
+            ((2 * MW, NLON), f32), ((NLON, 2 * MW), f32), square, square,
+            halves, wide32, wide16, wide32,
+        ],
+        state, cotangent, w_first, w_middle, w_last,
         name="first",
+        fetched=5,
+        scratch=[(state.shape, f32), (state.shape, f32), ((MW, lat_rows * bands), f32)],
     )
     waves = cross(waves)
     waves, x_1, h1_1, h2_1, ga1_1, ga2_1, gt_1 = call(
@@ -424,22 +443,20 @@
     final, send, ga2_0, gt_0 = call(
         last_kernel,
         [part, half32, wide16, thin16],
-        ids, waves, table_t, h1_0, s2_0, h1_1, ga2_1, w_last,
+        waves, table_t, h1_0, s2_0, h1_1, ga2_1, w_last,
         name="last",
-        scalars=1,
     )
     received = lax.ppermute(send, "c", SWAP)
     keep_thin, send_thin = call(
         thin_kernel,
         [thin32, thin32],
-        ids, x_0, h2_0, s1_0, ga2_0, gt_0, w_middle, x_1, h2_1, ga1_1, gt_1,
+        x_0, h2_0, s1_0, ga2_0, gt_0, w_middle, x_1, h2_1, ga1_1, gt_1,
         name="thin",
-        scalars=1,
         scratch=[wide16, thin32, ((hidden, features), f32)],
     )
     received_thin = lax.ppermute(send_thin, "c", SWAP)
     (keep,) = call(
-        keep_kernel, [half32], ids, h1_0, ga2_0, h1_1, ga2_1, name="keep", scalars=1
+        keep_kernel, [half32], h1_0, ga2_0, h1_1, ga2_1, name="keep"
     )
     (held,) = call(
         add_kernel, [packed], keep, keep_thin, received, received_thin, name="add"
@@ -455,7 +472,7 @@
     (held,) = call(spread_kernel, [((wide, piece, hidden), f32)], held, name="spread")
     held = exchange(held, WIDE).reshape(packed[0])
     other = lax.ppermute(held, "c", SWAP)
-    first, middle, last = unpack(ids, held, other, hidden, features)
+    first, middle, last = unpack(held, other, hidden, features)
     return final[None], first, middle, last
 
 

time: 195 us -> 189 us (0.969)
  local copies, waits for them, and re-layouts: 5.4 us -> 0 us
    unnamed x16 -> x0, local copies, waits for them, and re-layouts: 5.4 us -> none
    pallas_call x12 -> x11, Pallas kernels: 19.2 us -> 18.5 us  [call(): pl.pallas_call(kernel, out_shape=tuple((jax.ShapeDtypeStruct(shape, dtype...]
where the time goes in v5:
time: 189 us; the launch traced here: 188 us
  blocking collectives  156 us (83%)
  Pallas kernels  21.6 us (11%)
  starting transfers between devices  6.13 us (3%)
  waiting for transfers between devices  3.82 us (2%)
    all_to_all x4, blocking collectives, exchange(): lax.all_to_all(value, ALL, 0, 0, axis_index_groups=groups, tiled=True)  81.6 us
    all_to_all x2, blocking collectives, cross(): owned = lax.all_to_all(waves, LAT, 0, 0, tiled=True)  41.1 us
    all_to_all x2, blocking collectives, cross(): return lax.all_to_all(back, LAT, 0, 0, tiled=True)  33.2 us
    pallas_call x11, Pallas kernels, call(): pl.pallas_call(kernel, out_shape=tuple((jax.ShapeDtypeStruct(shape, dtype...  18.5 us
    ppermute x1, starting transfers between devices, body(): received = lax.ppermute(send, 'c', SWAP)  4.06 us
  transfers between devices with their start and end apart: 3, of which 2 were waited for; matrix products, arithmetic and copies ran while one was open for 0% of the time, Pallas kernels for 3%

profile of v5, /device:TPU:1, one launch (start us, length us, event | category | flops | bytes accessed | tf_op | source)
XLA Modules:
  0.0 188.4 jit_solution(5385388262556560867)
XLA Ops:
  0.6 5.8 %first.1 = (f32[64,8,128]{2,1,0:T(8,128)S(1)}, bf16[512,128]{1,0:T(8,128)(2,1)S(1)}, bf16[128,1024]{1,0:T(8,128)(2,1)S(1)}, bf16[1024,1024]{1,0:T(8,128)(2,1)S(1...) custom-call(f32[1,2,256,128]{3,2,1,0:T(8,128)} %state_hbm.1, ...), custom_call_target="tpu_custom_call" | custom-call | tf_op jit(solution)/shard_map/first/pallas_call | solution.py:112
  6.5 24.2 %all_to_all.40.owned = f32[64,8,128]{2,1,0:T(8,128)S(1)} all-to-all(f32[64,8,128]{2,1,0:T(8,128)S(1)} %get-tuple-element.36), channel_id=1, replica_groups=mesh['xl'=2,'z'=8,'y'=4,'xh'=2,'c'=2] {'xl','z','y'}, dimensions={0} | all-to-all | bytes 524288 | tf_op jit(solution)/shard_map/all_to_all | solution.py:410
  30.7 0.6 latitudes.2
  31.3 17.0 %all_to_all.41.waves_in = f32[64,8,128]{2,1,0:T(8,128)S(1)} all-to-all(f32[64,8,128]{2,1,0:T(8,128)S(1)} %latitudes.2), channel_id=1, replica_groups=mesh['xl'=2,'z'=8,'y'=4,'xh'=2,'c'=2] {'xl','z','y'}, dimensions={0} | all-to-all | bytes 524288 | tf_op jit(solution)/shard_map/all_to_all | solution.py:414
  48.3 5.0 %middle.1 = (f32[64,8,128]{2,1,0:T(8,128)S(1)}, bf16[512,128]{1,0:T(8,128)(2,1)S(1)}, bf16[2,512,512]{2,1,0:T(8,128)(2,1)S(1)}, bf16[512,1024]{1,0:T(8,128)(2,1)...) custom-call(f32[64,8,128]{2,1,0:T(8,128)S(1)} %all_to_all.41.waves_in, ...), custom_call_target="tpu_custom_call" | custom-call | tf_op jit(solution)/shard_map/middle/pallas_call | solution.py:112
  53.3 16.9 %all_to_all.42.owned = f32[64,8,128]{2,1,0:T(8,128)S(1)} all-to-all(f32[64,8,128]{2,1,0:T(8,128)S(1)} %get-tuple-element.44), channel_id=1, replica_groups=mesh['xl'=2,'z'=8,'y'=4,'xh'=2,'c'=2] {'xl','z','y'}, dimensions={0} | all-to-all | bytes 524288 | tf_op jit(solution)/shard_map/all_to_all | solution.py:410
  70.3 0.6 latitudes.3
  70.9 16.2 %all_to_all.43.waves_in = f32[64,8,128]{2,1,0:T(8,128)S(1)} all-to-all(f32[64,8,128]{2,1,0:T(8,128)S(1)} %latitudes.3), channel_id=1, replica_groups=mesh['xl'=2,'z'=8,'y'=4,'xh'=2,'c'=2] {'xl','z','y'}, dimensions={0} | all-to-all | bytes 524288 | tf_op jit(solution)/shard_map/all_to_all | solution.py:414
  87.1 2.1 %last.1 = (f32[2,256,128]{2,1,0:T(8,128)}, f32[512,1024]{1,0:T(8,128)S(1)}, bf16[512,1024]{1,0:T(8,128)(2,1)S(1)}, bf16[512,128]{1,0:T(8,128)(2,1)S(1)}) custom-call(f32[64,8,128]{2,1,0:T(8,128)S(1)} %all_to_all.43.waves_in, f32[256,128]{1,0:T(8,128)S(1)} %get-tuple-element.40.table_t, bf16[2,512,512]{2,1,0:T(8,128)(2,1)S(1)} %get-tuple-element.45.h1_0, ...), custom_call_target="tpu_custom_call" | custom-call | tf_op jit(solution)/shard_map/last/pallas_call | solution.py:112
  89.2 4.1 %collective-permute-start = (f32[512,1024]{1,0:T(8,128)S(1)}, f32[512,1024]{1,0:T(8,128)S(1)}, u32[]{:S(2)}, u32[]{:S(2)}) collective-permute-start(f32[512,1024]{1,0:T(8,128)S(1)} %get-tuple-element.60), channel_id=1, source_target_pairs={{0,1},{1,0},{2,3},{3,2},{4,5},{5,4},{6,7},{7,6},{8,9},{9,8},{10,11... | collective-permute-start | bytes 6291464 | tf_op jit(solution)/shard_map/ppermute | solution.py:449
  93.3 2.3 %thin.1 = (f32[128,1024]{1,0:T(8,128)S(1)}, f32[128,1024]{1,0:T(8,128)S(1)}) custom-call(bf16[512,128]{1,0:T(8,128)(2,1)S(1)} %get-tuple-element.51.x_0, bf16[512,1024]{1,0:T(8,128)(2,1)S(1)} %get-tuple-element.52.h2_0, f32[512,1024]{1,0:T(8,128)S(1)} %get-tuple-element.53.s1, bf16[512,1024]{1,0:T(8,128)(2,1)S(1)} %get-tuple-element.50.ga2_0.ga2, ...), custom_call_target="tpu_custom_call" | custom-call | tf_op jit(solution)/shard_map/thin/pallas_call | solution.py:112
  95.6 0.1 collective-permute-start.1
  95.7 1.3 keep.1.left
  97.0 0.8 collective-permute-done.1.right_thin
  97.8 0.0 collective-permute-done.right
  97.8 0.3 add.1
  98.1 23.1 %all_to_all.44.parts = f32[8,80,1024]{2,1,0:T(8,128)S(1)} all-to-all(f32[8,80,1024]{2,1,0:T(8,128)S(1)} %bitcast.5), channel_id=1, replica_groups={{0,16,128,144,2,18,130,146},{32,48,160,176,34,50,162,178},{64,80,192,20..., dimensions={0} | all-to-all | bytes 5242880 | tf_op jit(solution)/shard_map/all_to_all | solution.py:53
  121.1 0.1 sum_wide.1
  121.3 19.4 %all_to_all.45.parts = f32[16,40,128]{2,1,0:T(8,128)S(1)} all-to-all(f32[16,40,128]{2,1,0:T(8,128)S(1)} %sum_wide.1), channel_id=1, replica_groups={{0,32,64,96,4,36,68,100,8,40,72,104,12,44,76,108},{16,48,80,112,20,52,8..., dimensions={0} | all-to-all | bytes 655360 | tf_op jit(solution)/shard_map/all_to_all | solution.py:53
  140.7 17.2 %all_to_all.46.parts = f32[16,40,128]{2,1,0:T(8,128)S(1)} all-to-all(f32[16,40,128]{2,1,0:T(8,128)S(1)} %sum_deep.1), channel_id=1, replica_groups={{0,32,64,96,4,36,68,100,8,40,72,104,12,44,76,108},{16,48,80,112,20,52,8..., dimensions={0} | all-to-all | bytes 655360 | tf_op jit(solution)/shard_map/all_to_all | solution.py:53
  157.9 0.3 spread.1
  158.2 21.9 %all_to_all.47 = f32[8,80,1024]{2,1,0:T(8,128)S(1)} all-to-all(f32[8,80,1024]{2,1,0:T(8,128)S(1)} %spread.1), channel_id=1, replica_groups={{0,16,128,144,2,18,130,146},{32,48,160,176,34,50,162,178},{64,80,192,20..., dimensions={0} | all-to-all | bytes 5242880 | tf_op jit(solution)/shard_map/all_to_all | solution.py:53
  180.2 2.0 %collective-permute-start.2 = (f32[640,1024]{1,0:T(8,128)S(1)}, f32[640,1024]{1,0:T(8,128)S(1)}, u32[]{:S(2)}, u32[]{:S(2)}) collective-permute-start(f32[640,1024]{1,0:T(8,128)S(1)} %bitcast.3), channel_id=1, source_target_pairs={{0,1},{1,0},{2,3},{3,2},{4,5},{5,4},{6,7},{7,6},{8,9},{9,8},{10,11... | collective-permute-start | bytes 7864328 | tf_op jit(solution)/shard_map/ppermute | solution.py:474
  182.1 1.6 own.1
  183.7 3.0 %collective-permute-done.2.source = f32[640,1024]{1,0:T(8,128)S(1)} collective-permute-done((f32[640,1024]{1,0:T(8,128)S(1)}, f32[640,1024]{1,0:T(8,128)S(1)}, u32[]{:S(2)}, u32[]{:S(2)}) %collective-permute-start.2) | collective-permute-done | bytes 2621472 | tf_op jit(solution)/shard_map/ppermute | solution.py:474
  186.7 1.6 other.1
  (1 shorter events, 0.0 us)
Async XLA Ops:
  89.2 8.6 %collective-permute-start = (f32[512,1024]{1,0:T(8,128)S(1)}, f32[512,1024]{1,0:T(8,128)S(1)}, u32[]{:S(2)}, u32[]{:S(2)}) collective-permute-start(f32[512,1024]{1,0:T(8,128)S(1)} %get-tuple-element.60), channel_id=1, source_target_pairs={{0,1},{1,0},{2,3},{3,2},{4,5},{5,4},{6,7},{7,6},{8,9},{9,8},{10,11... | collective-permute-start | bytes 6291464 | tf_op jit(solution)/shard_map/ppermute | solution.py:449
  95.6 2.2 %collective-permute-start.1 = (f32[128,1024]{1,0:T(8,128)S(1)}, f32[128,1024]{1,0:T(8,128)S(1)}, u32[]{:S(2)}, u32[]{:S(2)}) collective-permute-start(f32[128,1024]{1,0:T(8,128)S(1)} %get-tuple-element.61), channel_id=1, source_target_pairs={{0,1},{1,0},{2,3},{3,2},{4,5},{5,4},{6,7},{7,6},{8,9},{9,8},{10,11... | collective-permute-start | bytes 1572872 | tf_op jit(solution)/shard_map/ppermute | solution.py:457
  180.2 6.5 %collective-permute-start.2 = (f32[640,1024]{1,0:T(8,128)S(1)}, f32[640,1024]{1,0:T(8,128)S(1)}, u32[]{:S(2)}, u32[]{:S(2)}) collective-permute-start(f32[640,1024]{1,0:T(8,128)S(1)} %bitcast.3), channel_id=1, source_target_pairs={{0,1},{1,0},{2,3},{3,2},{4,5},{5,4},{6,7},{7,6},{8,9},{9,8},{10,11... | collective-permute-start | bytes 7864328 | tf_op jit(solution)/shard_map/ppermute | solution.py:474

commit v6 on v5

--- a/solution.py
+++ b/solution.py
@@ -115,7 +115,7 @@
         in_specs=vmem(here) + [pl.BlockSpec(memory_space=pltpu.HBM)] * fetched,
         out_specs=tuple(vmem(len(shapes))),
         scratch_shapes=[pltpu.VMEM(shape, dtype) for shape, dtype in scratch]
-        + [pltpu.SemaphoreType.DMA((fetched,))] * bool(fetched),
+        + [pltpu.SemaphoreType.DMA((fetched + 3,))] * bool(fetched),
         name=name,
         compiler_params=pltpu.CompilerParams(
             vmem_limit_bytes=sum(nbytes(*each) for each in held) + spare * 1024 * 1024
@@ -193,17 +193,16 @@
     waves, x, w_first, w_middle, w_last, table, table_t, forward_op, backward_op, h1, s1, h2, s2,
     state, cotangent, poly, sem,
 ):
+    piece = w_middle.shape[0] // 4
+    parts = [pl.ds(i * piece, piece) for i in range(4)]
+    pairs = [(w_middle_hbm.at[part], w_middle.at[part]) for part in parts] + [
+        (state_hbm, state),
+        (w_first_hbm, w_first),
+        (w_last_hbm, w_last),
+        (cotangent_hbm, cotangent),
+    ]
     copies = [
-        pltpu.make_async_copy(start, end, sem.at[i])
-        for i, (start, end) in enumerate(
-            (
-                (state_hbm, state),
-                (cotangent_hbm, cotangent),
-                (w_first_hbm, w_first),
-                (w_middle_hbm, w_middle),
-                (w_last_hbm, w_last),
-            )
-        )
+        pltpu.make_async_copy(start, end, sem.at[i]) for i, (start, end) in enumerate(pairs)
     ]
     for copy in copies:
         copy.start()
@@ -212,14 +211,13 @@
     legendre(forward_op.shape[0], MW, lax.axis_index(LAT), forward_op, backward_op, poly)
     for copy in copies:
         copy.wait()
-    moved = []
-    for j in range(2):
-        rows = slice(j * NLON, (j + 1) * NLON)
-        field = state[0, j]
-        x[rows, :] = field.astype(jnp.bfloat16)
-        physics(field.astype(jnp.bfloat16), w_first, w_middle, h1, s1, h2, s2, j * NLON)
-        moved.append(field + tend_weight * mm(h2[rows, :], w_last[...]))
-    store_waves(table[...], moved + [cotangent[0, 0], cotangent[0, 1]], waves)
+    field = jnp.concatenate([state[0, 0], state[0, 1]], axis=0)
+    x[...] = field.astype(jnp.bfloat16)
+    physics(x[...], w_first, w_middle, h1, s1, h2, s2, 0)
+    moved = field + tend_weight * mm(h2[...], w_last[...])
+    store_waves(
+        table[...], [moved[:NLON], moved[NLON:], cotangent[0, 0], cotangent[0, 1]], waves
+    )
 
 
 def middle_kernel(
@@ -227,21 +225,16 @@
     waves, x, h1, h2, ga1, ga2, gt, s1, s2,
 ):
     fields = load_fields(table_t[...], waves_in)
-    moved, grads = [], []
-    for j in range(2):
-        rows = slice(j * NLON, (j + 1) * NLON)
-        field, pulled = fields[j], fields[2 + j]
-        x[rows, :] = field.astype(jnp.bfloat16)
-        physics(field.astype(jnp.bfloat16), w_first, w_middle, h1, s1, h2, s2, j * NLON)
-        moved.append(field + tend_weight * mm(h2[rows, :], w_last[...]))
-        scaled = (tend_weight * pulled).astype(jnp.bfloat16)
-        gt[rows, :] = scaled
-        back = (mm_nt(scaled, w_last[...]) * s2[rows, :]).astype(jnp.bfloat16)
-        ga2[rows, :] = back
-        back = (mm_nt(back, w_middle[...]) * s1[rows, :]).astype(jnp.bfloat16)
-        ga1[rows, :] = back
-        grads.append(pulled + mm_nt(back, w_first[...]))
-    store_waves(table[...], moved + grads, waves)
+    field = jnp.concatenate(fields[:2], axis=0)
+    pulled = jnp.concatenate(fields[2:], axis=0)
+    x[...] = field.astype(jnp.bfloat16)
+    gt[...] = (tend_weight * pulled).astype(jnp.bfloat16)
+    physics(x[...], w_first, w_middle, h1, s1, h2, s2, 0)
+    moved = field + tend_weight * mm(h2[...], w_last[...])
+    ga2[...] = (mm_nt(gt[...], w_last[...]) * s2[...]).astype(jnp.bfloat16)
+    ga1[...] = (mm_nt(ga2[...], w_middle[...]) * s1[...]).astype(jnp.bfloat16)
+    grad = pulled + mm_nt(ga1[...], w_first[...])
+    store_waves(table[...], [moved[:NLON], moved[NLON:], grad[:NLON], grad[NLON:]], waves)
 
 
 def last_kernel(
@@ -250,11 +243,9 @@
 ):
     fields = load_fields(table_t[...], waves_in)
     for j in range(2):
-        rows = slice(j * NLON, (j + 1) * NLON)
         final[j] = fields[j]
-        scaled = (tend_weight * fields[2 + j]).astype(jnp.bfloat16)
-        gt[rows, :] = scaled
-        ga2[rows, :] = (mm_nt(scaled, w_last[...]) * s2[rows, :]).astype(jnp.bfloat16)
+        gt[j * NLON : (j + 1) * NLON, :] = (tend_weight * fields[2 + j]).astype(jnp.bfloat16)
+    ga2[...] = (mm_nt(gt[...], w_last[...]) * s2[...]).astype(jnp.bfloat16)
     which = 1 - lax.axis_index("c")
     send[...] = mm_tn(h1_0[which], ga2[...]) + mm_tn(h1_1[which], ga2_1[...])
 
@@ -263,10 +254,7 @@
     x_0, h2_0, s1, ga2, gt_0, w_middle, x_1, h2_1, ga1_1, gt_1,
     keep, send, ga1, first, last,
 ):
-    for j in range(2):
-        rows = slice(j * NLON, (j + 1) * NLON)
-        back = mm_nt(ga2[rows, :], w_middle[...])
-        ga1[rows, :] = (back * s1[rows, :]).astype(jnp.bfloat16)
+    ga1[...] = (mm_nt(ga2[...], w_middle[...]) * s1[...]).astype(jnp.bfloat16)
     first[...] = mm_tn(x_0[...], ga1[...]) + mm_tn(x_1[...], ga1_1[...])
     last[...] = mm_tn(h2_0[...], gt_0[...]) + mm_tn(h2_1[...], gt_1[...])
     core = lax.axis_index("c")

time: 189 us -> 187 us (0.989)
  no operation moved by 1% of the time
where the time goes in v6:
time: 187 us
  blocking collectives  156 us (83%)
  Pallas kernels  20.1 us (11%)
  starting transfers between devices  6.12 us (3%)
  waiting for transfers between devices  3.83 us (2%)
    all_to_all x4, blocking collectives, exchange(): lax.all_to_all(value, ALL, 0, 0, axis_index_groups=groups, tiled=True)  81.6 us
    all_to_all x2, blocking collectives, cross(): owned = lax.all_to_all(waves, LAT, 0, 0, tiled=True)  41.1 us
    all_to_all x2, blocking collectives, cross(): return lax.all_to_all(back, LAT, 0, 0, tiled=True)  33.2 us
    pallas_call x11, Pallas kernels, call(): pl.pallas_call(kernel, out_shape=tuple((jax.ShapeDtypeStruct(shape, dtype...  17 us
    ppermute x1, starting transfers between devices, body(): received = lax.ppermute(send, 'c', SWAP)  4.06 us
  transfers between devices with their start and end apart: 3, of which 2 were waited for; matrix products, arithmetic and copies ran while one was open for 0% of the time, Pallas kernels for 3%

profile of v6, /device:TPU:1, one launch (start us, length us, event | category | flops | bytes accessed | tf_op | source)
XLA Modules:
  0.0 186.9 jit_solution(17902836557765134962)
XLA Ops:
  0.6 4.5 %first.1 = (f32[64,8,128]{2,1,0:T(8,128)S(1)}, bf16[512,128]{1,0:T(8,128)(2,1)S(1)}, bf16[128,1024]{1,0:T(8,128)(2,1)S(1)}, bf16[1024,1024]{1,0:T(8,128)(2,1)S(1...) custom-call(f32[1,2,256,128]{3,2,1,0:T(8,128)} %state_hbm.1, ...), custom_call_target="tpu_custom_call" | custom-call | tf_op jit(solution)/shard_map/first/pallas_call | solution.py:112
  5.2 24.2 %all_to_all.40.owned = f32[64,8,128]{2,1,0:T(8,128)S(1)} all-to-all(f32[64,8,128]{2,1,0:T(8,128)S(1)} %get-tuple-element.36), channel_id=1, replica_groups=mesh['xl'=2,'z'=8,'y'=4,'xh'=2,'c'=2] {'xl','z','y'}, dimensions={0} | all-to-all | bytes 524288 | tf_op jit(solution)/shard_map/all_to_all | solution.py:398
  29.4 0.6 latitudes.2
  30.0 17.0 %all_to_all.41.waves_in = f32[64,8,128]{2,1,0:T(8,128)S(1)} all-to-all(f32[64,8,128]{2,1,0:T(8,128)S(1)} %latitudes.2), channel_id=1, replica_groups=mesh['xl'=2,'z'=8,'y'=4,'xh'=2,'c'=2] {'xl','z','y'}, dimensions={0} | all-to-all | bytes 524288 | tf_op jit(solution)/shard_map/all_to_all | solution.py:402
  47.0 4.8 %middle.1 = (f32[64,8,128]{2,1,0:T(8,128)S(1)}, bf16[512,128]{1,0:T(8,128)(2,1)S(1)}, bf16[2,512,512]{2,1,0:T(8,128)(2,1)S(1)}, bf16[512,1024]{1,0:T(8,128)(2,1)...) custom-call(f32[64,8,128]{2,1,0:T(8,128)S(1)} %all_to_all.41.waves_in, ...), custom_call_target="tpu_custom_call" | custom-call | tf_op jit(solution)/shard_map/middle/pallas_call | solution.py:112
  51.8 16.9 %all_to_all.42.owned = f32[64,8,128]{2,1,0:T(8,128)S(1)} all-to-all(f32[64,8,128]{2,1,0:T(8,128)S(1)} %get-tuple-element.44), channel_id=1, replica_groups=mesh['xl'=2,'z'=8,'y'=4,'xh'=2,'c'=2] {'xl','z','y'}, dimensions={0} | all-to-all | bytes 524288 | tf_op jit(solution)/shard_map/all_to_all | solution.py:398
  68.8 0.6 latitudes.3
  69.4 16.2 %all_to_all.43.waves_in = f32[64,8,128]{2,1,0:T(8,128)S(1)} all-to-all(f32[64,8,128]{2,1,0:T(8,128)S(1)} %latitudes.3), channel_id=1, replica_groups=mesh['xl'=2,'z'=8,'y'=4,'xh'=2,'c'=2] {'xl','z','y'}, dimensions={0} | all-to-all | bytes 524288 | tf_op jit(solution)/shard_map/all_to_all | solution.py:402
  85.6 2.1 %last.1 = (f32[2,256,128]{2,1,0:T(8,128)}, f32[512,1024]{1,0:T(8,128)S(1)}, bf16[512,1024]{1,0:T(8,128)(2,1)S(1)}, bf16[512,128]{1,0:T(8,128)(2,1)S(1)}) custom-call(f32[64,8,128]{2,1,0:T(8,128)S(1)} %all_to_all.43.waves_in, f32[256,128]{1,0:T(8,128)S(1)} %get-tuple-element.40.table_t, bf16[2,512,512]{2,1,0:T(8,128)(2,1)S(1)} %get-tuple-element.45.h1_0, ...), custom_call_target="tpu_custom_call" | custom-call | tf_op jit(solution)/shard_map/last/pallas_call | solution.py:112
  87.7 4.1 %collective-permute-start = (f32[512,1024]{1,0:T(8,128)S(1)}, f32[512,1024]{1,0:T(8,128)S(1)}, u32[]{:S(2)}, u32[]{:S(2)}) collective-permute-start(f32[512,1024]{1,0:T(8,128)S(1)} %get-tuple-element.60), channel_id=1, source_target_pairs={{0,1},{1,0},{2,3},{3,2},{4,5},{5,4},{6,7},{7,6},{8,9},{9,8},{10,11... | collective-permute-start | bytes 6291464 | tf_op jit(solution)/shard_map/ppermute | solution.py:437
  91.8 2.3 %thin.1 = (f32[128,1024]{1,0:T(8,128)S(1)}, f32[128,1024]{1,0:T(8,128)S(1)}) custom-call(bf16[512,128]{1,0:T(8,128)(2,1)S(1)} %get-tuple-element.51.x_0, bf16[512,1024]{1,0:T(8,128)(2,1)S(1)} %get-tuple-element.52.h2_0, f32[512,1024]{1,0:T(8,128)S(1)} %get-tuple-element.53.s1, bf16[512,1024]{1,0:T(8,128)(2,1)S(1)} %get-tuple-element.50.ga2_0.ga2, ...), custom_call_target="tpu_custom_call" | custom-call | tf_op jit(solution)/shard_map/thin/pallas_call | solution.py:112
  94.1 0.1 collective-permute-start.1
  94.2 1.3 keep.1.left
  95.5 0.8 collective-permute-done.1.right_thin
  96.3 0.0 collective-permute-done.right
  96.3 0.3 add.1
  96.6 23.1 %all_to_all.44.parts = f32[8,80,1024]{2,1,0:T(8,128)S(1)} all-to-all(f32[8,80,1024]{2,1,0:T(8,128)S(1)} %bitcast.5), channel_id=1, replica_groups={{0,16,128,144,2,18,130,146},{32,48,160,176,34,50,162,178},{64,80,192,20..., dimensions={0} | all-to-all | bytes 5242880 | tf_op jit(solution)/shard_map/all_to_all | solution.py:53
  119.6 0.1 sum_wide.1
  119.8 19.4 %all_to_all.45.parts = f32[16,40,128]{2,1,0:T(8,128)S(1)} all-to-all(f32[16,40,128]{2,1,0:T(8,128)S(1)} %sum_wide.1), channel_id=1, replica_groups={{0,32,64,96,4,36,68,100,8,40,72,104,12,44,76,108},{16,48,80,112,20,52,8..., dimensions={0} | all-to-all | bytes 655360 | tf_op jit(solution)/shard_map/all_to_all | solution.py:53
  139.2 17.2 %all_to_all.46.parts = f32[16,40,128]{2,1,0:T(8,128)S(1)} all-to-all(f32[16,40,128]{2,1,0:T(8,128)S(1)} %sum_deep.1), channel_id=1, replica_groups={{0,32,64,96,4,36,68,100,8,40,72,104,12,44,76,108},{16,48,80,112,20,52,8..., dimensions={0} | all-to-all | bytes 655360 | tf_op jit(solution)/shard_map/all_to_all | solution.py:53
  156.4 0.3 spread.1
  156.7 21.9 %all_to_all.47 = f32[8,80,1024]{2,1,0:T(8,128)S(1)} all-to-all(f32[8,80,1024]{2,1,0:T(8,128)S(1)} %spread.1), channel_id=1, replica_groups={{0,16,128,144,2,18,130,146},{32,48,160,176,34,50,162,178},{64,80,192,20..., dimensions={0} | all-to-all | bytes 5242880 | tf_op jit(solution)/shard_map/all_to_all | solution.py:53
  178.7 2.0 %collective-permute-start.2 = (f32[640,1024]{1,0:T(8,128)S(1)}, f32[640,1024]{1,0:T(8,128)S(1)}, u32[]{:S(2)}, u32[]{:S(2)}) collective-permute-start(f32[640,1024]{1,0:T(8,128)S(1)} %bitcast.3), channel_id=1, source_target_pairs={{0,1},{1,0},{2,3},{3,2},{4,5},{5,4},{6,7},{7,6},{8,9},{9,8},{10,11... | collective-permute-start | bytes 7864328 | tf_op jit(solution)/shard_map/ppermute | solution.py:462
  180.6 1.6 own.1
  182.2 3.0 %collective-permute-done.2.source = f32[640,1024]{1,0:T(8,128)S(1)} collective-permute-done((f32[640,1024]{1,0:T(8,128)S(1)}, f32[640,1024]{1,0:T(8,128)S(1)}, u32[]{:S(2)}, u32[]{:S(2)}) %collective-permute-start.2) | collective-permute-done | bytes 2621472 | tf_op jit(solution)/shard_map/ppermute | solution.py:462
  185.2 1.6 other.1
  (1 shorter events, 0.0 us)
Async XLA Ops:
  87.7 8.6 %collective-permute-start = (f32[512,1024]{1,0:T(8,128)S(1)}, f32[512,1024]{1,0:T(8,128)S(1)}, u32[]{:S(2)}, u32[]{:S(2)}) collective-permute-start(f32[512,1024]{1,0:T(8,128)S(1)} %get-tuple-element.60), channel_id=1, source_target_pairs={{0,1},{1,0},{2,3},{3,2},{4,5},{5,4},{6,7},{7,6},{8,9},{9,8},{10,11... | collective-permute-start | bytes 6291464 | tf_op jit(solution)/shard_map/ppermute | solution.py:437
  94.1 2.2 %collective-permute-start.1 = (f32[128,1024]{1,0:T(8,128)S(1)}, f32[128,1024]{1,0:T(8,128)S(1)}, u32[]{:S(2)}, u32[]{:S(2)}) collective-permute-start(f32[128,1024]{1,0:T(8,128)S(1)} %get-tuple-element.61), channel_id=1, source_target_pairs={{0,1},{1,0},{2,3},{3,2},{4,5},{5,4},{6,7},{7,6},{8,9},{9,8},{10,11... | collective-permute-start | bytes 1572872 | tf_op jit(solution)/shard_map/ppermute | solution.py:445
  178.7 6.5 %collective-permute-start.2 = (f32[640,1024]{1,0:T(8,128)S(1)}, f32[640,1024]{1,0:T(8,128)S(1)}, u32[]{:S(2)}, u32[]{:S(2)}) collective-permute-start(f32[640,1024]{1,0:T(8,128)S(1)} %bitcast.3), channel_id=1, source_target_pairs={{0,1},{1,0},{2,3},{3,2},{4,5},{5,4},{6,7},{7,6},{8,9},{9,8},{10,11... | collective-permute-start | bytes 7864328 | tf_op jit(solution)/shard_map/ppermute | solution.py:462

commit v7 on v6

--- a/solution.py
+++ b/solution.py
@@ -15,7 +15,9 @@
 
 FINE = (("xl", 2), ("z", 8), ("y", 4), ("xh", 2), ("c", 2))
 ALL = tuple(name for name, _ in FINE)
-LAT = ("xl", "z", "y")
+BAND = ("xl", "z", "y")
+LAT = ("z", "y", "xl")
+XL = dict(FINE)["xl"]
 SWAP = [(0, 1), (1, 0)]
 
 
@@ -36,12 +38,12 @@
     for x in range(4):
         for parity in range(2):
             deep.append(
-                [device_id(x, y, 2 * pair + parity, 0) for y in range(4) for pair in range(4)]
+                [device_id(x, y, 2 * pair + parity, 0) for pair in range(4) for y in range(4)]
             )
     for y in range(4):
         for parity in range(2):
             deep.append(
-                [device_id(x, y, 2 * pair + parity, 1) for x in range(4) for pair in range(4)]
+                [device_id(x, y, 2 * pair + parity, 1) for pair in range(4) for x in range(4)]
             )
     return wide, deep
 
@@ -56,7 +58,10 @@
 def legendre(lat_count, wave_count, order, forward_ref, backward_ref, table):
     bands = lat_count // 2
     place = lax.broadcasted_iota(jnp.int32, (1, lat_count), 1)
-    lat_index = jnp.where(place >= bands, 2 * (place - bands) + 1, 2 * place).astype(jnp.float32)
+    row = place // bands
+    rank = place - row * bands
+    band = rank % XL * (bands // XL) + rank // XL
+    lat_index = (2 * band + row).astype(jnp.float32)
     latitude = (lat_index + 0.5) * (math.pi / lat_count) - 0.5 * math.pi
     sine_lat = jnp.sin(latitude)
     cosine_lat = jnp.cos(latitude)
@@ -466,7 +471,7 @@
 
 def solution(mesh):
     fine = Mesh(mesh.devices.reshape(tuple(size for _, size in FINE)), ALL)
-    grid = P(("xh", "c"), LAT, None, None)
+    grid = P(("xh", "c"), BAND, None, None)
     return jax.shard_map(
         body,
         mesh=fine,

time: 187 us -> 186 us (level)
  no operation moved by 1% of the time
where the time goes in v7:
time: 186 us; the launch traced here: 185 us
  blocking collectives  155 us (83%)
  Pallas kernels  20.1 us (11%)
  starting transfers between devices  5.75 us (3%)
  waiting for transfers between devices  3.81 us (2%)
    all_to_all x4, blocking collectives, exchange(): lax.all_to_all(value, ALL, 0, 0, axis_index_groups=groups, tiled=True)  80.8 us
    all_to_all x2, blocking collectives, cross(): owned = lax.all_to_all(waves, LAT, 0, 0, tiled=True)  40.9 us
    all_to_all x2, blocking collectives, cross(): return lax.all_to_all(back, LAT, 0, 0, tiled=True)  32.9 us
    pallas_call x11, Pallas kernels, call(): pl.pallas_call(kernel, out_shape=tuple((jax.ShapeDtypeStruct(shape, dtype...  17 us
    ppermute x1, starting transfers between devices, body(): received = lax.ppermute(send, 'c', SWAP)  4.04 us
  transfers between devices with their start and end apart: 3, of which 2 were waited for; matrix products, arithmetic and copies ran while one was open for 0% of the time, Pallas kernels for 3%

profile of v7, /device:TPU:1, one launch (start us, length us, event | category | flops | bytes accessed | tf_op | source)
XLA Modules:
  0.0 185.1 jit_solution(147747201841874672)
XLA Ops:
  0.6 4.5 %first.1 = (f32[64,8,128]{2,1,0:T(8,128)S(1)}, bf16[512,128]{1,0:T(8,128)(2,1)S(1)}, bf16[128,1024]{1,0:T(8,128)(2,1)S(1)}, bf16[1024,1024]{1,0:T(8,128)(2,1)S(1...) custom-call(f32[1,2,256,128]{3,2,1,0:T(8,128)} %state_hbm.1, ...), custom_call_target="tpu_custom_call" | custom-call | tf_op jit(solution)/shard_map/first/pallas_call | solution.py:117
  5.2 24.1 %all_to_all.40.owned = f32[64,8,128]{2,1,0:T(8,128)S(1)} all-to-all(f32[64,8,128]{2,1,0:T(8,128)S(1)} %get-tuple-element.36), channel_id=1, replica_groups=mesh['xl'=2,'z'=8,'y'=4,'xh'=2,'c'=2] {'z','y','xl'}, dimensions={0} | all-to-all | bytes 524288 | tf_op jit(solution)/shard_map/all_to_all | solution.py:403
  29.3 0.6 latitudes.2
  29.9 16.9 %all_to_all.41.waves_in = f32[64,8,128]{2,1,0:T(8,128)S(1)} all-to-all(f32[64,8,128]{2,1,0:T(8,128)S(1)} %latitudes.2), channel_id=1, replica_groups=mesh['xl'=2,'z'=8,'y'=4,'xh'=2,'c'=2] {'z','y','xl'}, dimensions={0} | all-to-all | bytes 524288 | tf_op jit(solution)/shard_map/all_to_all | solution.py:407
  46.8 4.8 %middle.1 = (f32[64,8,128]{2,1,0:T(8,128)S(1)}, bf16[512,128]{1,0:T(8,128)(2,1)S(1)}, bf16[2,512,512]{2,1,0:T(8,128)(2,1)S(1)}, bf16[512,1024]{1,0:T(8,128)(2,1)...) custom-call(f32[64,8,128]{2,1,0:T(8,128)S(1)} %all_to_all.41.waves_in, ...), custom_call_target="tpu_custom_call" | custom-call | tf_op jit(solution)/shard_map/middle/pallas_call | solution.py:117
  51.6 16.8 %all_to_all.42.owned = f32[64,8,128]{2,1,0:T(8,128)S(1)} all-to-all(f32[64,8,128]{2,1,0:T(8,128)S(1)} %get-tuple-element.44), channel_id=1, replica_groups=mesh['xl'=2,'z'=8,'y'=4,'xh'=2,'c'=2] {'z','y','xl'}, dimensions={0} | all-to-all | bytes 524288 | tf_op jit(solution)/shard_map/all_to_all | solution.py:403
  68.3 0.6 latitudes.3
  69.0 16.0 %all_to_all.43.waves_in = f32[64,8,128]{2,1,0:T(8,128)S(1)} all-to-all(f32[64,8,128]{2,1,0:T(8,128)S(1)} %latitudes.3), channel_id=1, replica_groups=mesh['xl'=2,'z'=8,'y'=4,'xh'=2,'c'=2] {'z','y','xl'}, dimensions={0} | all-to-all | bytes 524288 | tf_op jit(solution)/shard_map/all_to_all | solution.py:407
  85.0 2.1 %last.1 = (f32[2,256,128]{2,1,0:T(8,128)}, f32[512,1024]{1,0:T(8,128)S(1)}, bf16[512,1024]{1,0:T(8,128)(2,1)S(1)}, bf16[512,128]{1,0:T(8,128)(2,1)S(1)}) custom-call(f32[64,8,128]{2,1,0:T(8,128)S(1)} %all_to_all.43.waves_in, f32[256,128]{1,0:T(8,128)S(1)} %get-tuple-element.40.table_t, bf16[2,512,512]{2,1,0:T(8,128)(2,1)S(1)} %get-tuple-element.45.h1_0, ...), custom_call_target="tpu_custom_call" | custom-call | tf_op jit(solution)/shard_map/last/pallas_call | solution.py:117
  87.1 4.0 %collective-permute-start = (f32[512,1024]{1,0:T(8,128)S(1)}, f32[512,1024]{1,0:T(8,128)S(1)}, u32[]{:S(2)}, u32[]{:S(2)}) collective-permute-start(f32[512,1024]{1,0:T(8,128)S(1)} %get-tuple-element.60), channel_id=1, source_target_pairs={{0,1},{1,0},{2,3},{3,2},{4,5},{5,4},{6,7},{7,6},{8,9},{9,8},{10,11... | collective-permute-start | bytes 6291464 | tf_op jit(solution)/shard_map/ppermute | solution.py:442
  91.2 2.3 %thin.1 = (f32[128,1024]{1,0:T(8,128)S(1)}, f32[128,1024]{1,0:T(8,128)S(1)}) custom-call(bf16[512,128]{1,0:T(8,128)(2,1)S(1)} %get-tuple-element.51.x_0, bf16[512,1024]{1,0:T(8,128)(2,1)S(1)} %get-tuple-element.52.h2_0, f32[512,1024]{1,0:T(8,128)S(1)} %get-tuple-element.53.s1, bf16[512,1024]{1,0:T(8,128)(2,1)S(1)} %get-tuple-element.50.ga2_0.ga2, ...), custom_call_target="tpu_custom_call" | custom-call | tf_op jit(solution)/shard_map/thin/pallas_call | solution.py:117
  93.5 0.1 collective-permute-start.1
  93.6 1.3 keep.1.left
  94.9 0.8 collective-permute-done.1.right_thin
  95.7 0.0 collective-permute-done.right
  95.7 0.3 add.1
  96.0 22.5 %all_to_all.44.parts = f32[8,80,1024]{2,1,0:T(8,128)S(1)} all-to-all(f32[8,80,1024]{2,1,0:T(8,128)S(1)} %bitcast.5), channel_id=1, replica_groups={{0,16,128,144,2,18,130,146},{32,48,160,176,34,50,162,178},{64,80,192,20..., dimensions={0} | all-to-all | bytes 5242880 | tf_op jit(solution)/shard_map/all_to_all | solution.py:55
  118.5 0.1 sum_wide.1
  118.6 18.6 %all_to_all.45.parts = f32[16,40,128]{2,1,0:T(8,128)S(1)} all-to-all(f32[16,40,128]{2,1,0:T(8,128)S(1)} %sum_wide.1), channel_id=1, replica_groups={{0,4,8,12,32,36,40,44,64,68,72,76,96,100,104,108},{16,20,24,28,48,52,56..., dimensions={0} | all-to-all | bytes 655360 | tf_op jit(solution)/shard_map/all_to_all | solution.py:55
  137.3 17.1 %all_to_all.46.parts = f32[16,40,128]{2,1,0:T(8,128)S(1)} all-to-all(f32[16,40,128]{2,1,0:T(8,128)S(1)} %sum_deep.1), channel_id=1, replica_groups={{0,4,8,12,32,36,40,44,64,68,72,76,96,100,104,108},{16,20,24,28,48,52,56..., dimensions={0} | all-to-all | bytes 655360 | tf_op jit(solution)/shard_map/all_to_all | solution.py:55
  154.4 0.3 spread.1
  154.7 22.6 %all_to_all.47 = f32[8,80,1024]{2,1,0:T(8,128)S(1)} all-to-all(f32[8,80,1024]{2,1,0:T(8,128)S(1)} %spread.1), channel_id=1, replica_groups={{0,16,128,144,2,18,130,146},{32,48,160,176,34,50,162,178},{64,80,192,20..., dimensions={0} | all-to-all | bytes 5242880 | tf_op jit(solution)/shard_map/all_to_all | solution.py:55
  177.3 1.6 collective-permute-start.2
  178.9 1.6 own.1
  180.5 3.0 %collective-permute-done.2.source = f32[640,1024]{1,0:T(8,128)S(1)} collective-permute-done((f32[640,1024]{1,0:T(8,128)S(1)}, f32[640,1024]{1,0:T(8,128)S(1)}, u32[]{:S(2)}, u32[]{:S(2)}) %collective-permute-start.2) | collective-permute-done | bytes 2621472 | tf_op jit(solution)/shard_map/ppermute | solution.py:467
  183.4 1.6 other.1
  (1 shorter events, 0.0 us)
Async XLA Ops:
  87.1 8.6 %collective-permute-start = (f32[512,1024]{1,0:T(8,128)S(1)}, f32[512,1024]{1,0:T(8,128)S(1)}, u32[]{:S(2)}, u32[]{:S(2)}) collective-permute-start(f32[512,1024]{1,0:T(8,128)S(1)} %get-tuple-element.60), channel_id=1, source_target_pairs={{0,1},{1,0},{2,3},{3,2},{4,5},{5,4},{6,7},{7,6},{8,9},{9,8},{10,11... | collective-permute-start | bytes 6291464 | tf_op jit(solution)/shard_map/ppermute | solution.py:442
  93.5 2.2 %collective-permute-start.1 = (f32[128,1024]{1,0:T(8,128)S(1)}, f32[128,1024]{1,0:T(8,128)S(1)}, u32[]{:S(2)}, u32[]{:S(2)}) collective-permute-start(f32[128,1024]{1,0:T(8,128)S(1)} %get-tuple-element.61), channel_id=1, source_target_pairs={{0,1},{1,0},{2,3},{3,2},{4,5},{5,4},{6,7},{7,6},{8,9},{9,8},{10,11... | collective-permute-start | bytes 1572872 | tf_op jit(solution)/shard_map/ppermute | solution.py:450
  177.3 6.1 %collective-permute-start.2 = (f32[640,1024]{1,0:T(8,128)S(1)}, f32[640,1024]{1,0:T(8,128)S(1)}, u32[]{:S(2)}, u32[]{:S(2)}) collective-permute-start(f32[640,1024]{1,0:T(8,128)S(1)} %bitcast.3), channel_id=1, source_target_pairs={{0,1},{1,0},{2,3},{3,2},{4,5},{5,4},{6,7},{7,6},{8,9},{9,8},{10,11... | collective-permute-start | bytes 7864328 | tf_op jit(solution)/shard_map/ppermute | solution.py:467

commit v8 on v7

--- a/solution.py
+++ b/solution.py
@@ -144,8 +144,15 @@
     )
 
 
-def mm_exact(left, right):
-    return jnp.dot(left, right, precision=highest, preferred_element_type=jnp.float32)
+def split(value):
+    high = value.astype(jnp.bfloat16)
+    return high, (value - high.astype(jnp.float32)).astype(jnp.bfloat16)
+
+
+def mm_fine(left, right):
+    left_high, left_low = split(left)
+    right_high, right_low = split(right)
+    return mm(left_high, right_high) + (mm(left_high, right_low) + mm(left_low, right_high))
 
 
 def silu_pair(value):
@@ -163,7 +170,7 @@
 
 
 def store_waves(table, fields, out_ref):
-    waves = mm_exact(table, jnp.concatenate(fields, axis=1))
+    waves = mm_fine(table, jnp.concatenate(fields, axis=1))
     feat = fields[0].shape[1]
     for i in range(len(fields)):
         for p in range(2):
@@ -176,7 +183,7 @@
         for i in range(4)
     ]
     feat = columns[0].shape[1]
-    grid = mm_exact(table_t, jnp.concatenate(columns, axis=1))
+    grid = mm_fine(table_t, jnp.concatenate(columns, axis=1))
     return [grid[:, i * feat : (i + 1) * feat] for i in range(4)]
 
 
@@ -283,7 +290,7 @@
             jnp.concatenate([owned[:, 4 * i + p, :], owned[:, 4 * i + 2 + p, :]], axis=0)
             for p in range(2)
         ]
-        found = mm_exact(operator[...], jnp.concatenate(parts, axis=1))
+        found = mm_fine(operator[...], jnp.concatenate(parts, axis=1))
         bands = owned.shape[0]
         feat = owned.shape[2]
         for j in range(2):

time: 186 us -> 185 us (level)
  no operation moved by 1% of the time
where the time goes in v8:
time: 185 us; the launch traced here: 184 us
  blocking collectives  155 us (84%)
  Pallas kernels  19.2 us (10%)
  starting transfers between devices  5.32 us (3%)
  waiting for transfers between devices  3.81 us (2%)
    all_to_all x4, blocking collectives, exchange(): lax.all_to_all(value, ALL, 0, 0, axis_index_groups=groups, tiled=True)  81.1 us
    all_to_all x2, blocking collectives, cross(): owned = lax.all_to_all(waves, LAT, 0, 0, tiled=True)  40.9 us
    all_to_all x2, blocking collectives, cross(): return lax.all_to_all(back, LAT, 0, 0, tiled=True)  33 us
    pallas_call x11, Pallas kernels, call(): pl.pallas_call(kernel, out_shape=tuple((jax.ShapeDtypeStruct(shape, dtype...  16.1 us
    ppermute x1, starting transfers between devices, body(): received = lax.ppermute(send, 'c', SWAP)  3.95 us
  transfers between devices with their start and end apart: 3, of which 2 were waited for; matrix products, arithmetic and copies ran while one was open for 0% of the time, Pallas kernels for 3%

profile of v8, /device:TPU:1, one launch (start us, length us, event | category | flops | bytes accessed | tf_op | source)
XLA Modules:
  0.0 184.2 jit_solution(6038942751602748192)
XLA Ops:
  0.6 4.4 %first.1 = (f32[64,8,128]{2,1,0:T(8,128)S(1)}, bf16[512,128]{1,0:T(8,128)(2,1)S(1)}, bf16[128,1024]{1,0:T(8,128)(2,1)S(1)}, bf16[1024,1024]{1,0:T(8,128)(2,1)S(1...) custom-call(f32[1,2,256,128]{3,2,1,0:T(8,128)} %state_hbm.1, ...), custom_call_target="tpu_custom_call" | custom-call | tf_op jit(solution)/shard_map/first/pallas_call | solution.py:117
  5.0 24.1 %all_to_all.40.owned = f32[64,8,128]{2,1,0:T(8,128)S(1)} all-to-all(f32[64,8,128]{2,1,0:T(8,128)S(1)} %get-tuple-element.36), channel_id=1, replica_groups=mesh['xl'=2,'z'=8,'y'=4,'xh'=2,'c'=2] {'z','y','xl'}, dimensions={0} | all-to-all | bytes 524288 | tf_op jit(solution)/shard_map/all_to_all | solution.py:410
  29.1 0.5 latitudes.2
  29.6 16.9 %all_to_all.41.waves_in = f32[64,8,128]{2,1,0:T(8,128)S(1)} all-to-all(f32[64,8,128]{2,1,0:T(8,128)S(1)} %latitudes.2), channel_id=1, replica_groups=mesh['xl'=2,'z'=8,'y'=4,'xh'=2,'c'=2] {'z','y','xl'}, dimensions={0} | all-to-all | bytes 524288 | tf_op jit(solution)/shard_map/all_to_all | solution.py:414
  46.5 4.5 %middle.1 = (f32[64,8,128]{2,1,0:T(8,128)S(1)}, bf16[512,128]{1,0:T(8,128)(2,1)S(1)}, bf16[2,512,512]{2,1,0:T(8,128)(2,1)S(1)}, bf16[512,1024]{1,0:T(8,128)(2,1)...) custom-call(f32[64,8,128]{2,1,0:T(8,128)S(1)} %all_to_all.41.waves_in, ...), custom_call_target="tpu_custom_call" | custom-call | tf_op jit(solution)/shard_map/middle/pallas_call | solution.py:117
  51.1 16.8 %all_to_all.42.owned = f32[64,8,128]{2,1,0:T(8,128)S(1)} all-to-all(f32[64,8,128]{2,1,0:T(8,128)S(1)} %get-tuple-element.44), channel_id=1, replica_groups=mesh['xl'=2,'z'=8,'y'=4,'xh'=2,'c'=2] {'z','y','xl'}, dimensions={0} | all-to-all | bytes 524288 | tf_op jit(solution)/shard_map/all_to_all | solution.py:410
  67.8 0.5 latitudes.3
  68.3 16.1 %all_to_all.43.waves_in = f32[64,8,128]{2,1,0:T(8,128)S(1)} all-to-all(f32[64,8,128]{2,1,0:T(8,128)S(1)} %latitudes.3), channel_id=1, replica_groups=mesh['xl'=2,'z'=8,'y'=4,'xh'=2,'c'=2] {'z','y','xl'}, dimensions={0} | all-to-all | bytes 524288 | tf_op jit(solution)/shard_map/all_to_all | solution.py:414
  84.4 1.9 %last.1 = (f32[2,256,128]{2,1,0:T(8,128)}, f32[512,1024]{1,0:T(8,128)S(1)}, bf16[512,1024]{1,0:T(8,128)(2,1)S(1)}, bf16[512,128]{1,0:T(8,128)(2,1)S(1)}) custom-call(f32[64,8,128]{2,1,0:T(8,128)S(1)} %all_to_all.43.waves_in, f32[256,128]{1,0:T(8,128)S(1)} %get-tuple-element.40.table_t, bf16[2,512,512]{2,1,0:T(8,128)(2,1)S(1)} %get-tuple-element.45.h1_0, ...), custom_call_target="tpu_custom_call" | custom-call | tf_op jit(solution)/shard_map/last/pallas_call | solution.py:117
  86.3 4.0 %collective-permute-start = (f32[512,1024]{1,0:T(8,128)S(1)}, f32[512,1024]{1,0:T(8,128)S(1)}, u32[]{:S(2)}, u32[]{:S(2)}) collective-permute-start(f32[512,1024]{1,0:T(8,128)S(1)} %get-tuple-element.60), channel_id=1, source_target_pairs={{0,1},{1,0},{2,3},{3,2},{4,5},{5,4},{6,7},{7,6},{8,9},{9,8},{10,11... | collective-permute-start | bytes 6291464 | tf_op jit(solution)/shard_map/ppermute | solution.py:449
  90.3 2.3 %thin.1 = (f32[128,1024]{1,0:T(8,128)S(1)}, f32[128,1024]{1,0:T(8,128)S(1)}) custom-call(bf16[512,128]{1,0:T(8,128)(2,1)S(1)} %get-tuple-element.51.x_0, bf16[512,1024]{1,0:T(8,128)(2,1)S(1)} %get-tuple-element.52.h2_0, f32[512,1024]{1,0:T(8,128)S(1)} %get-tuple-element.53.s1, bf16[512,1024]{1,0:T(8,128)(2,1)S(1)} %get-tuple-element.50.ga2_0.ga2, ...), custom_call_target="tpu_custom_call" | custom-call | tf_op jit(solution)/shard_map/thin/pallas_call | solution.py:117
  92.6 0.1 collective-permute-start.1
  92.7 1.3 keep.1.left
  94.0 0.8 collective-permute-done.1.right_thin
  94.8 0.0 collective-permute-done.right
  94.8 0.3 add.1
  95.1 22.5 %all_to_all.44.parts = f32[8,80,1024]{2,1,0:T(8,128)S(1)} all-to-all(f32[8,80,1024]{2,1,0:T(8,128)S(1)} %bitcast.5), channel_id=1, replica_groups={{0,16,128,144,2,18,130,146},{32,48,160,176,34,50,162,178},{64,80,192,20..., dimensions={0} | all-to-all | bytes 5242880 | tf_op jit(solution)/shard_map/all_to_all | solution.py:55
  117.6 0.1 sum_wide.1
  117.8 18.6 %all_to_all.45.parts = f32[16,40,128]{2,1,0:T(8,128)S(1)} all-to-all(f32[16,40,128]{2,1,0:T(8,128)S(1)} %sum_wide.1), channel_id=1, replica_groups={{0,4,8,12,32,36,40,44,64,68,72,76,96,100,104,108},{16,20,24,28,48,52,56..., dimensions={0} | all-to-all | bytes 655360 | tf_op jit(solution)/shard_map/all_to_all | solution.py:55
  136.4 17.0 %all_to_all.46.parts = f32[16,40,128]{2,1,0:T(8,128)S(1)} all-to-all(f32[16,40,128]{2,1,0:T(8,128)S(1)} %sum_deep.1), channel_id=1, replica_groups={{0,4,8,12,32,36,40,44,64,68,72,76,96,100,104,108},{16,20,24,28,48,52,56..., dimensions={0} | all-to-all | bytes 655360 | tf_op jit(solution)/shard_map/all_to_all | solution.py:55
  153.4 0.3 spread.1
  153.7 23.0 %all_to_all.47 = f32[8,80,1024]{2,1,0:T(8,128)S(1)} all-to-all(f32[8,80,1024]{2,1,0:T(8,128)S(1)} %spread.1), channel_id=1, replica_groups={{0,16,128,144,2,18,130,146},{32,48,160,176,34,50,162,178},{64,80,192,20..., dimensions={0} | all-to-all | bytes 5242880 | tf_op jit(solution)/shard_map/all_to_all | solution.py:55
  176.7 1.2 collective-permute-start.2
  178.0 1.6 own.1
  179.5 3.0 %collective-permute-done.2.source = f32[640,1024]{1,0:T(8,128)S(1)} collective-permute-done((f32[640,1024]{1,0:T(8,128)S(1)}, f32[640,1024]{1,0:T(8,128)S(1)}, u32[]{:S(2)}, u32[]{:S(2)}) %collective-permute-start.2) | collective-permute-done | bytes 2621472 | tf_op jit(solution)/shard_map/ppermute | solution.py:474
  182.5 1.6 other.1
  (1 shorter events, 0.0 us)
Async XLA Ops:
  86.3 8.5 %collective-permute-start = (f32[512,1024]{1,0:T(8,128)S(1)}, f32[512,1024]{1,0:T(8,128)S(1)}, u32[]{:S(2)}, u32[]{:S(2)}) collective-permute-start(f32[512,1024]{1,0:T(8,128)S(1)} %get-tuple-element.60), channel_id=1, source_target_pairs={{0,1},{1,0},{2,3},{3,2},{4,5},{5,4},{6,7},{7,6},{8,9},{9,8},{10,11... | collective-permute-start | bytes 6291464 | tf_op jit(solution)/shard_map/ppermute | solution.py:449
  92.6 2.2 %collective-permute-start.1 = (f32[128,1024]{1,0:T(8,128)S(1)}, f32[128,1024]{1,0:T(8,128)S(1)}, u32[]{:S(2)}, u32[]{:S(2)}) collective-permute-start(f32[128,1024]{1,0:T(8,128)S(1)} %get-tuple-element.61), channel_id=1, source_target_pairs={{0,1},{1,0},{2,3},{3,2},{4,5},{5,4},{6,7},{7,6},{8,9},{9,8},{10,11... | collective-permute-start | bytes 1572872 | tf_op jit(solution)/shard_map/ppermute | solution.py:457
  176.7 5.8 %collective-permute-start.2 = (f32[640,1024]{1,0:T(8,128)S(1)}, f32[640,1024]{1,0:T(8,128)S(1)}, u32[]{:S(2)}, u32[]{:S(2)}) collective-permute-start(f32[640,1024]{1,0:T(8,128)S(1)} %bitcast.3), channel_id=1, source_target_pairs={{0,1},{1,0},{2,3},{3,2},{4,5},{5,4},{6,7},{7,6},{8,9},{9,8},{10,11... | collective-permute-start | bytes 7864328 | tf_op jit(solution)/shard_map/ppermute | solution.py:474

commit v9 on v8

--- a/solution.py
+++ b/solution.py
@@ -29,11 +29,11 @@
     wide, deep = [], []
     for y in range(4):
         for pair in range(4):
-            wide.append([device_id(x, y, 2 * pair + q, 0) for x in range(4) for q in range(2)])
+            wide.append([device_id(x, y, 2 * pair + q, 0) for q in range(2) for x in range(4)])
     for x in range(4):
         for pair in range(4):
             wide.append(
-                [device_id(x, y, (2 * pair + 1 + q) % 8, 1) for y in range(4) for q in range(2)]
+                [device_id(x, y, (2 * pair + 1 + q) % 8, 1) for q in range(2) for y in range(4)]
             )
     for x in range(4):
         for parity in range(2):

time: 185 us -> 185 us (level)
  no operation moved by 1% of the time
where the time goes in v9:
time: 185 us; the launch traced here: 184 us
  blocking collectives  155 us (84%)
  Pallas kernels  19.2 us (10%)
  starting transfers between devices  5.64 us (3%)
  waiting for transfers between devices  3.81 us (2%)
    all_to_all x4, blocking collectives, exchange(): lax.all_to_all(value, ALL, 0, 0, axis_index_groups=groups, tiled=True)  80.8 us
    all_to_all x2, blocking collectives, cross(): owned = lax.all_to_all(waves, LAT, 0, 0, tiled=True)  40.9 us
    all_to_all x2, blocking collectives, cross(): return lax.all_to_all(back, LAT, 0, 0, tiled=True)  33 us
    pallas_call x11, Pallas kernels, call(): pl.pallas_call(kernel, out_shape=tuple((jax.ShapeDtypeStruct(shape, dtype...  16.1 us
    ppermute x1, starting transfers between devices, body(): received = lax.ppermute(send, 'c', SWAP)  3.95 us
  transfers between devices with their start and end apart: 3, of which 2 were waited for; matrix products, arithmetic and copies ran while one was open for 0% of the time, Pallas kernels for 3%

profile of v9, /device:TPU:1, one launch (start us, length us, event | category | flops | bytes accessed | tf_op | source)
XLA Modules:
  0.0 184.2 jit_solution(654178026617154996)
XLA Ops:
  0.6 4.4 %first.1 = (f32[64,8,128]{2,1,0:T(8,128)S(1)}, bf16[512,128]{1,0:T(8,128)(2,1)S(1)}, bf16[128,1024]{1,0:T(8,128)(2,1)S(1)}, bf16[1024,1024]{1,0:T(8,128)(2,1)S(1...) custom-call(f32[1,2,256,128]{3,2,1,0:T(8,128)} %state_hbm.1, ...), custom_call_target="tpu_custom_call" | custom-call | tf_op jit(solution)/shard_map/first/pallas_call | solution.py:117
  5.0 24.1 %all_to_all.40.owned = f32[64,8,128]{2,1,0:T(8,128)S(1)} all-to-all(f32[64,8,128]{2,1,0:T(8,128)S(1)} %get-tuple-element.36), channel_id=1, replica_groups=mesh['xl'=2,'z'=8,'y'=4,'xh'=2,'c'=2] {'z','y','xl'}, dimensions={0} | all-to-all | bytes 524288 | tf_op jit(solution)/shard_map/all_to_all | solution.py:410
  29.1 0.5 latitudes.2
  29.6 16.9 %all_to_all.41.waves_in = f32[64,8,128]{2,1,0:T(8,128)S(1)} all-to-all(f32[64,8,128]{2,1,0:T(8,128)S(1)} %latitudes.2), channel_id=1, replica_groups=mesh['xl'=2,'z'=8,'y'=4,'xh'=2,'c'=2] {'z','y','xl'}, dimensions={0} | all-to-all | bytes 524288 | tf_op jit(solution)/shard_map/all_to_all | solution.py:414
  46.5 4.5 %middle.1 = (f32[64,8,128]{2,1,0:T(8,128)S(1)}, bf16[512,128]{1,0:T(8,128)(2,1)S(1)}, bf16[2,512,512]{2,1,0:T(8,128)(2,1)S(1)}, bf16[512,1024]{1,0:T(8,128)(2,1)...) custom-call(f32[64,8,128]{2,1,0:T(8,128)S(1)} %all_to_all.41.waves_in, ...), custom_call_target="tpu_custom_call" | custom-call | tf_op jit(solution)/shard_map/middle/pallas_call | solution.py:117
  51.1 16.8 %all_to_all.42.owned = f32[64,8,128]{2,1,0:T(8,128)S(1)} all-to-all(f32[64,8,128]{2,1,0:T(8,128)S(1)} %get-tuple-element.44), channel_id=1, replica_groups=mesh['xl'=2,'z'=8,'y'=4,'xh'=2,'c'=2] {'z','y','xl'}, dimensions={0} | all-to-all | bytes 524288 | tf_op jit(solution)/shard_map/all_to_all | solution.py:410
  67.8 0.5 latitudes.3
  68.3 16.1 %all_to_all.43.waves_in = f32[64,8,128]{2,1,0:T(8,128)S(1)} all-to-all(f32[64,8,128]{2,1,0:T(8,128)S(1)} %latitudes.3), channel_id=1, replica_groups=mesh['xl'=2,'z'=8,'y'=4,'xh'=2,'c'=2] {'z','y','xl'}, dimensions={0} | all-to-all | bytes 524288 | tf_op jit(solution)/shard_map/all_to_all | solution.py:414
  84.4 1.9 %last.1 = (f32[2,256,128]{2,1,0:T(8,128)}, f32[512,1024]{1,0:T(8,128)S(1)}, bf16[512,1024]{1,0:T(8,128)(2,1)S(1)}, bf16[512,128]{1,0:T(8,128)(2,1)S(1)}) custom-call(f32[64,8,128]{2,1,0:T(8,128)S(1)} %all_to_all.43.waves_in, f32[256,128]{1,0:T(8,128)S(1)} %get-tuple-element.40.table_t, bf16[2,512,512]{2,1,0:T(8,128)(2,1)S(1)} %get-tuple-element.45.h1_0, ...), custom_call_target="tpu_custom_call" | custom-call | tf_op jit(solution)/shard_map/last/pallas_call | solution.py:117
  86.3 4.0 %collective-permute-start = (f32[512,1024]{1,0:T(8,128)S(1)}, f32[512,1024]{1,0:T(8,128)S(1)}, u32[]{:S(2)}, u32[]{:S(2)}) collective-permute-start(f32[512,1024]{1,0:T(8,128)S(1)} %get-tuple-element.60), channel_id=1, source_target_pairs={{0,1},{1,0},{2,3},{3,2},{4,5},{5,4},{6,7},{7,6},{8,9},{9,8},{10,11... | collective-permute-start | bytes 6291464 | tf_op jit(solution)/shard_map/ppermute | solution.py:449
  90.3 2.3 %thin.1 = (f32[128,1024]{1,0:T(8,128)S(1)}, f32[128,1024]{1,0:T(8,128)S(1)}) custom-call(bf16[512,128]{1,0:T(8,128)(2,1)S(1)} %get-tuple-element.51.x_0, bf16[512,1024]{1,0:T(8,128)(2,1)S(1)} %get-tuple-element.52.h2_0, f32[512,1024]{1,0:T(8,128)S(1)} %get-tuple-element.53.s1, bf16[512,1024]{1,0:T(8,128)(2,1)S(1)} %get-tuple-element.50.ga2_0.ga2, ...), custom_call_target="tpu_custom_call" | custom-call | tf_op jit(solution)/shard_map/thin/pallas_call | solution.py:117
  92.6 0.1 collective-permute-start.1
  92.7 1.3 keep.1.left
  94.0 0.8 collective-permute-done.1.right_thin
  94.8 0.0 collective-permute-done.right
  94.8 0.3 add.1
  95.1 22.5 %all_to_all.44.parts = f32[8,80,1024]{2,1,0:T(8,128)S(1)} all-to-all(f32[8,80,1024]{2,1,0:T(8,128)S(1)} %bitcast.5), channel_id=1, replica_groups={{0,128,2,130,16,144,18,146},{32,160,34,162,48,176,50,178},{64,192,66,19..., dimensions={0} | all-to-all | bytes 5242880 | tf_op jit(solution)/shard_map/all_to_all | solution.py:55
  117.6 0.1 sum_wide.1
  117.8 17.6 %all_to_all.45.parts = f32[16,40,128]{2,1,0:T(8,128)S(1)} all-to-all(f32[16,40,128]{2,1,0:T(8,128)S(1)} %sum_wide.1), channel_id=1, replica_groups={{0,4,8,12,32,36,40,44,64,68,72,76,96,100,104,108},{16,20,24,28,48,52,56..., dimensions={0} | all-to-all | bytes 655360 | tf_op jit(solution)/shard_map/all_to_all | solution.py:55
  135.4 18.0 %all_to_all.46.parts = f32[16,40,128]{2,1,0:T(8,128)S(1)} all-to-all(f32[16,40,128]{2,1,0:T(8,128)S(1)} %sum_deep.1), channel_id=1, replica_groups={{0,4,8,12,32,36,40,44,64,68,72,76,96,100,104,108},{16,20,24,28,48,52,56..., dimensions={0} | all-to-all | bytes 655360 | tf_op jit(solution)/shard_map/all_to_all | solution.py:55
  153.5 0.3 spread.1
  153.8 22.7 %all_to_all.47 = f32[8,80,1024]{2,1,0:T(8,128)S(1)} all-to-all(f32[8,80,1024]{2,1,0:T(8,128)S(1)} %spread.1), channel_id=1, replica_groups={{0,128,2,130,16,144,18,146},{32,160,34,162,48,176,50,178},{64,192,66,19..., dimensions={0} | all-to-all | bytes 5242880 | tf_op jit(solution)/shard_map/all_to_all | solution.py:55
  176.4 1.6 collective-permute-start.2
  178.0 1.6 own.1
  179.5 3.0 %collective-permute-done.2.source = f32[640,1024]{1,0:T(8,128)S(1)} collective-permute-done((f32[640,1024]{1,0:T(8,128)S(1)}, f32[640,1024]{1,0:T(8,128)S(1)}, u32[]{:S(2)}, u32[]{:S(2)}) %collective-permute-start.2) | collective-permute-done | bytes 2621472 | tf_op jit(solution)/shard_map/ppermute | solution.py:474
  182.5 1.6 other.1
  (1 shorter events, 0.0 us)
Async XLA Ops:
  86.3 8.5 %collective-permute-start = (f32[512,1024]{1,0:T(8,128)S(1)}, f32[512,1024]{1,0:T(8,128)S(1)}, u32[]{:S(2)}, u32[]{:S(2)}) collective-permute-start(f32[512,1024]{1,0:T(8,128)S(1)} %get-tuple-element.60), channel_id=1, source_target_pairs={{0,1},{1,0},{2,3},{3,2},{4,5},{5,4},{6,7},{7,6},{8,9},{9,8},{10,11... | collective-permute-start | bytes 6291464 | tf_op jit(solution)/shard_map/ppermute | solution.py:449
  92.6 2.2 %collective-permute-start.1 = (f32[128,1024]{1,0:T(8,128)S(1)}, f32[128,1024]{1,0:T(8,128)S(1)}, u32[]{:S(2)}, u32[]{:S(2)}) collective-permute-start(f32[128,1024]{1,0:T(8,128)S(1)} %get-tuple-element.61), channel_id=1, source_target_pairs={{0,1},{1,0},{2,3},{3,2},{4,5},{5,4},{6,7},{7,6},{8,9},{9,8},{10,11... | collective-permute-start | bytes 1572872 | tf_op jit(solution)/shard_map/ppermute | solution.py:457
  176.4 6.1 %collective-permute-start.2 = (f32[640,1024]{1,0:T(8,128)S(1)}, f32[640,1024]{1,0:T(8,128)S(1)}, u32[]{:S(2)}, u32[]{:S(2)}) collective-permute-start(f32[640,1024]{1,0:T(8,128)S(1)} %bitcast.3), channel_id=1, source_target_pairs={{0,1},{1,0},{2,3},{3,2},{4,5},{5,4},{6,7},{7,6},{8,9},{9,8},{10,11... | collective-permute-start | bytes 7864328 | tf_op jit(solution)/shard_map/ppermute | solution.py:474
